TPU v7x, 32 devices: a whole 2x2x4 slice. The times are simulated.
32 devices in a mesh: dp: 8 (over z, y), tp: 4 (over x, core).
Axes of the slice: x: 2, y: 2, z: 4, core: 2. Of those that a mesh axis runs over, the one named last changes fastest.
Arguments:
- activations: bfloat16 [16, 256, 768], P('dp', 'tp'), may hold values from -6 to 6
- pair_rep: bfloat16 [16, 256, 256, 256], P('dp', 'tp'), may hold values from -6 to 6
- noise_times: float32 [16], P('dp'), may hold values from 0 to 1
- class_ids: int32 [16], P('dp'), may hold values from 0 to 40
- chain_lengths: int32 [16], P('dp'), may hold values from 64 to 256, as said below
- ada_weight: bfloat16 [256, 4608], replicated, may hold values from -0.375 to 0.375
- class_table: bfloat16 [41, 256], replicated, may hold values from -4 to 4
- pair_weight: bfloat16 [12, 256], replicated, may hold values from -0.375 to 0.375
- attn_in: bfloat16 [4, 768, 768], P(None, None, 'tp'), may hold values from -0.21875 to 0.21875
- attn_out: bfloat16 [768, 768], P('tp'), may hold values from -2.5 to 2.5
- ff_in: bfloat16 [2, 768, 3072], P(None, None, 'tp'), may hold values from -0.21875 to 0.21875
- ff_out: bfloat16 [3072, 768], P('tp'), may hold values from -0.109375 to 0.109375
- cotangent: bfloat16 [16, 256, 768], P('dp', 'tp'), may hold values from -6 to 6
Outputs:
- result: bfloat16 [16, 256, 768], P('dp', 'tp')
- grad_inputs: bfloat16 [16, 256, 768], P('dp', 'tp')
- grad_pair: bfloat16 [16, 256, 256, 256], P('dp', 'tp')
- grad_attn_in: float32 [4, 768, 768], P(None, 'dp', 'tp')
- grad_attn_out: float32 [768, 768], P('tp', 'dp')
- grad_ff_in: float32 [2, 768, 3072], P(None, 'dp', 'tp')
- grad_ff_out: float32 [3072, 768], P('tp', 'dp')
- grad_ada: float32 [256, 4608], P(None, 'dp')
- grad_table: float32 [41, 256], P(None, 'dp')
- grad_pair_weight: float32 [12, 256], P(None, 'dp')
Inputs may be any that keep to these rules, and one draw needn't show every extreme that they name: `chain_lengths`: every chain has at least a quarter of its 256 slots valid, and in each draw some chain has all 256.
All inputs are finite; a program needn't handle non-finite values.
Results may differ from a plain program's by a relative error of at most 0.02.
The roundings to bfloat16 on the way count: a program that leaves them out, or rounds other values in their place, can miss the bound.
Values may be sent and summed in bfloat16 or wider, within the bound.
A program may use at most 128 MiB of HBM per device.

v0:
```python
import math

import jax
import jax.numpy as jnp
from jax import lax
from jax.sharding import PartitionSpec as P

highest = lax.Precision.HIGHEST


def time_features(noise_times, cond_width):
    half_width = cond_width // 2
    freq_steps = jnp.arange(half_width).astype(jnp.float32)
    frequency = jnp.exp(freq_steps * (-math.log(10000.0) / half_width))
    angles = 100.0 * noise_times[:, None] * frequency[None, :]
    return jnp.concatenate([jnp.sin(angles), jnp.cos(angles)], axis=1)


def normalize(rows_in):
    centered = rows_in - jnp.mean(rows_in, axis=-1, keepdims=True)
    inverse = lax.rsqrt(jnp.mean(centered * centered, axis=-1, keepdims=True) + 1e-05)
    return (centered * inverse, inverse)


def norm_back(grad_rows, normed, inverse):
    mean_grad = jnp.mean(grad_rows, axis=-1, keepdims=True)
    mean_cross = jnp.mean(grad_rows * normed, axis=-1, keepdims=True)
    return inverse * (grad_rows - mean_grad - normed * mean_cross)


def row_sums(values):
    return jnp.sum(values, axis=1)


def local(
    activations,
    pair_rep,
    noise_times,
    class_ids,
    chain_lengths,
    ada_weight,
    class_table,
    pair_weight,
    attn_in,
    attn_out,
    ff_in,
    ff_out,
    cotangent,
):
    chains, local_rows, width = activations.shape
    length = pair_rep.shape[2]
    heads_here = pair_weight.shape[0] // lax.axis_size("tp")
    head_local = attn_in.shape[2]
    head_width = head_local // heads_here
    score_scale = head_width ** (-0.5)
    head_shape = (chains, length, heads_here, head_width)
    onehot = (class_ids[:, None] == jnp.arange(class_table.shape[0])[None, :]).astype(jnp.float32)
    table_full = class_table.astype(jnp.float32)
    ada_full = ada_weight.astype(jnp.float32)
    condition = time_features(noise_times, class_table.shape[1]) + jnp.dot(
        onehot, table_full, precision=highest
    )
    modulation = jnp.dot(condition, ada_full, precision=highest)
    pieces = [modulation[:, entry * width : (entry + 1) * width][:, None, :] for entry in range(6)]
    scale_attn, shift_attn, gate_attn, scale_ff, shift_ff, gate_ff = pieces
    inputs_full = activations.astype(jnp.float32)
    normed_attn, inverse_attn = normalize(inputs_full)
    rows_attn = (normed_attn * (1.0 + scale_attn) + shift_attn).astype(jnp.bfloat16)
    gathered_attn = lax.all_gather(rows_attn, "tp", axis=1, tiled=True)
    projected = jnp.einsum(
        "gld,kde->kgle", gathered_attn, attn_in, preferred_element_type=jnp.float32
    )
    query = projected[0].astype(jnp.bfloat16).reshape(head_shape)
    key_rows = projected[1].astype(jnp.bfloat16).reshape(head_shape)
    value_rows = projected[2].astype(jnp.bfloat16).reshape(head_shape)
    gate_pre = projected[3]
    bias_local = jnp.einsum(
        "gqkp,hp->ghqk", pair_rep, pair_weight, preferred_element_type=jnp.float32
    ).astype(jnp.bfloat16)
    pair_bias = lax.all_to_all(bias_local, "tp", split_axis=1, concat_axis=2, tiled=True)
    key_valid = (jnp.arange(length)[None, :] < chain_lengths[:, None])[:, None, None, :]

    def masked_scores():
        raw_scores = jnp.einsum(
            "gqhe,gkhe->ghqk", query, key_rows, preferred_element_type=jnp.float32
        ) * score_scale + pair_bias.astype(jnp.float32)
        return jnp.where(key_valid, raw_scores, -1e30)

    scores = masked_scores()
    row_top = jnp.max(scores, axis=-1, keepdims=True)
    log_total = row_top + jnp.log(jnp.sum(jnp.exp(scores - row_top), axis=-1, keepdims=True))
    soft_low = jnp.exp(scores - log_total).astype(jnp.bfloat16)
    head_mix = jnp.einsum(
        "ghqk,gkhe->gqhe", soft_low, value_rows, preferred_element_type=jnp.float32
    ).reshape(chains, length, head_local)
    gate_sig = jax.nn.sigmoid(gate_pre)
    gated_mix = (head_mix * gate_sig).astype(jnp.bfloat16)
    attn_terms = jnp.einsum("gle,ed->gld", gated_mix, attn_out, preferred_element_type=jnp.float32)
    attended = lax.psum_scatter(
        attn_terms.astype(jnp.bfloat16), "tp", scatter_dimension=1, tiled=True
    ).astype(jnp.float32)
    sig_attn = jax.nn.sigmoid(gate_attn)
    middle = inputs_full + sig_attn * attended
    normed_ff, inverse_ff = normalize(middle)
    rows_ff = (normed_ff * (1.0 + scale_ff) + shift_ff).astype(jnp.bfloat16)
    gathered_ff = lax.all_gather(rows_ff, "tp", axis=1, tiled=True)
    gate_up = jnp.einsum("gld,kdf->kglf", gathered_ff, ff_in, preferred_element_type=jnp.float32)
    sig_hidden = jax.nn.sigmoid(gate_up[0])
    silu_hidden = gate_up[0] * sig_hidden
    hidden = (silu_hidden * gate_up[1]).astype(jnp.bfloat16)
    ff_terms = jnp.einsum("glf,fd->gld", hidden, ff_out, preferred_element_type=jnp.float32)
    transition = lax.psum_scatter(
        ff_terms.astype(jnp.bfloat16), "tp", scatter_dimension=1, tiled=True
    ).astype(jnp.float32)
    sig_ff = jax.nn.sigmoid(gate_ff)
    result = (middle + sig_ff * transition).astype(jnp.bfloat16)
    upstream = cotangent.astype(jnp.float32)
    grad_trans = (sig_ff * upstream).astype(jnp.bfloat16)
    grad_gate_ff = row_sums(upstream * transition) * (sig_ff * (1.0 - sig_ff))[:, 0, :]
    gathered_grad_ff = lax.all_gather(grad_trans, "tp", axis=1, tiled=True)
    grad_ff_out = jnp.einsum(
        "glf,gld->fd", hidden, gathered_grad_ff, preferred_element_type=jnp.float32
    )
    grad_hidden = jnp.einsum(
        "gld,fd->glf", gathered_grad_ff, ff_out, preferred_element_type=jnp.float32
    )
    silu_slope = sig_hidden * (1.0 + gate_up[0] * (1.0 - sig_hidden))
    grad_gate_up = jnp.stack(
        [grad_hidden * gate_up[1] * silu_slope, grad_hidden * silu_hidden]
    ).astype(jnp.bfloat16)
    grad_ff_in = jnp.einsum(
        "gld,kglf->kdf", gathered_ff, grad_gate_up, preferred_element_type=jnp.float32
    )
    ff_row_terms = jnp.einsum(
        "kglf,kdf->gld", grad_gate_up, ff_in, preferred_element_type=jnp.float32
    )
    grad_rows_ff = lax.psum_scatter(
        ff_row_terms.astype(jnp.bfloat16), "tp", scatter_dimension=1, tiled=True
    ).astype(jnp.float32)
    grad_scale_ff = row_sums(grad_rows_ff * normed_ff)
    grad_shift_ff = row_sums(grad_rows_ff)
    grad_middle = upstream + norm_back(grad_rows_ff * (1.0 + scale_ff), normed_ff, inverse_ff)
    grad_attended = (sig_attn * grad_middle).astype(jnp.bfloat16)
    grad_gate_attn = row_sums(grad_middle * attended) * (sig_attn * (1.0 - sig_attn))[:, 0, :]
    gathered_grad_attn = lax.all_gather(grad_attended, "tp", axis=1, tiled=True)
    grad_attn_out = jnp.einsum(
        "gle,gld->ed", gated_mix, gathered_grad_attn, preferred_element_type=jnp.float32
    )
    grad_gated = jnp.einsum(
        "gld,ed->gle", gathered_grad_attn, attn_out, preferred_element_type=jnp.float32
    )
    grad_mix = (grad_gated * gate_sig).astype(jnp.bfloat16)
    grad_gate_pre = (grad_gated * head_mix * gate_sig * (1.0 - gate_sig)).astype(jnp.bfloat16)
    grad_mix_heads = grad_mix.reshape(head_shape)
    soft_full = jnp.exp(masked_scores() - log_total)
    grad_soft = jnp.einsum(
        "gqhe,gkhe->ghqk", grad_mix_heads, value_rows, preferred_element_type=jnp.float32
    )
    grad_scores = (
        soft_full * (grad_soft - jnp.sum(grad_soft * soft_full, axis=-1, keepdims=True))
    ).astype(jnp.bfloat16)
    grad_query = (
        jnp.einsum("ghqk,gkhe->gqhe", grad_scores, key_rows, preferred_element_type=jnp.float32)
        * score_scale
    ).astype(jnp.bfloat16)
    grad_key = (
        jnp.einsum("ghqk,gqhe->gkhe", grad_scores, query, preferred_element_type=jnp.float32)
        * score_scale
    ).astype(jnp.bfloat16)
    grad_value = jnp.einsum(
        "ghqk,gqhe->gkhe", soft_low, grad_mix_heads, preferred_element_type=jnp.float32
    ).astype(jnp.bfloat16)
    flat_shape = (chains, length, head_local)
    grad_heads = jnp.stack(
        [
            grad_query.reshape(flat_shape),
            grad_key.reshape(flat_shape),
            grad_value.reshape(flat_shape),
            grad_gate_pre,
        ]
    )
    grad_attn_in = jnp.einsum(
        "gld,kgle->kde", gathered_attn, grad_heads, preferred_element_type=jnp.float32
    )
    attn_row_terms = jnp.einsum(
        "kgle,kde->gld", grad_heads, attn_in, preferred_element_type=jnp.float32
    )
    grad_rows_attn = lax.psum_scatter(
        attn_row_terms.astype(jnp.bfloat16), "tp", scatter_dimension=1, tiled=True
    ).astype(jnp.float32)
    grad_scale_attn = row_sums(grad_rows_attn * normed_attn)
    grad_shift_attn = row_sums(grad_rows_attn)
    grad_inputs = (
        grad_middle + norm_back(grad_rows_attn * (1.0 + scale_attn), normed_attn, inverse_attn)
    ).astype(jnp.bfloat16)
    bias_grads = lax.all_to_all(grad_scores, "tp", split_axis=2, concat_axis=1, tiled=True)
    grad_pair = jnp.einsum(
        "ghqk,hp->gqkp", bias_grads, pair_weight, preferred_element_type=jnp.float32
    ).astype(jnp.bfloat16)
    pair_weight_part = jnp.einsum(
        "gqkp,ghqk->hp", pair_rep, bias_grads, preferred_element_type=jnp.float32
    )
    modulation_part = jnp.concatenate(
        [
            grad_scale_attn,
            grad_shift_attn,
            grad_gate_attn,
            grad_scale_ff,
            grad_shift_ff,
            grad_gate_ff,
        ],
        axis=1,
    )
    grad_modulation, grad_pair_weight = (
        lax.psum(modulation_part.astype(jnp.bfloat16), "tp").astype(jnp.float32),
        lax.psum(pair_weight_part.astype(jnp.bfloat16), "tp").astype(jnp.float32),
    )
    grad_condition = jnp.dot(grad_modulation, ada_full.T, precision=highest)
    grad_ada = jnp.dot(condition.T, grad_modulation, precision=highest)
    grad_table = jnp.dot(onehot.T, grad_condition, precision=highest)
    summed = (
        lax.psum_scatter(grad_attn_in, "dp", scatter_dimension=1, tiled=True),
        lax.psum_scatter(grad_attn_out, "dp", scatter_dimension=1, tiled=True),
        lax.psum_scatter(grad_ff_in, "dp", scatter_dimension=1, tiled=True),
        lax.psum_scatter(grad_ff_out, "dp", scatter_dimension=1, tiled=True),
        lax.psum_scatter(grad_ada, "dp", scatter_dimension=1, tiled=True),
        lax.psum_scatter(grad_table, "dp", scatter_dimension=1, tiled=True),
        lax.psum_scatter(grad_pair_weight, "dp", scatter_dimension=1, tiled=True),
    )
    return (result, grad_inputs, grad_pair) + tuple(summed)


def solution(mesh):
    return jax.shard_map(
        local,
        mesh=mesh,
        in_specs=(
            P("dp", "tp", None),
            P("dp", "tp", None, None),
            P("dp"),
            P("dp"),
            P("dp"),
            P(),
            P(),
            P(),
            P(None, None, "tp"),
            P("tp", None),
            P(None, None, "tp"),
            P("tp", None),
            P("dp", "tp", None),
        ),
        out_specs=(
            P("dp", "tp", None),
            P("dp", "tp", None),
            P("dp", "tp", None, None),
            P(None, "dp", "tp"),
            P("tp", "dp"),
            P(None, "dp", "tp"),
            P("tp", "dp"),
            P(None, "dp"),
            P(None, "dp"),
            P(None, "dp"),
        ),
        check_vma=False,
    )
```

profile of v0, /device:TPU:0, one launch (start us, length us, event | category | flops | bytes accessed | tf_op | source)
XLA Modules:
  0.0 813.2 jit_solution(961916389535711720)
XLA Ops:
  7.2 11.4 %fusion.10 = bf16[2,12,64,256]{3,1,2,0:T(8,128)(2,1)} fusion(bf16[2,64,256,256]{3,2,1,0:T(8,128)(2,1)} %param.14, bf16[12,256]{1,0:T(8,128)(2,1)} %param.20), kind=kOutput, calls=%fused_computation.29 | convolution fusion | flops 201719808 | bytes 17569792 | tf_op jit(solution)/shard_map/gqkp,hp->ghqk/dot_general | solution.py:77
  18.6 2.4 copy.70
  21.0 4.2 all-to-all-start
  26.0 2.8 fusion.95
  29.5 12.4 %all_gather.12 = bf16[2,256,768]{2,1,0:T(8,128)(2,1)S(1)} all-gather(bf16[2,64,768]{2,1,0:T(8,128)(2,1)S(1)} %fusion.39), channel_id=1, replica_groups=mesh['dp'=8,'tp'=4] {'tp'}, dimensions={1}, use_global_device_ids=true | all-gather | bytes 983040 | tf_op jit(solution)/shard_map/all_gather | solution.py:69
  47.0 3.1 copy.73
  57.2 9.2 %all_gather.14 = bf16[2,256,768]{2,1,0:T(8,128)(2,1)} all-gather(bf16[2,64,768]{2,1,0:T(8,128)(2,1)S(1)} %fusion.54), channel_id=1, replica_groups=mesh['dp'=8,'tp'=4] {'tp'}, dimensions={1}, use_global_device_ids=true | all-gather | bytes 983040 | tf_op jit(solution)/shard_map/all_gather | solution.py:120
  66.4 15.1 %reduce-scatter.17.cloned.1.call-done = bf16[2,64,768]{2,1,0:T(8,128)(2,1)} async-done(((bf16[2,256,768]{2,1,0:T(8,128)(2,1)}), bf16[2,64,768]{2,1,0:T(8,128)(2,1)}) %reduce-scatter.17.cloned.1.call-update) | async-done | bytes 196624 | tf_op jit(solution)/shard_map/reduce_scatter | solution.py:99
  84.8 8.0 all_gather.13
  97.7 2.3 bitcast_convert_fusion.1
  100.1 23.9 %reduce-scatter.21.cloned.1.call-done = bf16[2,64,768]{2,1,0:T(8,128)(2,1)} async-done(((bf16[2,256,768]{2,1,0:T(8,128)(2,1)}), bf16[2,64,768]{2,1,0:T(8,128)(2,1)}) %reduce-scatter.21.cloned.1.call-update) | async-done | bytes 196624 | tf_op jit(solution)/shard_map/reduce_scatter | solution.py:137
  127.0 8.2 %all_gather.15 = bf16[2,256,768]{2,1,0:T(8,128)(2,1)S(1)} all-gather(bf16[2,64,768]{2,1,0:T(8,128)(2,1)S(1)} %multiply_convert_fusion.5), channel_id=1, replica_groups=mesh['dp'=8,'tp'=4] {'tp'}, dimensions={1}, use_global_device_ids=true | all-gather | bytes 983040 | tf_op jit(solution)/shard_map/all_gather | solution.py:145
  142.7 3.2 convolution_convert_fusion.2
  147.9 3.5 all-to-all-start.1
  153.5 11.6 %all-to-all-done.1 = bf16[2,3,256,256]{3,0,1,2:T(2,128)(2,1)S(1)} async-done(((bf16[2,3,256,256]{3,0,1,2:T(2,128)(2,1)}), bf16[2,3,256,256]{3,0,1,2:T(2,128)(2,1)S(1)}, u32[]{:S(2)}, u32[]{:S(2)}) %all-to-all-start.1) | async-done | bytes 786464 | tf_op jit(solution)/shard_map/all_to_all | solution.py:196
  165.3 8.9 %fusion.19 = bf16[12,256]{1,0:T(8,128)(2,1)} fusion(bf16[2,64,256,256]{3,2,1,0:T(8,128)(2,1)} %param.14, bf16[2,12,64,256]{3,2,1,0:T(8,128)(2,1)S(1)} %bitcast.195), kind=kOutput, calls=%fused_computation.43 | convolution fusion | flops 201329664 | bytes 17569792 | tf_op jit(solution)/shard_map/gqkp,ghqk->hp/dot_general | solution.py:200
  175.8 18.6 %reduce-scatter.19.cloned.1.call-done = bf16[2,64,768]{2,1,0:T(8,128)(2,1)} async-done(((bf16[2,256,768]{2,1,0:T(8,128)(2,1)}), bf16[2,64,768]{2,1,0:T(8,128)(2,1)}) %reduce-scatter.19.cloned.1.call-update) | async-done | bytes 196624 | tf_op jit(solution)/shard_map/reduce_scatter | solution.py:112
  194.5 2.9 fusion.51
  203.0 11.9 %all-reduce.1 = (bf16[12,256]{1,0:T(8,128)(2,1)}, bf16[2,4608]{1,0:T(2,128)(2,1)}) all-reduce(bf16[12,256]{1,0:T(8,128)(2,1)} %fusion.19, bf16[2,4608]{1,0:T(2,128)(2,1)} %constant_dynamic-update-slice_fusion), channel_id=1, replica_groups=mesh['dp'=8,'tp'=4] {'tp'}, use_global_device_ids=true, to_apply=%region_28.29 | all-reduce | flops 12288 | bytes 49152 | tf_op jit(solution)/shard_map/psum | solution.py:216
  216.4 4.8 convolution_bitcast_fusion
  221.1 8.2 %copy.84 = f32[2,768,768]{2,0,1:T(2,128)} copy(f32[2,768,768]{1,2,0:T(8,128)} %convolution_bitcast_fusion) | data formatting | bytes 9437184 | tf_op jit(solution)/shard_map/gld,kglf->kdf/transpose | solution.py:131
  232.7 4.5 copy.101
  237.3 4.7 reshape.161
  242.7 2.3 fusion.97
  249.1 4.3 fusion.96
  255.4 8.6 %convolution_convert_fusion = bf16[2,64,256,256]{3,2,1,0:T(8,128)(2,1)} fusion(bf16[2,12,64,256]{3,2,1,0:T(8,128)(2,1)S(1)} %bitcast.196, bf16[12,256]{1,0:T(8,128)(2,1)S(1)} %copy-done.43), kind=kOutput, calls=%fused_computation | convolution fusion | flops 209715200 | bytes 17569792 | tf_op jit(solution)/shard_map/ghqk,hp->gqkp/dot_general | solution.py:197
  266.8 58.7 %reduce-scatter.35.cloned.1.call-done = f32[32,12]{1,0:T(8,128)} async-done(((f32[256,12]{1,0:T(8,128)}), f32[32,12]{1,0:T(8,128)}) %reduce-scatter.35.cloned.1.call-update) | async-done | bytes 1552
  326.9 170.8 %all-reduce.4.cloned.1.call-done = f32[2,768,768]{2,0,1:T(2,128)} async-done(((f32[2,768,768]{2,0,1:T(2,128)}), f32[2,768,768]{2,0,1:T(2,128)}) %all-reduce.4.cloned.1.call-update) | async-done | bytes 4718608
  499.8 70.2 %reduce-scatter.31.cloned.1.call-done = f32[96,768]{1,0:T(8,128)} async-done(((f32[768,768]{1,0:T(8,128)}), f32[96,768]{1,0:T(8,128)}) %reduce-scatter.31.cloned.1.call-update) | async-done | bytes 294928
  572.0 63.0 %reduce-scatter.29.cloned.1.call-done = f32[41,32]{0,1:T(8,128)} async-done(((f32[41,256]{0,1:T(8,128)}), f32[41,32]{0,1:T(8,128)}) %reduce-scatter.29.cloned.1.call-update) | async-done | bytes 5264 | tf_op jit(solution)/shard_map/reduce_scatter | solution.py:227
  635.0 72.6 %reduce-scatter.25.cloned.1.call-done = f32[768,96]{0,1:T(8,128)} async-done(((f32[768,768]{0,1:T(8,128)}), f32[768,96]{0,1:T(8,128)}) %reduce-scatter.25.cloned.1.call-update) | async-done | bytes 294928 | tf_op jit(solution)/shard_map/reduce_scatter | solution.py:225
  707.5 99.1 %reduce-scatter.27.cloned.1.call-done = f32[256,576]{0,1:T(8,128)} async-done(((f32[256,4608]{0,1:T(8,128)}), f32[256,576]{0,1:T(8,128)}) %reduce-scatter.27.cloned.1.call-update) | async-done | bytes 589840 | tf_op jit(solution)/shard_map/reduce_scatter | solution.py:226
  (227 shorter events, 62.6 us)
Async XLA Ops:
  7.2 85.7 %copy-start = (bf16[2,768,768]{2,1,0:T(8,128)(2,1)S(1)}, bf16[2,768,768]{2,1,0:T(8,128)(2,1)}, u32[]{:S(2)}) copy-start(bf16[2,768,768]{2,1,0:T(8,128)(2,1)} %param.23) | copy-start | bytes 7077892
  21.0 24.4 %all-to-all-start = ((bf16[2,12,64,256]{3,2,0,1:T(8,128)(2,1)}), bf16[2,12,64,256]{3,2,0,1:T(8,128)(2,1)S(1)}, u32[]{:S(2)}, u32[]{:S(2)}) async-start(bf16[2,12,64,256]{3,2,0,1:T(8,128)(2,1)} %copy.70), calls=%async_computation | async-start | bytes 1572864 | tf_op jit(solution)/shard_map/all_to_all | solution.py:80
  25.2 56.3 %reduce-scatter.17.cloned.1.call-start = ((), (), s32[]{:S(2)}) async-start(), calls=%async_computation.12 | async-start | bytes 983040 | tf_op jit(solution)/shard_map/reduce_scatter | solution.py:99
  25.6 16.3 %copy-start.47 = (f32[2,64]{1,0:T(2,128)}, f32[2,64]{1,0:T(2,128)S(1)}, u32[]{:S(2)}) copy-start(f32[2,64]{1,0:T(2,128)S(1)} %add_rsqrt_fusion.1) | copy-start | bytes 1540
  26.0 16.0 %copy-start.63 = (s32[2]{0:T(128)S(1)}, s32[2]{0:T(128)}, u32[]{:S(2)}) copy-start(s32[2]{0:T(128)} %param.17) | copy-start | bytes 28
  26.0 16.7 %copy-start.23 = (bf16[4,768,192]{1,2,0:T(8,128)(2,1)S(1)}, bf16[4,768,192]{1,2,0:T(8,128)(2,1)}, u32[]{:S(2)}) copy-start(bf16[4,768,192]{1,2,0:T(8,128)(2,1)} %param.21) | copy-start | bytes 3538948
  29.4 12.6 %copy-start.35 = (f32[2,768]{1,0:T(2,128)}, f32[2,768]{1,0:T(2,128)S(1)}, u32[]{:S(2)}) copy-start(f32[2,768]{1,0:T(2,128)S(1)} %get-tuple-element.76) | copy-start | bytes 18436
  57.0 26.7 %copy-start.46 = (f32[2,768]{1,0:T(2,128)S(1)}, f32[2,768]{1,0:T(2,128)}, u32[]{:S(2)}) copy-start(f32[2,768]{1,0:T(2,128)} %get-tuple-element.73) | copy-start | bytes 18436
  57.1 66.9 %reduce-scatter.21.cloned.1.call-start = ((), (), s32[]{:S(2)}) async-start(), calls=%async_computation.14 | async-start | bytes 983040 | tf_op jit(solution)/shard_map/reduce_scatter | solution.py:137
  97.7 26.3 %copy-start.5 = (bf16[2,64,768]{2,1,0:T(8,128)(2,1)S(1)}, bf16[2,64,768]{2,1,0:T(8,128)(2,1)}, u32[]{:S(2)}) copy-start(bf16[2,64,768]{2,1,0:T(8,128)(2,1)} %reduce-scatter.17.cloned.1.call-done) | copy-start | bytes 589828
  100.1 74.1 %reduce-scatter.23.cloned.1.call-start = ((), (), s32[]{:S(2)}) async-start(), calls=%async_computation.15 | async-start | bytes 983040 | tf_op jit(solution)/shard_map/reduce_scatter | solution.py:188
  142.7 51.8 %reduce-scatter.19.cloned.1.call-start = ((), (), s32[]{:S(2)}) async-start(), calls=%async_computation.13 | async-start | bytes 983040 | tf_op jit(solution)/shard_map/reduce_scatter | solution.py:112
  147.9 17.3 %all-to-all-start.1 = ((bf16[2,3,256,256]{3,0,1,2:T(2,128)(2,1)}), bf16[2,3,256,256]{3,0,1,2:T(2,128)(2,1)S(1)}, u32[]{:S(2)}, u32[]{:S(2)}) async-start(bf16[2,3,256,256]{3,0,1,2:T(2,128)(2,1)} %copy.79), calls=%async_computation.5 | async-start | bytes 1572864 | tf_op jit(solution)/shard_map/all_to_all | solution.py:196
  151.4 112.6 %reduce-scatter.33.cloned.1.call-start = ((), (), s32[]{:S(2)}) async-start(), calls=%async_computation.20 | async-start | bytes 884736
  152.8 172.6 %reduce-scatter.35.cloned.1.call-start = ((), (), s32[]{:S(2)}) async-start(), calls=%async_computation.21 | async-start | bytes 147456
  165.3 29.2 %copy-start.10 = (bf16[2,64,768]{2,1,0:T(8,128)(2,1)S(1)}, bf16[2,64,768]{2,1,0:T(8,128)(2,1)}, u32[]{:S(2)}) copy-start(bf16[2,64,768]{2,1,0:T(8,128)(2,1)} %param.25) | copy-start | bytes 589828
  174.2 42.2 %copy-start.26 = (bf16[1,2,256,768]{3,2,1,0:T(8,128)(2,1)S(1)}, bf16[1,2,256,768]{3,2,1,0:T(8,128)(2,1)}, u32[]{:S(2)}) copy-start(bf16[1,2,256,768]{3,2,1,0:T(8,128)(2,1)} %copy-done.25) | copy-start | bytes 2359300
  216.3 281.3 %all-reduce.4.cloned.1.call-start = ((), (), s32[]{:S(2)}) async-start(), calls=%async_computation.22 | async-start | bytes 9437184
  229.4 340.6 %reduce-scatter.31.cloned.1.call-start = ((), (), s32[]{:S(2)}) async-start(), calls=%async_computation.19 | async-start | bytes 2654208
  242.1 392.9 %reduce-scatter.29.cloned.1.call-start = ((), (), s32[]{:S(2)}) async-start(), calls=%async_computation.18 | async-start | bytes 147456 | tf_op jit(solution)/shard_map/reduce_scatter | solution.py:227
  246.1 461.4 %reduce-scatter.25.cloned.1.call-start = ((), (), s32[]{:S(2)}) async-start(), calls=%async_computation.16 | async-start | bytes 2654208 | tf_op jit(solution)/shard_map/reduce_scatter | solution.py:225
  248.5 558.2 %reduce-scatter.27.cloned.1.call-start = ((), (), s32[]{:S(2)}) async-start(), calls=%async_computation.17 | async-start | bytes 5308416 | tf_op jit(solution)/shard_map/reduce_scatter | solution.py:226
  255.3 10.3 %copy-start.56 = (f32[2,64]{1,0:T(2,128)S(1)}, f32[2,64]{1,0:T(2,128)}, u32[]{:S(2)}) copy-start(f32[2,64]{1,0:T(2,128)} %get-tuple-element.58) | copy-start | bytes 1540
  255.4 10.3 %copy-start.17 = (bf16[2,64,768]{2,1,0:T(8,128)(2,1)S(1)}, bf16[2,64,768]{2,1,0:T(8,128)(2,1)}, u32[]{:S(2)}) copy-start(bf16[2,64,768]{2,1,0:T(8,128)(2,1)} %reduce-scatter.23.cloned.1.call-done) | copy-start | bytes 589828
  255.4 10.3 %copy-start.36 = (f32[2,768]{1,0:T(2,128)S(1)}, f32[2,768]{1,0:T(2,128)}, u32[]{:S(2)}) copy-start(f32[2,768]{1,0:T(2,128)} %copy-done.35) | copy-start | bytes 18436
  255.4 10.3 %copy-start.40 = (f32[2,64]{1,0:T(2,128)S(1)}, f32[2,64]{1,0:T(2,128)}, u32[]{:S(2)}) copy-start(f32[2,64]{1,0:T(2,128)} %copy-done.39) | copy-start | bytes 1540
  255.4 10.3 %copy-start.42 = (f32[2,64]{1,0:T(2,128)S(1)}, f32[2,64]{1,0:T(2,128)}, u32[]{:S(2)}) copy-start(f32[2,64]{1,0:T(2,128)} %copy-done.41) | copy-start | bytes 1540
  255.4 10.3 %copy-start.45 = (f32[2,64]{1,0:T(2,128)S(1)}, f32[2,64]{1,0:T(2,128)}, u32[]{:S(2)}) copy-start(f32[2,64]{1,0:T(2,128)} %copy-done.44) | copy-start | bytes 1540
  255.4 10.3 %copy-start.48 = (f32[2,64]{1,0:T(2,128)S(1)}, f32[2,64]{1,0:T(2,128)}, u32[]{:S(2)}) copy-start(f32[2,64]{1,0:T(2,128)} %copy-done.47) | copy-start | bytes 1540
  255.4 10.3 %copy-start.50 = (f32[2,64]{1,0:T(2,128)S(1)}, f32[2,64]{1,0:T(2,128)}, u32[]{:S(2)}) copy-start(f32[2,64]{1,0:T(2,128)} %copy-done.49) | copy-start | bytes 1540
  255.4 10.3 %copy-start.52 = (f32[2,64]{1,0:T(2,128)S(1)}, f32[2,64]{1,0:T(2,128)}, u32[]{:S(2)}) copy-start(f32[2,64]{1,0:T(2,128)} %copy-done.51) | copy-start | bytes 1540
  497.6 309.0 %copy-start.1 = (bf16[2,768,768]{2,1,0:T(8,128)(2,1)S(1)}, bf16[2,768,768]{2,1,0:T(8,128)(2,1)}, u32[]{:S(2)}) copy-start(bf16[2,768,768]{2,1,0:T(8,128)(2,1)} %param.23) | copy-start | bytes 7077892
  (49 other events, 137.6 us)
Sparse Core Ops, SparseCore 0:
  57.2 24.2 reduce-scatter.16
  100.2 23.7 reduce-scatter.20
  142.8 25.3 reduce-scatter.22
  171.2 23.2 reduce-scatter.18
  197.6 63.2 reduce-scatter.32
  264.7 60.7 reduce-scatter.34
  329.1 168.5 all-reduce.3
  501.1 68.7 reduce-scatter.30
  573.8 61.0 reduce-scatter.28
  638.9 68.6 reduce-scatter.24
  711.8 94.8 reduce-scatter.26
where the time goes:
time: 815 us; the launch traced here: 813 us
  waiting for transfers between devices  604 us (74%)
  matrix products  69.8 us (9%)
  blocking collectives  49.7 us (6%)
  local copies, waits for them, and re-layouts  48.6 us (6%)
  other arithmetic  17.8 us (2%)
  between operations  15.3 us (2%)
  starting transfers between devices  8.39 us (1%)
    unnamed x15, waiting for transfers between devices  300 us
    reduce_scatter x1, waiting for transfers between devices, local(): lax.psum_scatter(grad_ada, 'dp', scatter_dimension=1, tiled=True)  99.1 us
    reduce_scatter x1, waiting for transfers between devices, local(): lax.psum_scatter(grad_ff_out, 'dp', scatter_dimension=1, tiled=True)  72.6 us
    reduce_scatter x1, waiting for transfers between devices, local(): lax.psum_scatter(grad_table, 'dp', scatter_dimension=1, tiled=True)  63 us
    unnamed x150, local copies, waits for them, and re-layouts  30.7 us
    reduce_scatter x1, waiting for transfers between devices, local(): lax.psum_scatter(ff_row_terms.astype(jnp.bfloat16), 'tp', scatter_dimensi...  23.9 us
    reduce_scatter x1, waiting for transfers between devices, local(): lax.psum_scatter(ff_terms.astype(jnp.bfloat16), 'tp', scatter_dimension=1...  18.6 us
  transfers between devices with their start and end apart: 13, of which 10 were waited for; matrix products, arithmetic and copies ran while one was open for 11% of the time, Pallas kernels for 0%

commit v1 on v0

--- a/solution.py
+++ b/solution.py
@@ -211,21 +211,62 @@
         ],
         axis=1,
     )
-    grad_modulation, grad_pair_weight = (
+    grad_modulation, pair_weight_sum = (
         lax.psum(modulation_part.astype(jnp.bfloat16), "tp").astype(jnp.float32),
         lax.psum(pair_weight_part.astype(jnp.bfloat16), "tp").astype(jnp.float32),
     )
     grad_condition = jnp.dot(grad_modulation, ada_full.T, precision=highest)
-    grad_ada = jnp.dot(condition.T, grad_modulation, precision=highest)
-    grad_table = jnp.dot(onehot.T, grad_condition, precision=highest)
+    parts = lax.axis_size("dp")
+    place = lax.axis_index("dp")
+    sizes = [ada_full.shape[1], condition.shape[1], condition.shape[1], onehot.shape[1]]
+    chain_rows = jnp.concatenate([grad_modulation, grad_condition, condition, onehot], axis=1)
+    packed = jnp.concatenate([chain_rows.reshape(-1), pair_weight_sum.reshape(-1)])
+    packed = jnp.pad(packed, (0, -packed.size % 1024)).reshape(-1, 128)
+    gathered = lax.all_gather(packed, "dp", axis=0, tiled=True).reshape(parts, -1)
+    rows_all = gathered[:, : chain_rows.size].reshape(parts * chains, chain_rows.shape[1])
+    pair_all = gathered[:, chain_rows.size : chain_rows.size + pair_weight.size].reshape(
+        (parts,) + pair_weight.shape
+    )
+    cuts = [sum(sizes[:entry]) for entry in range(5)]
+    mod_all, grad_cond_all, cond_all, onehot_all = [
+        rows_all[:, cuts[entry] : cuts[entry + 1]] for entry in range(4)
+    ]
+
+    def own_columns(values, axis):
+        width_here = values.shape[axis] // parts
+        return lax.dynamic_slice_in_dim(values, place * width_here, width_here, axis)
+
+    grad_ada = jnp.dot(cond_all.T, own_columns(mod_all, 1), precision=highest)
+    grad_table = jnp.dot(onehot_all.T, own_columns(grad_cond_all, 1), precision=highest)
+    grad_pair_weight = jnp.sum(own_columns(pair_all, 2), axis=0)
+
+    def summed_over_chains(values_list, axes):
+        pieces, shapes = [], []
+        for values, axis in zip(values_list, axes):
+            split = values.shape[:axis] + (parts, values.shape[axis] // parts) + values.shape[axis + 1 :]
+            moved = jnp.moveaxis(values.astype(jnp.bfloat16).reshape(split), axis, 0)
+            shapes.append(moved.shape[1:])
+            pieces.append(moved.reshape(parts, -1, 128))
+        joined = jnp.concatenate(pieces, axis=1)
+        own = lax.psum_scatter(
+            joined.reshape(-1, 128), "dp", scatter_dimension=0, tiled=True
+        ).astype(jnp.float32)
+        results, start = [], 0
+        for piece, shape in zip(pieces, shapes):
+            results.append(own[start : start + piece.shape[1]].reshape(shape))
+            start += piece.shape[1]
+        return results
+
+    sum_ff_in, sum_ff_out = summed_over_chains([grad_ff_in, grad_ff_out], [1, 1])
+    sum_attn_in, sum_attn_out = summed_over_chains([grad_attn_in, grad_attn_out], [1, 1])
     summed = (
-        lax.psum_scatter(grad_attn_in, "dp", scatter_dimension=1, tiled=True),
-        lax.psum_scatter(grad_attn_out, "dp", scatter_dimension=1, tiled=True),
-        lax.psum_scatter(grad_ff_in, "dp", scatter_dimension=1, tiled=True),
-        lax.psum_scatter(grad_ff_out, "dp", scatter_dimension=1, tiled=True),
-        lax.psum_scatter(grad_ada, "dp", scatter_dimension=1, tiled=True),
-        lax.psum_scatter(grad_table, "dp", scatter_dimension=1, tiled=True),
-        lax.psum_scatter(grad_pair_weight, "dp", scatter_dimension=1, tiled=True),
+        sum_attn_in,
+        sum_attn_out,
+        sum_ff_in,
+        sum_ff_out,
+        grad_ada,
+        grad_table,
+        grad_pair_weight,
     )
     return (result, grad_inputs, grad_pair) + tuple(summed)
 

time: 815 us -> 356 us (0.44)
  waiting for transfers between devices: 604 us -> 121 us
  blocking collectives: 49.7 us -> 80.8 us
    unnamed x15 -> x6, waiting for transfers between devices: 300 us -> 0.1 us
    reduce_scatter x3 -> x2, waiting for transfers between devices: 235 us -> 70.3 us  [summed_over_chains(): lax.psum_scatter(joined.reshape(-1, 128), 'dp', scatter_dimension=0, tile...]
    all_gather x0 -> x1, blocking collectives: none -> 32.3 us  [local(): lax.all_gather(packed, 'dp', axis=0, tiled=True).reshape(parts, -1)]
    reshape x0 -> x18, local copies, waits for them, and re-layouts: none -> 24.3 us  [the longest x4 12.3 us: summed_over_chains(): pieces.append(moved.reshape(parts, -1, 128))]
    unnamed x150 -> x133, local copies, waits for them, and re-layouts: 30.7 us -> 6.75 us
    reduce_scatter x1, waiting for transfers between devices: 18.6 us -> 0.02 us  [local(): lax.psum_scatter(ff_terms.astype(jnp.bfloat16), 'tp', scatter_dimension=1...]
    transpose x1 -> x0, local copies, waits for them, and re-layouts: 8.2 us -> none  [local(): jnp.einsum('gld,kglf->kdf', gathered_ff, grad_gate_up, preferred_element_...]
  transfers between devices with their start and end apart: 13 -> 8, of which waited for: 10 -> 4; matrix products, arithmetic and copies ran while one was open for 11% -> 22% of each run, Pallas kernels for 0% -> 0%
where the time goes in v1:
time: 356 us; the launch traced here: 355 us
  waiting for transfers between devices  121 us (34%)
  blocking collectives  80.8 us (23%)
  matrix products  65.1 us (18%)
  local copies, waits for them, and re-layouts  44.4 us (12%)
  other arithmetic  19.8 us (6%)
  between operations  15 us (4%)
  starting transfers between devices  8.16 us (2%)
    reduce_scatter x2, waiting for transfers between devices, summed_over_chains(): lax.psum_scatter(joined.reshape(-1, 128), 'dp', scatter_dimension=0, tile...  70.3 us
    all_gather x1, blocking collectives, local(): lax.all_gather(packed, 'dp', axis=0, tiled=True).reshape(parts, -1)  32.3 us
    reduce_scatter x1, waiting for transfers between devices, local(): lax.psum_scatter(ff_row_terms.astype(jnp.bfloat16), 'tp', scatter_dimensi...  23.8 us
    reduce_scatter x1, waiting for transfers between devices, local(): lax.psum_scatter(attn_terms.astype(jnp.bfloat16), 'tp', scatter_dimension...  15.1 us
    all_gather x1, blocking collectives, local(): gathered_attn = lax.all_gather(rows_attn, 'tp', axis=1, tiled=True)  12.4 us
    reshape x4, local copies, waits for them, and re-layouts, summed_over_chains(): pieces.append(moved.reshape(parts, -1, 128))  12.3 us
    all_to_all x1, waiting for transfers between devices, local(): lax.all_to_all(grad_scores, 'tp', split_axis=2, concat_axis=1, tiled=True)  12 us
    dot_general x1, matrix products, local(): jnp.einsum('gqkp,hp->ghqk', pair_rep, pair_weight, preferred_element_type...  11.4 us
  transfers between devices with their start and end apart: 8, of which 4 were waited for; matrix products, arithmetic and copies ran while one was open for 22% of the time, Pallas kernels for 0%

profile of v1, /device:TPU:0, one launch (start us, length us, event | category | flops | bytes accessed | tf_op | source)
XLA Modules:
  0.0 354.6 jit_solution(2040315591612026860)
XLA Ops:
  7.2 11.4 %fusion.11 = bf16[2,12,64,256]{3,1,2,0:T(8,128)(2,1)} fusion(bf16[2,64,256,256]{3,2,1,0:T(8,128)(2,1)} %param.14, bf16[12,256]{1,0:T(8,128)(2,1)} %param.20), kind=kOutput, calls=%fused_computation.33 | convolution fusion | flops 201719808 | bytes 17569792 | tf_op jit(solution)/shard_map/gqkp,hp->ghqk/dot_general | solution.py:77
  18.6 2.4 copy.89
  21.0 4.2 %all-to-all-start = ((bf16[2,12,64,256]{3,2,0,1:T(8,128)(2,1)}), bf16[2,12,64,256]{3,2,0,1:T(8,128)(2,1)S(1)}, u32[]{:S(2)}, u32[]{:S(2)}) async-start(bf16[2,12,64,256]{3,2,0,1:T(8,128)(2,1)} %copy.89), calls=%async_computation | async-start | bytes 1572864 | tf_op jit(solution)/shard_map/all_to_all | solution.py:80
  25.9 2.8 fusion.105
  29.5 12.4 %all_gather.15 = bf16[2,256,768]{2,1,0:T(8,128)(2,1)S(1)} all-gather(bf16[2,64,768]{2,1,0:T(8,128)(2,1)S(1)} %fusion.41), channel_id=1, replica_groups=mesh['dp'=8,'tp'=4] {'tp'}, dimensions={1}, use_global_device_ids=true | all-gather | bytes 983040 | tf_op jit(solution)/shard_map/all_gather | solution.py:69
  47.0 3.1 copy.92
  56.4 9.2 %all_gather.17 = bf16[2,256,768]{2,1,0:T(8,128)(2,1)} all-gather(bf16[2,64,768]{2,1,0:T(8,128)(2,1)S(1)} %fusion.56), channel_id=1, replica_groups=mesh['dp'=8,'tp'=4] {'tp'}, dimensions={1}, use_global_device_ids=true | all-gather | bytes 983040 | tf_op jit(solution)/shard_map/all_gather | solution.py:120
  65.6 15.1 %reduce-scatter.7.cloned.1.call-done = bf16[2,64,768]{2,1,0:T(8,128)(2,1)} async-done(((bf16[2,256,768]{2,1,0:T(8,128)(2,1)}), bf16[2,64,768]{2,1,0:T(8,128)(2,1)}) %reduce-scatter.7.cloned.1.call-update) | async-done | bytes 196624 | tf_op jit(solution)/shard_map/reduce_scatter | solution.py:99
  84.0 8.0 %all_gather.16 = bf16[2,256,768]{2,1,0:T(8,128)(2,1)S(1)} all-gather(bf16[2,64,768]{2,1,0:T(8,128)(2,1)S(1)} %add_convert_fusion), channel_id=1, replica_groups=mesh['dp'=8,'tp'=4] {'tp'}, dimensions={1}, use_global_device_ids=true | all-gather | bytes 983040 | tf_op jit(solution)/shard_map/all_gather | solution.py:106
  94.5 2.1 fusion.29
  97.8 2.3 bitcast_convert_fusion.4
  100.2 23.8 %reduce-scatter.11.cloned.1.call-done = bf16[2,64,768]{2,1,0:T(8,128)(2,1)} async-done(((bf16[2,256,768]{2,1,0:T(8,128)(2,1)}), bf16[2,64,768]{2,1,0:T(8,128)(2,1)}) %reduce-scatter.11.cloned.1.call-update) | async-done | bytes 196624 | tf_op jit(solution)/shard_map/reduce_scatter | solution.py:137
  126.9 8.2 %all_gather.18 = bf16[2,256,768]{2,1,0:T(8,128)(2,1)S(1)} all-gather(bf16[2,64,768]{2,1,0:T(8,128)(2,1)S(1)} %multiply_convert_fusion.5), channel_id=1, replica_groups=mesh['dp'=8,'tp'=4] {'tp'}, dimensions={1}, use_global_device_ids=true | all-gather | bytes 983040 | tf_op jit(solution)/shard_map/all_gather | solution.py:145
  142.4 3.3 convolution_convert_fusion.2
  147.1 3.0 fusion.10
  150.2 3.1 reshape.208
  153.3 2.1 copy.102
  155.3 3.3 reshape.209
  160.1 3.2 bitcast_convert_fusion.1
  165.2 3.0 reshape.218
  168.2 2.8 bitcast_convert_fusion
  172.6 5.5 %reshape.216 = bf16[8,1152,128]{2,1,0:T(8,128)(2,1)} reshape(bf16[8,2,96,768]{3,2,1,0:T(8,128)(2,1)} %bitcast.210) | data formatting | bytes 4718592 | tf_op jit(solution)/shard_map/reshape | solution.py:249
  178.0 3.7 %pad_maximum_fusion = bf16[8,1728,128]{2,1,0:T(8,128)(2,1)} fusion(bf16[8,576,128]{2,1,0:T(8,128)(2,1)S(1)} %copy-done.7, bf16[8,1152,128]{2,1,0:T(8,128)(2,1)} %reshape.216), kind=kLoop, calls=%fused_computation.2 | loop fusion | flops 7077888 | bytes 7077888 | tf_op jit(solution)/shard_map/concatenate | solution.py:250
  183.5 3.5 all-to-all-start.1
  187.2 12.0 %all-to-all-done.1 = bf16[2,3,256,256]{3,0,1,2:T(2,128)(2,1)S(1)} async-done(((bf16[2,3,256,256]{3,0,1,2:T(2,128)(2,1)}), bf16[2,3,256,256]{3,0,1,2:T(2,128)(2,1)S(1)}, u32[]{:S(2)}, u32[]{:S(2)}) %all-to-all-start.1) | async-done | bytes 786464 | tf_op jit(solution)/shard_map/all_to_all | solution.py:196
  199.4 8.3 %fusion.21 = bf16[12,256]{1,0:T(8,128)(2,1)S(1)} fusion(bf16[2,64,256,256]{3,2,1,0:T(8,128)(2,1)} %param.14, bf16[2,12,64,256]{3,2,1,0:T(8,128)(2,1)S(1)} %bitcast.207), kind=kOutput, calls=%fused_computation.48 | convolution fusion | flops 201329664 | bytes 17569792 | tf_op jit(solution)/shard_map/gqkp,ghqk->hp/dot_general | solution.py:200
  207.9 8.6 %convolution_convert_fusion = bf16[2,64,256,256]{3,2,1,0:T(8,128)(2,1)} fusion(bf16[2,12,64,256]{3,2,1,0:T(8,128)(2,1)S(1)} %bitcast.208, bf16[12,256]{1,0:T(8,128)(2,1)S(1)} %copy-done.42), kind=kOutput, calls=%fused_computation | convolution fusion | flops 209715200 | bytes 17569792 | tf_op jit(solution)/shard_map/ghqk,hp->gqkp/dot_general | solution.py:197
  217.6 2.3 fusion.53
  220.0 10.7 %all-reduce.1 = (bf16[3072]{0:T(1024)(128)(2,1)S(1)}, bf16[2,4608]{1,0:T(2,128)(2,1)S(1)}) all-reduce(bf16[3072]{0:T(1024)(128)(2,1)S(1)} %reshape.223, bf16[2,4608]{1,0:T(2,128)(2,1)S(1)} %constant_dynamic-update-slice_fusion), channel_id=1, replica_groups=mesh['dp'=8,'tp'=4] {'tp'}, use_global_device_ids=true, to_apply=%region_24.25 | all-reduce | flops 12288 | bytes 49152 | tf_op jit(solution)/shard_map/psum | solution.py:216
  230.7 2.4 fusion.106
  233.3 32.3 %all_gather.19 = f32[896,128]{1,0:T(8,128)S(1)} all-gather(f32[112,128]{1,0:T(8,128)S(1)} %fusion.73), channel_id=1, replica_groups=mesh['dp'=8,'tp'=4] {'dp'}, dimensions={0}, use_global_device_ids=true | all-gather | bytes 516096 | tf_op jit(solution)/shard_map/all_gather | solution.py:225
  273.6 70.3 %reduce-scatter.17.cloned.1.call-done = bf16[1728,128]{1,0:T(8,128)(2,1)} async-done(((bf16[13824,128]{1,0:T(8,128)(2,1)}), bf16[1728,128]{1,0:T(8,128)(2,1)}) %reduce-scatter.17.cloned.1.call-update) | async-done | bytes 442384 | tf_op jit(solution)/shard_map/reduce_scatter | solution.py:251
  (229 shorter events, 51.2 us)
Async XLA Ops:
  7.2 85.8 %copy-start = (bf16[2,768,768]{2,1,0:T(8,128)(2,1)S(1)}, bf16[2,768,768]{2,1,0:T(8,128)(2,1)}, u32[]{:S(2)}) copy-start(bf16[2,768,768]{2,1,0:T(8,128)(2,1)} %param.23) | copy-start | bytes 7077892
  18.6 7.1 %copy-start.56 = (bf16[41,256]{1,0:T(8,128)(2,1)S(1)}, bf16[41,256]{1,0:T(8,128)(2,1)}, u32[]{:S(2)}) copy-start(bf16[41,256]{1,0:T(8,128)(2,1)} %param.19) | copy-start | bytes 62980
  18.6 7.2 %copy-start.59 = (s32[2]{0:T(128)S(1)}, s32[2]{0:T(128)}, u32[]{:S(2)}) copy-start(s32[2]{0:T(128)} %param.16) | copy-start | bytes 28
  21.0 24.4 %all-to-all-start = ((bf16[2,12,64,256]{3,2,0,1:T(8,128)(2,1)}), bf16[2,12,64,256]{3,2,0,1:T(8,128)(2,1)S(1)}, u32[]{:S(2)}, u32[]{:S(2)}) async-start(bf16[2,12,64,256]{3,2,0,1:T(8,128)(2,1)} %copy.89), calls=%async_computation | async-start | bytes 1572864 | tf_op jit(solution)/shard_map/all_to_all | solution.py:80
  25.2 55.5 %reduce-scatter.7.cloned.1.call-start = ((), (), s32[]{:S(2)}) async-start(), calls=%async_computation.8 | async-start | bytes 983040 | tf_op jit(solution)/shard_map/reduce_scatter | solution.py:99
  25.6 16.3 %copy-start.46 = (f32[2,64]{1,0:T(2,128)}, f32[2,64]{1,0:T(2,128)S(1)}, u32[]{:S(2)}) copy-start(f32[2,64]{1,0:T(2,128)S(1)} %add_rsqrt_fusion.1) | copy-start | bytes 1540
  25.9 16.0 %copy-start.58 = (s32[2]{0:T(128)S(1)}, s32[2]{0:T(128)}, u32[]{:S(2)}) copy-start(s32[2]{0:T(128)} %param.17) | copy-start | bytes 28
  25.9 16.7 %copy-start.23 = (bf16[4,768,192]{1,2,0:T(8,128)(2,1)S(1)}, bf16[4,768,192]{1,2,0:T(8,128)(2,1)}, u32[]{:S(2)}) copy-start(bf16[4,768,192]{1,2,0:T(8,128)(2,1)} %param.21) | copy-start | bytes 3538948
  29.3 12.6 %copy-start.34 = (f32[2,768]{1,0:T(2,128)}, f32[2,768]{1,0:T(2,128)S(1)}, u32[]{:S(2)}) copy-start(f32[2,768]{1,0:T(2,128)S(1)} %get-tuple-element.76) | copy-start | bytes 18436
  55.0 10.6 %copy-start.14 = (bf16[2,256,192]{1,2,0:T(8,128)(2,1)}, bf16[2,256,192]{1,2,0:T(8,128)(2,1)S(1)}, u32[]{:S(2)}) copy-start(bf16[2,256,192]{1,2,0:T(8,128)(2,1)S(1)} %fusion.62) | copy-start | bytes 589828
  56.3 26.7 %copy-start.45 = (f32[2,768]{1,0:T(2,128)S(1)}, f32[2,768]{1,0:T(2,128)}, u32[]{:S(2)}) copy-start(f32[2,768]{1,0:T(2,128)} %get-tuple-element.73) | copy-start | bytes 18436
  56.3 67.7 %reduce-scatter.11.cloned.1.call-start = ((), (), s32[]{:S(2)}) async-start(), calls=%async_computation.10 | async-start | bytes 983040 | tf_op jit(solution)/shard_map/reduce_scatter | solution.py:137
  81.8 43.4 %copy-start.38 = (f32[2,64]{1,0:T(2,128)}, f32[2,64]{1,0:T(2,128)S(1)}, u32[]{:S(2)}) copy-start(f32[2,64]{1,0:T(2,128)S(1)} %broadcast_multiply_fusion.4) | copy-start | bytes 1540
  82.9 42.3 %copy-start.40 = (f32[2,64]{1,0:T(2,128)}, f32[2,64]{1,0:T(2,128)S(1)}, u32[]{:S(2)}) copy-start(f32[2,64]{1,0:T(2,128)S(1)} %add_rsqrt_fusion) | copy-start | bytes 1540
  97.8 26.3 %copy-start.5 = (bf16[2,64,768]{2,1,0:T(8,128)(2,1)S(1)}, bf16[2,64,768]{2,1,0:T(8,128)(2,1)}, u32[]{:S(2)}) copy-start(bf16[2,64,768]{2,1,0:T(8,128)(2,1)} %reduce-scatter.7.cloned.1.call-done) | copy-start | bytes 589828
  100.1 35.0 %copy-start.22 = (f32[2,3,64,256]{3,2,1,0:T(8,128)S(1)}, f32[2,3,64,256]{3,2,1,0:T(8,128)}, u32[]{:S(2)}) copy-start(f32[2,3,64,256]{3,2,1,0:T(8,128)} %copy-done.21) | copy-start | bytes 1179652
  100.1 116.3 %reduce-scatter.13.cloned.1.call-start = ((), (), s32[]{:S(2)}) async-start(), calls=%async_computation.11 | async-start | bytes 983040 | tf_op jit(solution)/shard_map/reduce_scatter | solution.py:188
  142.3 75.2 %reduce-scatter.9.cloned.1.call-start = ((), (), s32[]{:S(2)}) async-start(), calls=%async_computation.9 | async-start | bytes 983040 | tf_op jit(solution)/shard_map/reduce_scatter | solution.py:112
  145.7 124.6 %reduce-scatter.15.cloned.1.call-start = ((), (), s32[]{:S(2)}) async-start(), calls=%async_computation.12 | async-start | bytes 1658880 | tf_op jit(solution)/shard_map/reduce_scatter | solution.py:251
  159.8 184.0 %reduce-scatter.17.cloned.1.call-start = ((), (), s32[]{:S(2)}) async-start(), calls=%async_computation.13 | async-start | bytes 3981312 | tf_op jit(solution)/shard_map/reduce_scatter | solution.py:251
  183.5 15.7 %all-to-all-start.1 = ((bf16[2,3,256,256]{3,0,1,2:T(2,128)(2,1)}), bf16[2,3,256,256]{3,0,1,2:T(2,128)(2,1)S(1)}, u32[]{:S(2)}, u32[]{:S(2)}) async-start(bf16[2,3,256,256]{3,0,1,2:T(2,128)(2,1)} %copy.98), calls=%async_computation.5 | async-start | bytes 1572864 | tf_op jit(solution)/shard_map/all_to_all | solution.py:196
  199.4 8.4 %copy-start.42 = (bf16[12,256]{1,0:T(8,128)(2,1)S(1)}, bf16[12,256]{1,0:T(8,128)(2,1)}, u32[]{:S(2)}) copy-start(bf16[12,256]{1,0:T(8,128)(2,1)} %param.20) | copy-start | bytes 18436
  207.8 9.7 %copy-start.9 = (bf16[2,64,768]{2,1,0:T(8,128)(2,1)S(1)}, bf16[2,64,768]{2,1,0:T(8,128)(2,1)}, u32[]{:S(2)}) copy-start(bf16[2,64,768]{2,1,0:T(8,128)(2,1)} %param.25) | copy-start | bytes 589828
  207.8 9.7 %copy-start.35 = (f32[2,768]{1,0:T(2,128)S(1)}, f32[2,768]{1,0:T(2,128)}, u32[]{:S(2)}) copy-start(f32[2,768]{1,0:T(2,128)} %copy-done.34) | copy-start | bytes 18436
  207.8 9.7 %copy-start.37 = (f32[2,768]{1,0:T(2,128)S(1)}, f32[2,768]{1,0:T(2,128)}, u32[]{:S(2)}) copy-start(f32[2,768]{1,0:T(2,128)} %get-tuple-element.72) | copy-start | bytes 18436
  207.8 9.7 %copy-start.39 = (f32[2,64]{1,0:T(2,128)S(1)}, f32[2,64]{1,0:T(2,128)}, u32[]{:S(2)}) copy-start(f32[2,64]{1,0:T(2,128)} %copy-done.38) | copy-start | bytes 1540
  207.8 9.7 %copy-start.41 = (f32[2,64]{1,0:T(2,128)S(1)}, f32[2,64]{1,0:T(2,128)}, u32[]{:S(2)}) copy-start(f32[2,64]{1,0:T(2,128)} %copy-done.40) | copy-start | bytes 1540
  207.8 9.7 %copy-start.44 = (f32[2,64]{1,0:T(2,128)S(1)}, f32[2,64]{1,0:T(2,128)}, u32[]{:S(2)}) copy-start(f32[2,64]{1,0:T(2,128)} %copy-done.43) | copy-start | bytes 1540
  207.9 9.7 %copy-start.47 = (f32[2,64]{1,0:T(2,128)S(1)}, f32[2,64]{1,0:T(2,128)}, u32[]{:S(2)}) copy-start(f32[2,64]{1,0:T(2,128)} %copy-done.46) | copy-start | bytes 1540
  207.9 9.7 %copy-start.49 = (f32[2,64]{1,0:T(2,128)S(1)}, f32[2,64]{1,0:T(2,128)}, u32[]{:S(2)}) copy-start(f32[2,64]{1,0:T(2,128)} %copy-done.48) | copy-start | bytes 1540
  207.9 9.7 %copy-start.51 = (f32[2,64]{1,0:T(2,128)S(1)}, f32[2,64]{1,0:T(2,128)}, u32[]{:S(2)}) copy-start(f32[2,64]{1,0:T(2,128)} %copy-done.50) | copy-start | bytes 1540
  219.9 13.2 %copy-start.53 = (f32[2,256]{1,0:T(2,128)S(1)}, f32[2,256]{1,0:T(2,128)}, u32[]{:S(2)}) copy-start(f32[2,256]{1,0:T(2,128)} %copy-done.52) | copy-start | bytes 6148
  (40 other events, 109.3 us)
Sparse Core Ops, SparseCore 0:
  56.4 24.2 reduce-scatter.6
  100.2 23.7 reduce-scatter.10
  142.4 23.7 reduce-scatter.12
  168.6 23.7 reduce-scatter.8
  195.8 65.7 reduce-scatter.14
  265.1 78.7 reduce-scatter.16

commit v2 on v1

v2 whole, which is shorter than its diff:
```python
import functools
import math

import jax
import jax.numpy as jnp
from jax import lax
from jax.experimental import pallas as pl
from jax.experimental.pallas import tpu as pltpu
from jax.sharding import PartitionSpec as P

highest = lax.Precision.HIGHEST
MESH = pl.DeviceIdType.MESH
f32, bf16 = jnp.float32, jnp.bfloat16
EPS = 1e-05
LANES = 128
NN = (((1,), (0,)), ((), ()))
NT = (((1,), (1,)), ((), ()))
TN = (((0,), (0,)), ((), ()))


def dot(left, right, dims=NN):
    return lax.dot_general(left, right, dims, preferred_element_type=f32)


def time_features(noise_times, cond_width):
    half_width = cond_width // 2
    freq_steps = jnp.arange(half_width).astype(jnp.float32)
    frequency = jnp.exp(freq_steps * (-math.log(10000.0) / half_width))
    angles = 100.0 * noise_times[:, None] * frequency[None, :]
    return jnp.concatenate([jnp.sin(angles), jnp.cos(angles)], axis=1)


def normalize(rows_in):
    centered = rows_in - jnp.mean(rows_in, axis=-1, keepdims=True)
    inverse = lax.rsqrt(jnp.mean(centered * centered, axis=-1, keepdims=True) + EPS)
    return centered * inverse, inverse


def norm_back(grad_rows, normed, inverse):
    mean_grad = jnp.mean(grad_rows, axis=-1, keepdims=True)
    mean_cross = jnp.mean(grad_rows * normed, axis=-1, keepdims=True)
    return inverse * (grad_rows - mean_grad - normed * mean_cross)


def lanes(part):
    return slice(part * LANES, (part + 1) * LANES)


def enter(peers):
    barrier = pltpu.get_barrier_semaphore()
    for peer in peers:
        pl.semaphore_signal(barrier, inc=1, device_id=peer, device_id_type=MESH)
    pl.semaphore_wait(barrier, len(peers))


def send(src, dst, sems, index, peer):
    copy = pltpu.make_async_remote_copy(
        src_ref=src,
        dst_ref=dst,
        send_sem=sems.at[(0,) + index],
        recv_sem=sems.at[(1,) + index],
        device_id=peer,
        device_id_type=MESH,
    )
    copy.start()
    return copy


def own_rows(me, rows):
    return pl.ds(pl.multiple_of(me * rows, rows), rows)


def gather_send(full, chain, me, rows, sems, peers):
    place = full.at[chain, own_rows(me, rows)]
    return [
        send(place, place, sems, (chain, step), peer) for step, (_, peer) in enumerate(peers)
    ]


def scatter_send(terms, landing, chain, rows, sems, peers):
    return [
        send(terms.at[chain, own_rows(index, rows)], landing.at[step, chain], sems, (chain, step), peer)
        for step, (index, peer) in enumerate(peers)
    ]


def scatter_take(terms, landing, chain, me, rows):
    total = terms[chain, own_rows(me, rows)].astype(f32)
    for step in range(landing.shape[0]):
        total = total + landing[step, chain].astype(f32)
    return total


def tp_peers(n_tp):
    me = lax.axis_index("tp")
    return me, [(me ^ step, {"tp": me ^ step}) for step in range(1, n_tp)]


def attn_fwd_kernel(
    sizes,
    inputs,
    mods,
    valid,
    pair_w,
    w_in,
    w_out,
    pair_hbm,
    rows_full,
    heads_out,
    gate_out,
    soft_out,
    mix_out,
    gated_out,
    attended_out,
    middle_out,
    pair_buf,
    stack,
    bias_send,
    bias_full,
    terms,
    landing,
    rows_sems,
    bias_sems,
    terms_sems,
    pair_sems,
):
    n_tp, heads, width = sizes
    chains, rows, _ = inputs.shape
    length = rows_full.shape[1]
    block = heads * width
    me, peers = tp_peers(n_tp)
    step_rows = pair_buf.shape[1]
    steps = rows // step_rows

    def fetch(turn, slot):
        return pltpu.make_async_copy(
            pair_hbm.at[turn // steps, pl.ds(lax.rem(turn, steps) * step_rows, step_rows)],
            pair_buf.at[slot],
            pair_sems.at[slot],
        )

    fetch(0, 0).start()
    fetch(1, 1).start()
    enter([peer for _, peer in peers])
    rows_sent = []
    for chain in range(chains):
        normed, _ = normalize(inputs[chain].astype(f32))
        rows_full[chain, own_rows(me, rows)] = (normed * mods[0, chain] + mods[1, chain]).astype(bf16)
        rows_sent.append(gather_send(rows_full, chain, me, rows, rows_sems, peers))

    all_heads = heads * n_tp
    padded = pair_w.shape[0]
    pair_w_here = pair_w[...]
    bias_sent = []
    for chain in range(chains):

        def bias_step(step, carry):
            turn = chain * steps + step
            slot = lax.rem(turn, 2)
            fetch(turn, slot).wait()
            for row in range(step_rows):
                found = dot(pair_w_here, pair_buf[slot, row], NT)
                for part in range(length // LANES):
                    stack[part, row * padded : (row + 1) * padded, :] = found[:, lanes(part)]

            @pl.when(turn + 2 < chains * steps)
            def _():
                fetch(turn + 2, slot).start()

            place = pl.ds(pl.multiple_of(step * step_rows, step_rows), step_rows)
            for head in range(all_heads):
                for part in range(length // LANES):
                    bias_send[head // heads, chain, head % heads, place, lanes(part)] = stack[
                        part, pl.ds(head, step_rows, stride=padded), :
                    ].astype(bf16)
            return carry

        lax.fori_loop(0, steps, bias_step, 0)
        bias_sent.append(
            [
                send(
                    bias_send.at[index, chain],
                    bias_full.at[chain, :, own_rows(me, rows), :],
                    bias_sems,
                    (chain, step),
                    peer,
                )
                for step, (index, peer) in enumerate(peers)
            ]
        )

    for chain in range(chains):
        bias_full[chain, :, own_rows(me, rows), :] = bias_send[me, chain]

    terms_sent = []
    for chain in range(chains):
        for copy in rows_sent[chain]:
            copy.wait_recv()
        projected = dot(rows_full[chain], w_in[...])
        heads_out[chain] = projected.astype(bf16)
        gate_out[chain] = jax.nn.sigmoid(projected[:, 3 * block :])
        for copy in bias_sent[chain]:
            copy.wait_recv()
        mixes = []
        for head in range(heads):
            at = head * width
            query = heads_out[chain, :, at : at + width]
            key_rows = heads_out[chain, :, block + at : block + at + width]
            value_rows = heads_out[chain, :, 2 * block + at : 2 * block + at + width]
            scores = dot(query, key_rows, NT) * width ** (-0.5) + bias_full[chain, head].astype(f32)
            scores = jnp.where(valid[chain] > 0.0, scores, -1e30)
            top = jnp.max(scores, axis=-1, keepdims=True)
            raised = jnp.exp(scores - top)
            soft = raised / jnp.sum(raised, axis=-1, keepdims=True)
            soft_out[chain, head] = soft
            mixes.append(dot(soft.astype(bf16), value_rows))
        mix = jnp.concatenate(mixes, axis=1)
        mix_out[chain] = mix
        gated = (mix * gate_out[chain]).astype(bf16)
        gated_out[chain] = gated
        terms[chain] = dot(gated, w_out[...]).astype(bf16)
        terms_sent.append(scatter_send(terms, landing, chain, rows, terms_sems, peers))

    for chain in range(chains):
        for copy in terms_sent[chain]:
            copy.wait_recv()
        attended = scatter_take(terms, landing, chain, me, rows)
        attended_out[chain] = attended
        middle_out[chain] = inputs[chain].astype(f32) + mods[2, chain] * attended
    for group in rows_sent + bias_sent + terms_sent:
        for copy in group:
            copy.wait_send()


def ff_kernel(
    sizes,
    middle,
    cotangent,
    attended,
    mods,
    w_in,
    w_out,
    result_out,
    grad_middle_out,
    grad_att_out,
    sums_out,
    weight_out,
    rows_full,
    grad_full,
    gate_keep,
    up_keep,
    hidden_keep,
    grad_gu,
    terms,
    back_terms,
    landing,
    back_landing,
    rows_sems,
    grad_sems,
    terms_sems,
    back_sems,
):
    n_tp, tile = sizes
    chains, rows, depth = middle.shape
    length = rows_full.shape[1]
    hidden_width = w_out.shape[0]
    tiles = hidden_width // tile
    me, peers = tp_peers(n_tp)
    enter([peer for _, peer in peers])
    rows_sent, grad_sent, terms_sent, back_sent = [], [], [], []
    for chain in range(chains):
        normed, _ = normalize(middle[chain])
        rows_full[chain, own_rows(me, rows)] = (normed * mods[3, chain] + mods[4, chain]).astype(bf16)
        rows_sent.append(gather_send(rows_full, chain, me, rows, rows_sems, peers))
    for chain in range(chains):
        grad_full[chain, own_rows(me, rows)] = (mods[5, chain] * cotangent[chain].astype(f32)).astype(bf16)
        grad_sent.append(gather_send(grad_full, chain, me, rows, grad_sems, peers))
    for chain in range(chains):
        for copy in rows_sent[chain]:
            copy.wait_recv()
        for part in range(tiles):
            here = slice(part * tile, (part + 1) * tile)
            gate = dot(rows_full[chain], w_in[0, :, here])
            up = dot(rows_full[chain], w_in[1, :, here])
            gate_keep[chain, :, here] = gate
            up_keep[chain, :, here] = up
            hidden_keep[chain, :, here] = (gate * jax.nn.sigmoid(gate) * up).astype(bf16)
        for part in range(depth // tile):
            here = slice(part * tile, (part + 1) * tile)
            terms[chain, :, here] = dot(hidden_keep[chain], w_out[:, here]).astype(bf16)
        terms_sent.append(scatter_send(terms, landing, chain, rows, terms_sems, peers))
    for chain in range(chains):
        for copy in grad_sent[chain]:
            copy.wait_recv()
        for part in range(tiles):
            here = slice(part * tile, (part + 1) * tile)
            grad_hidden = dot(grad_full[chain], w_out[here, :], NT)
            gate = gate_keep[chain, :, here]
            sig = jax.nn.sigmoid(gate)
            slope = sig * (1.0 + gate * (1.0 - sig))
            grad_gu[0, chain, :, here] = (grad_hidden * up_keep[chain, :, here] * slope).astype(bf16)
            grad_gu[1, chain, :, here] = (grad_hidden * (gate * sig)).astype(bf16)
        for part in range(depth // tile):
            here = slice(part * tile, (part + 1) * tile)
            back_terms[chain, :, here] = (
                dot(grad_gu[0, chain], w_in[0, here, :], NT) + dot(grad_gu[1, chain], w_in[1, here, :], NT)
            ).astype(bf16)
        back_sent.append(scatter_send(back_terms, back_landing, chain, rows, back_sems, peers))

    def flat(ref_value):
        return ref_value.reshape(chains * length, ref_value.shape[-1])

    for part in range(tiles):
        here = slice(part * tile, (part + 1) * tile)
        for which in range(2):
            weight_out[which, :, here] = dot(
                flat(rows_full[...]), flat(grad_gu[which, :, :, here]), TN
            ).astype(bf16)
        weight_out[2, :, here] = dot(
            flat(grad_full[...]), flat(hidden_keep[:, :, here]), TN
        ).astype(bf16)

    for chain in range(chains):
        for copy in terms_sent[chain]:
            copy.wait_recv()
        transition = scatter_take(terms, landing, chain, me, rows)
        upstream = cotangent[chain].astype(f32)
        result_out[chain] = (middle[chain] + mods[5, chain] * transition).astype(bf16)
        sums_out[3, chain] = jnp.sum(upstream * transition, axis=0, keepdims=True)
    for chain in range(chains):
        for copy in back_sent[chain]:
            copy.wait_recv()
        grad_rows = scatter_take(back_terms, back_landing, chain, me, rows)
        normed, inverse = normalize(middle[chain])
        sums_out[1, chain] = jnp.sum(grad_rows * normed, axis=0, keepdims=True)
        sums_out[2, chain] = jnp.sum(grad_rows, axis=0, keepdims=True)
        grad_middle = cotangent[chain].astype(f32) + norm_back(grad_rows * mods[3, chain], normed, inverse)
        grad_middle_out[chain] = grad_middle
        grad_att_out[chain] = (mods[2, chain] * grad_middle).astype(bf16)
        sums_out[0, chain] = jnp.sum(grad_middle * attended[chain], axis=0, keepdims=True)
    for group in rows_sent + grad_sent + terms_sent + back_sent:
        for copy in group:
            copy.wait_send()


def attn_bwd_kernel(
    sizes,
    inputs,
    mods,
    grad_att,
    grad_middle,
    rows_full,
    heads_kept,
    gate_sig,
    soft,
    mix,
    gated,
    w_in,
    w_out,
    pair_w,
    pair_hbm,
    grad_inputs_out,
    sums_out,
    pair_w_out,
    weight_out,
    grad_pair_hbm,
    grad_full,
    grad_heads,
    score_send,
    score_full,
    terms,
    landing,
    stack,
    pair_buf,
    out_buf,
    grad_sems,
    score_sems,
    terms_sems,
    pair_sems,
    out_sems,
):
    n_tp, heads, width = sizes
    chains, rows, depth = inputs.shape
    length = rows_full.shape[1]
    block = heads * width
    scale = width ** (-0.5)
    me, peers = tp_peers(n_tp)
    step_rows = pair_buf.shape[1]
    steps = rows // step_rows
    turns = chains * steps

    def fetch(turn, slot):
        return pltpu.make_async_copy(
            pair_hbm.at[turn // steps, pl.ds(lax.rem(turn, steps) * step_rows, step_rows)],
            pair_buf.at[slot],
            pair_sems.at[slot],
        )

    def put(turn, slot):
        return pltpu.make_async_copy(
            out_buf.at[slot],
            grad_pair_hbm.at[turn // steps, pl.ds(lax.rem(turn, steps) * step_rows, step_rows)],
            out_sems.at[slot],
        )

    fetch(0, 0).start()
    fetch(1, 1).start()
    enter([peer for _, peer in peers])
    grad_sent, score_sent, terms_sent = [], [], []
    for chain in range(chains):
        grad_full[chain, own_rows(me, rows)] = grad_att[chain]
        grad_sent.append(gather_send(grad_full, chain, me, rows, grad_sems, peers))
    for chain in range(chains):
        for copy in grad_sent[chain]:
            copy.wait_recv()
        grad_gated = dot(grad_full[chain], w_out[...], NT)
        sig = gate_sig[chain]
        grad_mix = (grad_gated * sig).astype(bf16)
        grad_gate = (grad_gated * mix[chain] * sig * (1.0 - sig)).astype(bf16)
        queries, keys, values = [], [], []
        for head in range(heads):
            at = head * width
            query = heads_kept[chain, :, at : at + width]
            key_rows = heads_kept[chain, :, block + at : block + at + width]
            value_rows = heads_kept[chain, :, 2 * block + at : 2 * block + at + width]
            grad_mix_head = grad_mix[:, at : at + width]
            weights = soft[chain, head]
            grad_soft = dot(grad_mix_head, value_rows, NT)
            inner = jnp.sum(grad_soft * weights, axis=-1, keepdims=True)
            grad_scores = (weights * (grad_soft - inner)).astype(bf16)
            for owner in range(n_tp):
                score_send[owner, chain, head] = grad_scores[owner * rows : (owner + 1) * rows, :]
            queries.append((dot(grad_scores, key_rows) * scale).astype(bf16))
            keys.append((dot(grad_scores, query, TN) * scale).astype(bf16))
            values.append(dot(weights.astype(bf16), grad_mix_head, TN).astype(bf16))
        score_sent.append(
            [
                send(
                    score_send.at[index, chain],
                    score_full.at[me, chain],
                    score_sems,
                    (chain, step),
                    peer,
                )
                for step, (index, peer) in enumerate(peers)
            ]
        )
        score_full[me, chain] = score_send[me, chain]
        grad_heads[chain] = jnp.concatenate(queries + keys + values + [grad_gate], axis=1)
        terms[chain] = dot(grad_heads[chain], w_in[...], NT).astype(bf16)
        terms_sent.append(scatter_send(terms, landing, chain, rows, terms_sems, peers))

    def flat(ref_value):
        return ref_value.reshape(chains * length, ref_value.shape[-1])

    weight_out[0, :, : 4 * block] = dot(flat(rows_full[...]), flat(grad_heads[...]), TN).astype(bf16)
    weight_out[0, :, 4 * block : 5 * block] = dot(
        flat(grad_full[...]), flat(gated[...]), TN
    ).astype(bf16)
    weight_out[0, :, 5 * block :] = jnp.zeros((depth, weight_out.shape[2] - 5 * block), bf16)

    for chain in range(chains):
        for copy in terms_sent[chain]:
            copy.wait_recv()
        grad_rows = scatter_take(terms, landing, chain, me, rows)
        normed, inverse = normalize(inputs[chain].astype(f32))
        sums_out[0, chain] = jnp.sum(grad_rows * normed, axis=0, keepdims=True)
        sums_out[1, chain] = jnp.sum(grad_rows, axis=0, keepdims=True)
        grad_inputs_out[chain] = (
            grad_middle[chain] + norm_back(grad_rows * mods[0, chain], normed, inverse)
        ).astype(bf16)

    for chain in range(chains):
        for copy in score_sent[chain]:
            copy.wait_recv()

    padded = pair_w.shape[0]
    pair_w_here = pair_w[...]
    pair_w_out[...] = jnp.zeros_like(pair_w_out)
    stack[...] = jnp.zeros_like(stack)

    def pair_step(turn, carry):
        slot = lax.rem(turn, 2)
        chain = turn // steps
        fetch(turn, slot).wait()
        place = pl.ds(pl.multiple_of(lax.rem(turn, steps) * step_rows, step_rows), step_rows)
        for head in range(heads * n_tp):
            for part in range(length // LANES):
                stack[part, pl.ds(head, step_rows, stride=padded), :] = score_full[
                    head // heads, chain, head % heads, place, lanes(part)
                ].astype(f32)

        @pl.when(turn >= 2)
        def _():
            put(turn - 2, slot).wait()

        total = jnp.zeros(pair_w_out.shape, f32)
        for row in range(step_rows):
            scores = jnp.concatenate(
                [stack[part, row * padded : (row + 1) * padded, :] for part in range(length // LANES)],
                axis=1,
            ).astype(bf16)
            out_buf[slot, row] = dot(scores, pair_w_here, TN).astype(bf16)
            total = total + dot(scores, pair_buf[slot, row])
        pair_w_out[...] += total

        @pl.when(turn + 2 < turns)
        def _():
            fetch(turn + 2, slot).start()

        put(turn, slot).start()
        return carry

    lax.fori_loop(0, turns, pair_step, 0)
    put(turns - 2, lax.rem(turns - 2, 2)).wait()
    put(turns - 1, lax.rem(turns - 1, 2)).wait()
    for group in grad_sent + score_sent + terms_sent:
        for copy in group:
            copy.wait_send()


def dp_sum_kernel(sizes, values, out, stage, sums, landing, first_sems, second_sems):
    n_z, n_y, pieces = sizes
    place = lax.axis_index("dp")
    z, y = place // n_y, lax.rem(place, n_y)
    other = {"dp": place ^ 1}
    line = [(lax.rem(z + step, n_z), {"dp": lax.rem(z + step, n_z) * n_y + y}) for step in range(1, n_z)]
    enter([other] + [peer for _, peer in line])
    size = out.shape[1] // pieces

    def cut(piece):
        return pl.ds(piece * size, size)

    first = {}
    for piece in range(pieces):
        for step in range(n_z):
            target = line[step][0] if step < n_z - 1 else z
            first[piece, step] = send(
                values.at[:, target * n_y + 1 - y, cut(piece)],
                stage.at[step, :, cut(piece)],
                first_sems,
                (piece, step),
                other,
            )
    second = {}
    for piece in range(pieces):
        for step in range(n_z):
            target = line[step][0] if step < n_z - 1 else z
            first[piece, step].wait_recv()
            total = values[:, target * n_y + y, cut(piece)].astype(f32) + stage[step, :, cut(piece)].astype(f32)
            if step < n_z - 1:
                sums[step, :, cut(piece)] = total.astype(bf16)
                second[piece, step] = send(
                    sums.at[step, :, cut(piece)],
                    landing.at[step, :, cut(piece)],
                    second_sems,
                    (piece, step),
                    line[step][1],
                )
            else:
                out[:, cut(piece)] = total
    for piece in range(pieces):
        for step in range(n_z - 1):
            second[piece, step].wait_recv()
            out[:, cut(piece)] += landing[step, :, cut(piece)].astype(f32)
    for copy in list(first.values()) + list(second.values()):
        copy.wait_send()


VMEM_SPEC = pl.BlockSpec(memory_space=pltpu.VMEM)
ANY_SPEC = pl.BlockSpec(memory_space=pl.ANY)


def pair_sems(*shape):
    return pltpu.SemaphoreType.DMA((2,) + shape)


def params(collective_id):
    return pltpu.CompilerParams(
        collective_id=collective_id, has_side_effects=True, vmem_limit_bytes=62 * 1024 * 1024
    )


def local(
    activations,
    pair_rep,
    noise_times,
    class_ids,
    chain_lengths,
    ada_weight,
    class_table,
    pair_weight,
    attn_in,
    attn_out,
    ff_in,
    ff_out,
    cotangent,
):
    n_tp, n_dp = lax.axis_size("tp"), lax.axis_size("dp")
    chains, rows, depth = activations.shape
    length, channels = pair_rep.shape[2:]
    all_heads = pair_weight.shape[0]
    heads = all_heads // n_tp
    block = attn_in.shape[2]
    width = block // heads
    hidden_width = ff_out.shape[0]
    sds = jax.ShapeDtypeStruct

    onehot = (class_ids[:, None] == jnp.arange(class_table.shape[0])[None, :]).astype(f32)
    table_full = class_table.astype(f32)
    ada_full = ada_weight.astype(f32)
    condition = time_features(noise_times, class_table.shape[1]) + jnp.dot(
        onehot, table_full, precision=highest
    )
    modulation = jnp.dot(condition, ada_full, precision=highest)
    pieces = modulation.reshape(chains, 6, 1, depth)
    sig_attn, sig_ff = jax.nn.sigmoid(pieces[:, 2]), jax.nn.sigmoid(pieces[:, 5])
    mods = jnp.stack(
        [1.0 + pieces[:, 0], pieces[:, 1], sig_attn, 1.0 + pieces[:, 3], pieces[:, 4], sig_ff]
    )
    valid = (jnp.arange(length)[None, :] < chain_lengths[:, None]).astype(f32)[:, None, :]
    padded = -(-all_heads // 16) * 16
    pair_w = jnp.pad(pair_weight, ((0, padded - all_heads), (0, 0)))
    w_in = jnp.swapaxes(attn_in, 0, 1).reshape(depth, 4 * block)

    step_rows = 16
    full = (chains, length, depth)
    own = (chains, rows, depth)
    rows_full, heads_kept, gate_sig, soft, mix, gated, attended, middle = pl.pallas_call(
        functools.partial(attn_fwd_kernel, (n_tp, heads, width)),
        out_shape=(
            sds(full, bf16),
            sds((chains, length, 4 * block), bf16),
            sds((chains, length, block), f32),
            sds((chains, heads, length, length), f32),
            sds((chains, length, block), f32),
            sds((chains, length, block), bf16),
            sds(own, f32),
            sds(own, f32),
        ),
        in_specs=[VMEM_SPEC] * 6 + [ANY_SPEC],
        out_specs=[VMEM_SPEC] * 8,
        scratch_shapes=[
            pltpu.VMEM((2, step_rows, length, channels), bf16),
            pltpu.VMEM((length // LANES, step_rows * padded, LANES), f32),
            pltpu.VMEM((n_tp, chains, heads, rows, length), bf16),
            pltpu.VMEM((chains, heads, length, length), bf16),
            pltpu.VMEM(full, bf16),
            pltpu.VMEM((n_tp - 1,) + own, bf16),
            pair_sems(chains, n_tp - 1),
            pair_sems(chains, n_tp - 1),
            pair_sems(chains, n_tp - 1),
            pltpu.SemaphoreType.DMA((2,)),
        ],
        compiler_params=params(0),
        name="attn_fwd",
    )(activations, mods, valid, pair_w, w_in, attn_out, pair_rep)

    result, grad_middle, grad_att, ff_sums, ff_weights = pl.pallas_call(
        functools.partial(ff_kernel, (n_tp, 256)),
        out_shape=(
            sds(own, bf16),
            sds(own, f32),
            sds(own, bf16),
            sds((4, chains, 1, depth), f32),
            sds((3, depth, hidden_width), bf16),
        ),
        in_specs=[VMEM_SPEC] * 6,
        out_specs=[VMEM_SPEC] * 5,
        scratch_shapes=[
            pltpu.VMEM(full, bf16),
            pltpu.VMEM(full, bf16),
            pltpu.VMEM((chains, length, hidden_width), f32),
            pltpu.VMEM((chains, length, hidden_width), f32),
            pltpu.VMEM((chains, length, hidden_width), bf16),
            pltpu.VMEM((2, chains, length, hidden_width), bf16),
            pltpu.VMEM(full, bf16),
            pltpu.VMEM(full, bf16),
            pltpu.VMEM((n_tp - 1,) + own, bf16),
            pltpu.VMEM((n_tp - 1,) + own, bf16),
            pair_sems(chains, n_tp - 1),
            pair_sems(chains, n_tp - 1),
            pair_sems(chains, n_tp - 1),
            pair_sems(chains, n_tp - 1),
        ],
        compiler_params=params(1),
        name="ff",
    )(middle, cotangent, attended, mods, ff_in, ff_out)

    grad_inputs, attn_sums, pair_part, attn_weights, grad_pair = pl.pallas_call(
        functools.partial(attn_bwd_kernel, (n_tp, heads, width)),
        out_shape=(
            sds(own, bf16),
            sds((2, chains, 1, depth), f32),
            sds((padded, channels), f32),
            sds((1, depth, -(-5 * block // LANES) * LANES), bf16),
            sds(pair_rep.shape, bf16),
        ),
        in_specs=[VMEM_SPEC] * 13 + [ANY_SPEC],
        out_specs=[VMEM_SPEC] * 4 + [ANY_SPEC],
        scratch_shapes=[
            pltpu.VMEM(full, bf16),
            pltpu.VMEM((chains, length, 4 * block), bf16),
            pltpu.VMEM((n_tp, chains, heads, rows, length), bf16),
            pltpu.VMEM((n_tp, chains, heads, rows, length), bf16),
            pltpu.VMEM(full, bf16),
            pltpu.VMEM((n_tp - 1,) + own, bf16),
            pltpu.VMEM((length // LANES, step_rows * padded, LANES), f32),
            pltpu.VMEM((2, step_rows, length, channels), bf16),
            pltpu.VMEM((2, step_rows, length, channels), bf16),
            pair_sems(chains, n_tp - 1),
            pair_sems(chains, n_tp - 1),
            pair_sems(chains, n_tp - 1),
            pltpu.SemaphoreType.DMA((2,)),
            pltpu.SemaphoreType.DMA((2,)),
        ],
        compiler_params=params(2),
        name="attn_bwd",
    )(
        activations,
        mods,
        grad_att,
        grad_middle,
        rows_full,
        heads_kept,
        gate_sig,
        soft,
        mix,
        gated,
        w_in,
        attn_out,
        pair_w,
        pair_rep,
    )

    slope = lambda s: (s * (1.0 - s))[:, 0, :]
    modulation_part = jnp.concatenate(
        [
            attn_sums[0, :, 0],
            attn_sums[1, :, 0],
            ff_sums[0, :, 0] * slope(sig_attn),
            ff_sums[1, :, 0],
            ff_sums[2, :, 0],
            ff_sums[3, :, 0] * slope(sig_ff),
        ],
        axis=1,
    )
    grad_modulation, pair_weight_sum = (
        lax.psum(modulation_part.astype(bf16), "tp").astype(f32),
        lax.psum(pair_part[:all_heads].astype(bf16), "tp").astype(f32),
    )
    grad_condition = jnp.dot(grad_modulation, ada_full.T, precision=highest)
    place = lax.axis_index("dp")
    sizes = [ada_full.shape[1], condition.shape[1], condition.shape[1], onehot.shape[1]]
    chain_rows = jnp.concatenate([grad_modulation, grad_condition, condition, onehot], axis=1)
    packed = jnp.concatenate([chain_rows.reshape(-1), pair_weight_sum.reshape(-1)])
    packed = jnp.pad(packed, (0, -packed.size % 1024)).reshape(-1, 128)
    gathered = lax.all_gather(packed, "dp", axis=0, tiled=True).reshape(n_dp, -1)
    rows_all = gathered[:, : chain_rows.size].reshape(n_dp * chains, chain_rows.shape[1])
    pair_all = gathered[:, chain_rows.size : chain_rows.size + pair_weight.size].reshape(
        (n_dp,) + pair_weight.shape
    )
    cuts = [sum(sizes[:entry]) for entry in range(5)]
    mod_all, grad_cond_all, cond_all, onehot_all = [
        rows_all[:, cuts[entry] : cuts[entry + 1]] for entry in range(4)
    ]

    def own_columns(values, axis):
        width_here = values.shape[axis] // n_dp
        return lax.dynamic_slice_in_dim(values, place * width_here, width_here, axis)

    grad_ada = jnp.dot(cond_all.T, own_columns(mod_all, 1), precision=highest)
    grad_table = jnp.dot(onehot_all.T, own_columns(grad_cond_all, 1), precision=highest)
    grad_pair_weight = jnp.sum(own_columns(pair_all, 2), axis=0)

    def summed_over_chains(values, collective_id, cuts_here):
        count, _, wide = values.shape
        if n_dp != 8:
            split = values.reshape(count, n_dp, depth // n_dp, wide)
            flat_values = jnp.swapaxes(split, 0, 1).reshape(-1, wide)
            own_part = lax.psum_scatter(flat_values, "dp", scatter_dimension=0, tiled=True)
            return own_part.astype(f32).reshape(count, depth // n_dp, wide)
        own_count = depth // n_dp
        n_y = 2
        n_z = n_dp // n_y
        return pl.pallas_call(
            functools.partial(dp_sum_kernel, (n_z, n_y, cuts_here)),
            out_shape=sds((count, own_count, wide), f32),
            in_specs=[VMEM_SPEC],
            out_specs=VMEM_SPEC,
            scratch_shapes=[
                pltpu.VMEM((n_z, count, own_count, wide), bf16),
                pltpu.VMEM((n_z - 1, count, own_count, wide), bf16),
                pltpu.VMEM((n_z - 1, count, own_count, wide), bf16),
                pair_sems(cuts_here, n_z),
                pair_sems(cuts_here, n_z - 1),
            ],
            compiler_params=params(collective_id),
            name="dp_sum",
        )(values.reshape(count, n_dp, own_count, wide))

    ff_own = summed_over_chains(ff_weights, 3, 6)
    attn_own = summed_over_chains(attn_weights, 4, 3)
    own_in = attn_own[0, :, : 4 * block].reshape(-1, 4, block)
    return (
        result,
        grad_inputs,
        grad_pair,
        jnp.swapaxes(own_in, 0, 1),
        attn_own[0, :, 4 * block : 5 * block].T,
        ff_own[:2],
        ff_own[2].T,
        grad_ada,
        grad_table,
        grad_pair_weight,
    )


def solution(mesh):
    return jax.shard_map(
        local,
        mesh=mesh,
        in_specs=(
            P("dp", "tp", None),
            P("dp", "tp", None, None),
            P("dp"),
            P("dp"),
            P("dp"),
            P(),
            P(),
            P(),
            P(None, None, "tp"),
            P("tp", None),
            P(None, None, "tp"),
            P("tp", None),
            P("dp", "tp", None),
        ),
        out_specs=(
            P("dp", "tp", None),
            P("dp", "tp", None),
            P("dp", "tp", None, None),
            P(None, "dp", "tp"),
            P("tp", "dp"),
            P(None, "dp", "tp"),
            P("tp", "dp"),
            P(None, "dp"),
            P(None, "dp"),
            P(None, "dp"),
        ),
        check_vma=False,
    )
```

time: 356 us -> 284 us (0.80)
  Pallas kernels: 0 us -> 199 us
  waiting for transfers between devices: 121 us -> 0 us
  matrix products: 65.1 us -> 8.4 us
  blocking collectives: 80.8 us -> 42.5 us
  other arithmetic: 19.8 us -> 3.82 us
  local copies, waits for them, and re-layouts: 44.4 us -> 28.9 us
  between operations: 15 us -> 0.87 us
  starting transfers between devices: 8.16 us -> 0 us
    pallas_call x0 -> x5, Pallas kernels: none -> 199 us  [the longest x2 76 us: summed_over_chains(): pl.pallas_call(functools.partial(dp_sum_kernel, (n_z, n_y, cuts_here)), o...]
    reduce_scatter x6 -> x0, waiting for transfers between devices: 109 us -> none  [the longest x2 70.3 us: summed_over_chains(): lax.psum_scatter(joined.reshape(-1, 128), 'dp', scatter_dimension=0, tile...]
    dot_general x21 -> x0, matrix products: 57.2 us -> none  [the longest x1 11.4 us: local(): jnp.einsum('gqkp,hp->ghqk', pair_rep, pair_weight, preferred_element_type...]
    all_gather x5 -> x1, blocking collectives: 70.2 us -> 31.4 us  [local(): lax.all_gather(packed, 'dp', axis=0, tiled=True).reshape(n_dp, -1)]
    reshape x16 -> x3, local copies, waits for them, and re-layouts: 24.2 us -> 1.64 us  [the longest x1 1.45 us: local(): w_in = jnp.swapaxes(attn_in, 0, 1).reshape(depth, 4 * block)]
    all_to_all x2 -> x0, waiting for transfers between devices: 12 us -> none  [the longest x1 12 us: local(): lax.all_to_all(grad_scores, 'tp', split_axis=2, concat_axis=1, tiled=True)]
    unnamed x133 -> x26, local copies, waits for them, and re-layouts: 6.75 us -> 16.2 us
    convert_element_type x4 -> x0, local copies, waits for them, and re-layouts: 8.55 us -> none  [the longest x2 4.36 us: masked_scores(): pair_bias.astype(jnp.float32)]
  transfers between devices with their start and end apart: 8 -> 0, of which waited for: 4 -> 0; matrix products, arithmetic and copies ran while one was open for 22% -> 0% of each run, Pallas kernels for 0% -> 0%
where the time goes in v2:
time: 284 us; the launch traced here: 283 us
  Pallas kernels  199 us (70%)
  blocking collectives  42.5 us (15%)
  local copies, waits for them, and re-layouts  28.9 us (10%)
  matrix products  8.4 us (3%)
  other arithmetic  3.82 us (1%)
    pallas_call x2, Pallas kernels, summed_over_chains(): pl.pallas_call(functools.partial(dp_sum_kernel, (n_z, n_y, cuts_here)), o...  76 us
    pallas_call x1, Pallas kernels, local(): pl.pallas_call(functools.partial(attn_bwd_kernel, (n_tp, heads, width)),...  47.3 us
    pallas_call x1, Pallas kernels, local(): pl.pallas_call(functools.partial(ff_kernel, (n_tp, 256)), out_shape=(sds(...  41.5 us
    pallas_call x1, Pallas kernels, local(): pl.pallas_call(functools.partial(attn_fwd_kernel, (n_tp, heads, width)),...  34 us
    all_gather x1, blocking collectives, local(): lax.all_gather(packed, 'dp', axis=0, tiled=True).reshape(n_dp, -1)  31.4 us
    unnamed x26, local copies, waits for them, and re-layouts  16.2 us
    psum x1, blocking collectives, local(): lax.psum(pair_part[:all_heads].astype(bf16), 'tp').astype(f32)  11.2 us

profile of v2, /device:TPU:0, one launch (start us, length us, event | category | flops | bytes accessed | tf_op | source)
XLA Modules:
  0.0 283.3 jit_solution(16345327385881762886)
XLA Ops:
  0.7 0.8 broadcast_multiply_fusion
  1.4 0.7 fusion.19
  2.3 0.8 convolution_add_fusion
  3.1 1.3 compare_convert_fusion.valid
  4.4 1.3 pad.8.pair_w
  5.7 2.7 fusion.24
  8.6 1.5 copy.59.w_in
  10.0 34.0 %attn_fwd.1 = (bf16[2,256,768]{2,1,0:T(8,128)(2,1)}, bf16[2,256,768]{2,1,0:T(8,128)(2,1)}, f32[2,256,192]{2,1,0:T(8,128)}, f32[2,3,256,256]{3,2,1,0:T(8,128)}, f...) custom-call(bf16[2,64,768]{2,1,0:T(8,128)(2,1)} %inputs.3, ...), custom_call_target="tpu_custom_call" | custom-call | tf_op jit(solution)/shard_map/attn_fwd/pallas_call | solution.py:629
  44.1 41.5 %ff.1 = (bf16[2,64,768]{2,1,0:T(8,128)(2,1)}, f32[2,64,768]{2,1,0:T(8,128)}, bf16[2,64,768]{2,1,0:T(8,128)(2,1)}, f32[4,2,1,768]{3,2,1,0:T(1,128)}, bf16[3,768,768]{2,1,0:T(8,128)(2,1)}) custom-call(f32[2,64,768]{2,1,0:T(8,128)} %get-tuple-element.28.middle, bf16[2,64,768]{2,1,0:T(8,128)(2,1)} %cotangent.1, f32[2,64,768]{2,1,0:T(8,128)} %get-tuple-element.29.attended, ...), custom_call_target="tpu_custom_call" | custom-call | tf_op jit(solution)/shard_map/ff/pallas_call | solution.py:659
  85.5 0.8 copy.82
  86.3 0.8 copy.63
  87.1 50.3 %dp_sum.3 = f32[3,96,768]{2,1,0:T(8,128)} custom-call(bf16[3,8,96,768]{3,2,1,0:T(8,128)(2,1)} %bitcast.73), custom_call_target="tpu_custom_call" | custom-call | tf_op jit(solution)/shard_map/dp_sum/pallas_call | solution.py:786
  137.3 1.7 slice_bitcast_fusion
  139.0 1.9 slice.82
  140.9 47.3 %attn_bwd.1 = (bf16[2,64,768]{2,1,0:T(8,128)(2,1)}, f32[2,2,1,768]{3,2,1,0:T(1,128)}, f32[16,256]{1,0:T(8,128)}, bf16[1,768,1024]{2,1,0:T(8,128)(2,1)}, bf16[2,64,256,256]{3,2,1,0:T(8,128)(2,1)}) custom-call(bf16[2,64,768]{2,1,0:T(8,128)(2,1)} %inputs.3, f32[6,2,1,768]{3,2,1,0:T(1,128)} %copy-done.3, bf16[2,64,768]{2,1,0:T(8,128)(2,1)} %get-tuple-element.31.grad_att, ...), custom_call_target="tpu_custom_call" | custom-call | tf_op jit(solution)/shard_map/attn_bwd/pallas_call | solution.py:690
  188.2 0.7 copy.81
  188.9 0.7 slice.171
  189.8 11.2 %all-reduce.2 = (bf16[3072]{0:T(1024)(128)(2,1)S(1)}, bf16[2,4608]{1,0:T(2,128)(2,1)S(1)}) all-reduce(bf16[3072]{0:T(1024)(128)(2,1)S(1)} %reshape.209, bf16[2,4608]{1,0:T(2,128)(2,1)S(1)} %constant_dynamic-update-slice_fusion.6), channel_id=1, replica_groups=mesh['dp'=8,'tp'=4] {'tp'}, use_global_device_ids=true, to_apply=%region_1.2 | all-reduce | flops 12288 | bytes 49152 | tf_op jit(solution)/shard_map/psum | solution.py:750
  200.9 2.4 fusion.25
  203.5 25.7 %dp_sum.2 = f32[1,96,1024]{2,1,0:T(8,128)} custom-call(bf16[1,8,96,1024]{3,2,1,0:T(8,128)(2,1)} %bitcast.74), custom_call_target="tpu_custom_call" | custom-call | tf_op jit(solution)/shard_map/dp_sum/pallas_call | solution.py:786
  229.3 0.9 slice_bitcast_fusion.1
  230.2 1.0 slice.80
  231.2 0.7 copy.66
  231.9 0.3 reshape_squeeze.3
  232.2 0.8 copy.83
  233.0 31.4 %all_gather.3 = f32[896,128]{1,0:T(8,128)S(1)} all-gather(f32[112,128]{1,0:T(8,128)S(1)} %fusion), channel_id=1, replica_groups=mesh['dp'=8,'tp'=4] {'dp'}, dimensions={0}, use_global_device_ids=true | all-gather | bytes 516096 | tf_op jit(solution)/shard_map/all_gather | solution.py:758
  264.6 0.7 dynamic-slice_reduce_fusion
  265.4 0.9 fusion.4
  266.3 1.6 fusion.1
  267.9 0.7 copy.97
  268.6 0.7 copy.98
  269.3 14.0 %copy.99 = bf16[2,64,256,256]{3,2,1,0:T(8,128)(2,1)} copy(bf16[2,64,256,256]{3,2,1,0:T(8,128)(2,1)} %get-tuple-element.98) | data formatting | bytes 33554432
  (40 shorter events, 0.9 us)
Async XLA Ops:
  0.6 1.6 copy-start
  0.7 7.9 %copy-start.2 = (bf16[4,768,192]{1,2,0:T(8,128)(2,1)S(1)}, bf16[4,768,192]{1,2,0:T(8,128)(2,1)}, u32[]{:S(2)}) copy-start(bf16[4,768,192]{1,2,0:T(8,128)(2,1)} %param.21) | copy-start | bytes 3538948
  8.6 1.5 copy-start.3
  233.0 34.9 %copy-start.4 = (bf16[2,64,768]{2,1,0:T(8,128)(2,1)S(1)}, bf16[2,64,768]{2,1,0:T(8,128)(2,1)}, u32[]{:S(2)}) copy-start(bf16[2,64,768]{2,1,0:T(8,128)(2,1)} %get-tuple-element.96) | copy-start | bytes 589828
  233.0 35.6 %copy-start.5 = (bf16[2,64,768]{2,1,0:T(8,128)(2,1)S(1)}, bf16[2,64,768]{2,1,0:T(8,128)(2,1)}, u32[]{:S(2)}) copy-start(bf16[2,64,768]{2,1,0:T(8,128)(2,1)} %get-tuple-element.97) | copy-start | bytes 589828
  269.3 14.0 %copy-start.1 = (bf16[41,256]{1,0:T(8,128)(2,1)S(1)}, bf16[41,256]{1,0:T(8,128)(2,1)}, u32[]{:S(2)}) copy-start(bf16[41,256]{1,0:T(8,128)(2,1)} %param.19) | copy-start | bytes 62980

commit v3 on v2

--- a/solution.py
+++ b/solution.py
@@ -91,6 +91,96 @@
     return total
 
 
+class DpSum:
+    def __init__(self, sizes, values, out, stage, sums, landing, first_sems, second_sems):
+        self.n_z, self.n_y, self.pieces = sizes
+        self.values, self.out, self.stage, self.sums, self.landing = values, out, stage, sums, landing
+        self.first_sems, self.second_sems = first_sems, second_sems
+        place = lax.axis_index("dp")
+        self.z, self.y = place // self.n_y, lax.rem(place, self.n_y)
+        self.other = {"dp": place ^ 1}
+        self.line = []
+        for step in range(1, self.n_z):
+            target = lax.rem(self.z + step, self.n_z)
+            self.line.append((target, {"dp": target * self.n_y + self.y}))
+        self.size = out.shape[1] // self.pieces
+        self.first, self.second = {}, {}
+        self.todo = [(piece, step) for piece in range(self.pieces) for step in range(self.n_z)]
+
+    def peers(self):
+        return [self.other] + [peer for _, peer in self.line]
+
+    def cut(self, piece):
+        return pl.ds(piece * self.size, self.size)
+
+    def target(self, step):
+        return self.line[step][0] if step < self.n_z - 1 else self.z
+
+    def start(self):
+        for piece, step in self.todo:
+            self.first[piece, step] = send(
+                self.values.at[:, self.target(step) * self.n_y + 1 - self.y, self.cut(piece)],
+                self.stage.at[step, :, self.cut(piece)],
+                self.first_sems,
+                (piece, step),
+                self.other,
+            )
+
+    def work(self, count):
+        for _ in range(min(count, len(self.todo))):
+            piece, step = self.todo.pop(0)
+            here = self.cut(piece)
+            self.first[piece, step].wait_recv()
+            kept = self.values[:, self.target(step) * self.n_y + self.y, here].astype(f32)
+            total = kept + self.stage[step, :, here].astype(f32)
+            if step == self.n_z - 1:
+                self.out[:, here] = total
+                continue
+            self.sums[step, :, here] = total.astype(bf16)
+            self.second[piece, step] = send(
+                self.sums.at[step, :, here],
+                self.landing.at[step, :, here],
+                self.second_sems,
+                (piece, step),
+                self.line[step][1],
+            )
+
+    def finish(self):
+        self.work(len(self.todo))
+        for piece in range(self.pieces):
+            here = self.cut(piece)
+            total = self.out[:, here]
+            for step in range(self.n_z - 1):
+                self.second[piece, step].wait_recv()
+                total = total + self.landing[step, :, here].astype(f32)
+            self.out[:, here] = total
+        for copy in list(self.first.values()) + list(self.second.values()):
+            copy.wait_send()
+
+
+def dp_sum_scratch(sizes, count, own_count, wide):
+    n_z, _, pieces = sizes
+    return [
+        pltpu.VMEM((n_z, count, own_count, wide), bf16),
+        pltpu.VMEM((n_z - 1, count, own_count, wide), bf16),
+        pltpu.VMEM((n_z - 1, count, own_count, wide), bf16),
+        pair_sems(pieces, n_z),
+        pair_sems(pieces, n_z - 1),
+    ]
+
+
+def dp_others(n_dp):
+    place = lax.axis_index("dp")
+    return place, [{"dp": lax.rem(place + step, n_dp)} for step in range(1, n_dp)]
+
+
+def share_over_dp(full, place, others, sems):
+    return [
+        send(full.at[place], full.at[place], sems, (step,), peer)
+        for step, peer in enumerate(others)
+    ]
+
+
 def tp_peers(n_tp):
     me = lax.axis_index("tp")
     return me, [(me ^ step, {"tp": me ^ step}) for step in range(1, n_tp)]
@@ -104,6 +194,7 @@
     pair_w,
     w_in,
     w_out,
+    chain_facts,
     pair_hbm,
     rows_full,
     heads_out,
@@ -113,6 +204,7 @@
     gated_out,
     attended_out,
     middle_out,
+    facts_all,
     pair_buf,
     stack,
     bias_send,
@@ -122,9 +214,10 @@
     rows_sems,
     bias_sems,
     terms_sems,
+    facts_sems,
     pair_sems,
 ):
-    n_tp, heads, width = sizes
+    n_tp, n_dp, heads, width = sizes
     chains, rows, _ = inputs.shape
     length = rows_full.shape[1]
     block = heads * width
@@ -141,12 +234,16 @@
 
     fetch(0, 0).start()
     fetch(1, 1).start()
-    enter([peer for _, peer in peers])
+    place_dp, others = dp_others(n_dp)
+    enter([peer for _, peer in peers] + others)
     rows_sent = []
     for chain in range(chains):
         normed, _ = normalize(inputs[chain].astype(f32))
         rows_full[chain, own_rows(me, rows)] = (normed * mods[0, chain] + mods[1, chain]).astype(bf16)
         rows_sent.append(gather_send(rows_full, chain, me, rows, rows_sems, peers))
+
+    facts_all[place_dp] = chain_facts[...]
+    facts_sent = share_over_dp(facts_all, place_dp, others, facts_sems)
 
     all_heads = heads * n_tp
     padded = pair_w.shape[0]
@@ -227,7 +324,9 @@
         attended = scatter_take(terms, landing, chain, me, rows)
         attended_out[chain] = attended
         middle_out[chain] = inputs[chain].astype(f32) + mods[2, chain] * attended
-    for group in rows_sent + bias_sent + terms_sent:
+    for copy in facts_sent:
+        copy.wait_recv()
+    for group in rows_sent + bias_sent + terms_sent + [facts_sent]:
         for copy in group:
             copy.wait_send()
 
@@ -357,62 +456,45 @@
     gated,
     w_in,
     w_out,
-    pair_w,
-    pair_hbm,
+    ff_values,
     grad_inputs_out,
     sums_out,
-    pair_w_out,
     weight_out,
-    grad_pair_hbm,
+    score_full,
+    ff_out,
     grad_full,
     grad_heads,
     score_send,
-    score_full,
     terms,
     landing,
-    stack,
-    pair_buf,
-    out_buf,
     grad_sems,
     score_sems,
     terms_sems,
-    pair_sems,
-    out_sems,
+    *dp_scratch,
 ):
-    n_tp, heads, width = sizes
+    n_tp, heads, width, dp_sizes = sizes
     chains, rows, depth = inputs.shape
     length = rows_full.shape[1]
     block = heads * width
     scale = width ** (-0.5)
     me, peers = tp_peers(n_tp)
-    step_rows = pair_buf.shape[1]
-    steps = rows // step_rows
-    turns = chains * steps
-
-    def fetch(turn, slot):
-        return pltpu.make_async_copy(
-            pair_hbm.at[turn // steps, pl.ds(lax.rem(turn, steps) * step_rows, step_rows)],
-            pair_buf.at[slot],
-            pair_sems.at[slot],
-        )
-
-    def put(turn, slot):
-        return pltpu.make_async_copy(
-            out_buf.at[slot],
-            grad_pair_hbm.at[turn // steps, pl.ds(lax.rem(turn, steps) * step_rows, step_rows)],
-            out_sems.at[slot],
-        )
-
-    fetch(0, 0).start()
-    fetch(1, 1).start()
-    enter([peer for _, peer in peers])
+    ff_sum = DpSum(dp_sizes, ff_values, ff_out, *dp_scratch) if dp_sizes else None
+    enter([peer for _, peer in peers] + (ff_sum.peers() if ff_sum else []))
+
+    def work(count):
+        if ff_sum:
+            ff_sum.work(count)
+
     grad_sent, score_sent, terms_sent = [], [], []
     for chain in range(chains):
         grad_full[chain, own_rows(me, rows)] = grad_att[chain]
         grad_sent.append(gather_send(grad_full, chain, me, rows, grad_sems, peers))
+    if ff_sum:
+        ff_sum.start()
     for chain in range(chains):
         for copy in grad_sent[chain]:
             copy.wait_recv()
+        work(2)
         grad_gated = dot(grad_full[chain], w_out[...], NT)
         sig = gate_sig[chain]
         grad_mix = (grad_gated * sig).astype(bf16)
@@ -446,22 +528,27 @@
             ]
         )
         score_full[me, chain] = score_send[me, chain]
+        work(2)
         grad_heads[chain] = jnp.concatenate(queries + keys + values + [grad_gate], axis=1)
         terms[chain] = dot(grad_heads[chain], w_in[...], NT).astype(bf16)
         terms_sent.append(scatter_send(terms, landing, chain, rows, terms_sems, peers))
+        work(2)
 
     def flat(ref_value):
         return ref_value.reshape(chains * length, ref_value.shape[-1])
 
     weight_out[0, :, : 4 * block] = dot(flat(rows_full[...]), flat(grad_heads[...]), TN).astype(bf16)
+    work(2)
     weight_out[0, :, 4 * block : 5 * block] = dot(
         flat(grad_full[...]), flat(gated[...]), TN
     ).astype(bf16)
     weight_out[0, :, 5 * block :] = jnp.zeros((depth, weight_out.shape[2] - 5 * block), bf16)
+    work(1)
 
     for chain in range(chains):
         for copy in terms_sent[chain]:
             copy.wait_recv()
+        work(2)
         grad_rows = scatter_take(terms, landing, chain, me, rows)
         normed, inverse = normalize(inputs[chain].astype(f32))
         sums_out[0, chain] = jnp.sum(grad_rows * normed, axis=0, keepdims=True)
@@ -473,7 +560,50 @@
     for chain in range(chains):
         for copy in score_sent[chain]:
             copy.wait_recv()
-
+    if ff_sum:
+        ff_sum.finish()
+    else:
+        ff_out[...] = jnp.zeros_like(ff_out)
+    for group in grad_sent + score_sent + terms_sent:
+        for copy in group:
+            copy.wait_send()
+
+
+def pair_kernel(
+    sizes,
+    score_full,
+    pair_w,
+    pair_hbm,
+    pair_w_out,
+    grad_pair_hbm,
+    stack,
+    pair_buf,
+    out_buf,
+    in_sems,
+    out_sems,
+):
+    n_tp, heads = sizes
+    chains, rows, length = score_full.shape[1], score_full.shape[3], score_full.shape[4]
+    step_rows = pair_buf.shape[1]
+    steps = rows // step_rows
+    turns = chains * steps
+
+    def fetch(turn, slot):
+        return pltpu.make_async_copy(
+            pair_hbm.at[turn // steps, pl.ds(lax.rem(turn, steps) * step_rows, step_rows)],
+            pair_buf.at[slot],
+            in_sems.at[slot],
+        )
+
+    def put(turn, slot):
+        return pltpu.make_async_copy(
+            out_buf.at[slot],
+            grad_pair_hbm.at[turn // steps, pl.ds(lax.rem(turn, steps) * step_rows, step_rows)],
+            out_sems.at[slot],
+        )
+
+    fetch(0, 0).start()
+    fetch(1, 1).start()
     padded = pair_w.shape[0]
     pair_w_here = pair_w[...]
     pair_w_out[...] = jnp.zeros_like(pair_w_out)
@@ -514,56 +644,60 @@
     lax.fori_loop(0, turns, pair_step, 0)
     put(turns - 2, lax.rem(turns - 2, 2)).wait()
     put(turns - 1, lax.rem(turns - 1, 2)).wait()
-    for group in grad_sent + score_sent + terms_sent:
-        for copy in group:
-            copy.wait_send()
-
-
-def dp_sum_kernel(sizes, values, out, stage, sums, landing, first_sems, second_sems):
-    n_z, n_y, pieces = sizes
-    place = lax.axis_index("dp")
-    z, y = place // n_y, lax.rem(place, n_y)
-    other = {"dp": place ^ 1}
-    line = [(lax.rem(z + step, n_z), {"dp": lax.rem(z + step, n_z) * n_y + y}) for step in range(1, n_z)]
-    enter([other] + [peer for _, peer in line])
-    size = out.shape[1] // pieces
-
-    def cut(piece):
-        return pl.ds(piece * size, size)
-
-    first = {}
-    for piece in range(pieces):
-        for step in range(n_z):
-            target = line[step][0] if step < n_z - 1 else z
-            first[piece, step] = send(
-                values.at[:, target * n_y + 1 - y, cut(piece)],
-                stage.at[step, :, cut(piece)],
-                first_sems,
-                (piece, step),
-                other,
-            )
-    second = {}
-    for piece in range(pieces):
-        for step in range(n_z):
-            target = line[step][0] if step < n_z - 1 else z
-            first[piece, step].wait_recv()
-            total = values[:, target * n_y + y, cut(piece)].astype(f32) + stage[step, :, cut(piece)].astype(f32)
-            if step < n_z - 1:
-                sums[step, :, cut(piece)] = total.astype(bf16)
-                second[piece, step] = send(
-                    sums.at[step, :, cut(piece)],
-                    landing.at[step, :, cut(piece)],
-                    second_sems,
-                    (piece, step),
-                    line[step][1],
-                )
-            else:
-                out[:, cut(piece)] = total
-    for piece in range(pieces):
-        for step in range(n_z - 1):
-            second[piece, step].wait_recv()
-            out[:, cut(piece)] += landing[step, :, cut(piece)].astype(f32)
-    for copy in list(first.values()) + list(second.values()):
+
+
+def tail_kernel(
+    sizes,
+    attn_sums,
+    ff_sums,
+    pair_part,
+    mods,
+    *rest,
+):
+    n_tp, n_dp, all_heads, dp_sizes = sizes
+    if dp_sizes:
+        values, totals, own_out, own, arrived, tp_sems, dp_sems, *dp_scratch = rest
+        attn_sum = DpSum(dp_sizes, values, own_out, *dp_scratch)
+    else:
+        totals, own, arrived, tp_sems, dp_sems = rest
+        attn_sum = None
+    chains, depth = mods.shape[1], mods.shape[3]
+    channels = pair_part.shape[1]
+    _, peers = tp_peers(n_tp)
+    place, others = dp_others(n_dp)
+    enter([peer for _, peer in peers] + others)
+    if attn_sum:
+        attn_sum.start()
+    for chain in range(chains):
+        sig_attn, sig_ff = mods[2, chain], mods[5, chain]
+        entries = [
+            attn_sums[0, chain],
+            attn_sums[1, chain],
+            ff_sums[0, chain] * (sig_attn * (1.0 - sig_attn)),
+            ff_sums[1, chain],
+            ff_sums[2, chain],
+            ff_sums[3, chain] * (sig_ff * (1.0 - sig_ff)),
+        ]
+        for entry, value in enumerate(entries):
+            own[entry * chains + chain : entry * chains + chain + 1, :] = value.astype(bf16)
+    per_row = depth // channels
+    for head in range(all_heads):
+        row = 6 * chains + head // per_row
+        at = head % per_row * channels
+        own[row : row + 1, at : at + channels] = pair_part[head : head + 1, :].astype(bf16)
+    tp_sent = [send(own, arrived.at[step], tp_sems, (step,), peer) for step, (_, peer) in enumerate(peers)]
+    for copy in tp_sent:
+        copy.wait_recv()
+    total = own[...].astype(f32)
+    for step in range(n_tp - 1):
+        total = total + arrived[step].astype(f32)
+    totals[place] = total.astype(bf16)
+    dp_sent = share_over_dp(totals, place, others, dp_sems)
+    if attn_sum:
+        attn_sum.finish()
+    for copy in dp_sent:
+        copy.wait_recv()
+    for copy in tp_sent + dp_sent:
         copy.wait_send()
 
 
@@ -623,11 +757,19 @@
     pair_w = jnp.pad(pair_weight, ((0, padded - all_heads), (0, 0)))
     w_in = jnp.swapaxes(attn_in, 0, 1).reshape(depth, 4 * block)
 
+    high = condition.astype(bf16)
+    low = (condition - high.astype(f32)).astype(bf16)
+    classes = onehot.shape[1]
+    facts = jnp.concatenate([high, low, onehot.astype(bf16)], axis=1)
+    facts = jnp.pad(facts, ((0, -chains % 16), (0, -facts.shape[1] % LANES)))
+    direct = n_dp == 8
+    dp_grid = (n_dp // 2, 2)
+    own_count = depth // n_dp
     step_rows = 16
     full = (chains, length, depth)
     own = (chains, rows, depth)
-    rows_full, heads_kept, gate_sig, soft, mix, gated, attended, middle = pl.pallas_call(
-        functools.partial(attn_fwd_kernel, (n_tp, heads, width)),
+    rows_full, heads_kept, gate_sig, soft, mix, gated, attended, middle, facts_all = pl.pallas_call(
+        functools.partial(attn_fwd_kernel, (n_tp, n_dp, heads, width)),
         out_shape=(
             sds(full, bf16),
             sds((chains, length, 4 * block), bf16),
@@ -637,9 +779,10 @@
             sds((chains, length, block), bf16),
             sds(own, f32),
             sds(own, f32),
+            sds((n_dp,) + facts.shape, bf16),
         ),
-        in_specs=[VMEM_SPEC] * 6 + [ANY_SPEC],
-        out_specs=[VMEM_SPEC] * 8,
+        in_specs=[VMEM_SPEC] * 7 + [ANY_SPEC],
+        out_specs=[VMEM_SPEC] * 9,
         scratch_shapes=[
             pltpu.VMEM((2, step_rows, length, channels), bf16),
             pltpu.VMEM((length // LANES, step_rows * padded, LANES), f32),
@@ -650,11 +793,12 @@
             pair_sems(chains, n_tp - 1),
             pair_sems(chains, n_tp - 1),
             pair_sems(chains, n_tp - 1),
+            pair_sems(n_dp - 1),
             pltpu.SemaphoreType.DMA((2,)),
         ],
         compiler_params=params(0),
         name="attn_fwd",
-    )(activations, mods, valid, pair_w, w_in, attn_out, pair_rep)
+    )(activations, mods, valid, pair_w, w_in, attn_out, facts, pair_rep)
 
     result, grad_middle, grad_att, ff_sums, ff_weights = pl.pallas_call(
         functools.partial(ff_kernel, (n_tp, 256)),
@@ -687,33 +831,32 @@
         name="ff",
     )(middle, cotangent, attended, mods, ff_in, ff_out)
 
-    grad_inputs, attn_sums, pair_part, attn_weights, grad_pair = pl.pallas_call(
-        functools.partial(attn_bwd_kernel, (n_tp, heads, width)),
+    wide = -(-5 * block // LANES) * LANES
+    ff_sizes = dp_grid + (6,) if direct else None
+    ff_values = ff_weights.reshape(3, n_dp, own_count, hidden_width)
+    score_shape = (n_tp, chains, heads, rows, length)
+    grad_inputs, attn_sums, attn_weights, score_full, ff_own = pl.pallas_call(
+        functools.partial(attn_bwd_kernel, (n_tp, heads, width, ff_sizes)),
         out_shape=(
             sds(own, bf16),
             sds((2, chains, 1, depth), f32),
-            sds((padded, channels), f32),
-            sds((1, depth, -(-5 * block // LANES) * LANES), bf16),
-            sds(pair_rep.shape, bf16),
+            sds((1, depth, wide), bf16),
+            sds(score_shape, bf16),
+            sds((3, own_count, hidden_width), f32),
         ),
-        in_specs=[VMEM_SPEC] * 13 + [ANY_SPEC],
-        out_specs=[VMEM_SPEC] * 4 + [ANY_SPEC],
+        in_specs=[VMEM_SPEC] * 13,
+        out_specs=[VMEM_SPEC] * 5,
         scratch_shapes=[
             pltpu.VMEM(full, bf16),
             pltpu.VMEM((chains, length, 4 * block), bf16),
-            pltpu.VMEM((n_tp, chains, heads, rows, length), bf16),
-            pltpu.VMEM((n_tp, chains, heads, rows, length), bf16),
+            pltpu.VMEM(score_shape, bf16),
             pltpu.VMEM(full, bf16),
             pltpu.VMEM((n_tp - 1,) + own, bf16),
-            pltpu.VMEM((length // LANES, step_rows * padded, LANES), f32),
-            pltpu.VMEM((2, step_rows, length, channels), bf16),
-            pltpu.VMEM((2, step_rows, length, channels), bf16),
             pair_sems(chains, n_tp - 1),
             pair_sems(chains, n_tp - 1),
             pair_sems(chains, n_tp - 1),
-            pltpu.SemaphoreType.DMA((2,)),
-            pltpu.SemaphoreType.DMA((2,)),
-        ],
+        ]
+        + (dp_sum_scratch(ff_sizes, 3, own_count, hidden_width) if direct else []),
         compiler_params=params(2),
         name="attn_bwd",
     )(
@@ -729,78 +872,79 @@
         gated,
         w_in,
         attn_out,
-        pair_w,
-        pair_rep,
+        ff_values,
     )
 
-    slope = lambda s: (s * (1.0 - s))[:, 0, :]
-    modulation_part = jnp.concatenate(
-        [
-            attn_sums[0, :, 0],
-            attn_sums[1, :, 0],
-            ff_sums[0, :, 0] * slope(sig_attn),
-            ff_sums[1, :, 0],
-            ff_sums[2, :, 0],
-            ff_sums[3, :, 0] * slope(sig_ff),
+    pair_part, grad_pair = pl.pallas_call(
+        functools.partial(pair_kernel, (n_tp, heads)),
+        out_shape=(sds((padded, channels), f32), sds(pair_rep.shape, bf16)),
+        in_specs=[VMEM_SPEC] * 2 + [ANY_SPEC],
+        out_specs=[VMEM_SPEC, ANY_SPEC],
+        scratch_shapes=[
+            pltpu.VMEM((length // LANES, step_rows * padded, LANES), f32),
+            pltpu.VMEM((2, step_rows, length, channels), bf16),
+            pltpu.VMEM((2, step_rows, length, channels), bf16),
+            pltpu.SemaphoreType.DMA((2,)),
+            pltpu.SemaphoreType.DMA((2,)),
         ],
-        axis=1,
-    )
-    grad_modulation, pair_weight_sum = (
-        lax.psum(modulation_part.astype(bf16), "tp").astype(f32),
-        lax.psum(pair_part[:all_heads].astype(bf16), "tp").astype(f32),
-    )
-    grad_condition = jnp.dot(grad_modulation, ada_full.T, precision=highest)
+        compiler_params=pltpu.CompilerParams(vmem_limit_bytes=62 * 1024 * 1024),
+        name="pair_grad",
+    )(score_full, pair_w, pair_rep)
+
+    attn_sizes = dp_grid + (6,) if direct else None
+    total_rows = 6 * chains + all_heads * channels // depth
+    tail_in = [attn_sums, ff_sums, pair_part, mods]
+    tail_out = [sds((n_dp, total_rows, depth), bf16)]
+    tail_scratch = [
+        pltpu.VMEM((total_rows, depth), bf16),
+        pltpu.VMEM((n_tp - 1, total_rows, depth), bf16),
+        pair_sems(n_tp - 1),
+        pair_sems(n_dp - 1),
+    ]
+    if direct:
+        tail_in.append(attn_weights.reshape(1, n_dp, own_count, wide))
+        tail_out.append(sds((1, own_count, wide), f32))
+        tail_scratch += dp_sum_scratch(attn_sizes, 1, own_count, wide)
+    totals, *rest = pl.pallas_call(
+        functools.partial(tail_kernel, (n_tp, n_dp, all_heads, attn_sizes)),
+        out_shape=tuple(tail_out),
+        in_specs=[VMEM_SPEC] * len(tail_in),
+        out_specs=tuple([VMEM_SPEC] * len(tail_out)),
+        scratch_shapes=tail_scratch,
+        compiler_params=params(3),
+        name="tail",
+    )(*tail_in)
+
+    def summed_over_chains(values):
+        count, _, here = values.shape
+        split = values.reshape(count, n_dp, own_count, here)
+        flat_values = jnp.swapaxes(split, 0, 1).reshape(-1, here)
+        own_part = lax.psum_scatter(flat_values, "dp", scatter_dimension=0, tiled=True)
+        return own_part.astype(f32).reshape(count, own_count, here)
+
+    if direct:
+        attn_own = rest[0]
+    else:
+        ff_own, attn_own = summed_over_chains(ff_weights), summed_over_chains(attn_weights)
+
     place = lax.axis_index("dp")
-    sizes = [ada_full.shape[1], condition.shape[1], condition.shape[1], onehot.shape[1]]
-    chain_rows = jnp.concatenate([grad_modulation, grad_condition, condition, onehot], axis=1)
-    packed = jnp.concatenate([chain_rows.reshape(-1), pair_weight_sum.reshape(-1)])
-    packed = jnp.pad(packed, (0, -packed.size % 1024)).reshape(-1, 128)
-    gathered = lax.all_gather(packed, "dp", axis=0, tiled=True).reshape(n_dp, -1)
-    rows_all = gathered[:, : chain_rows.size].reshape(n_dp * chains, chain_rows.shape[1])
-    pair_all = gathered[:, chain_rows.size : chain_rows.size + pair_weight.size].reshape(
-        (n_dp,) + pair_weight.shape
-    )
-    cuts = [sum(sizes[:entry]) for entry in range(5)]
-    mod_all, grad_cond_all, cond_all, onehot_all = [
-        rows_all[:, cuts[entry] : cuts[entry + 1]] for entry in range(4)
-    ]
 
     def own_columns(values, axis):
         width_here = values.shape[axis] // n_dp
         return lax.dynamic_slice_in_dim(values, place * width_here, width_here, axis)
 
+    totals = totals.astype(f32)
+    mod_all = totals[:, : 6 * chains].reshape(n_dp, 6, chains, depth)
+    mod_all = jnp.swapaxes(mod_all, 1, 2).reshape(n_dp * chains, 6 * depth)
+    pair_all = totals[:, 6 * chains :].reshape(n_dp, all_heads, channels)
+    facts_rows = facts_all[:, :chains].astype(f32).reshape(n_dp * chains, -1)
+    cond_wide = condition.shape[1]
+    cond_all = facts_rows[:, :cond_wide] + facts_rows[:, cond_wide : 2 * cond_wide]
+    onehot_all = facts_rows[:, 2 * cond_wide : 2 * cond_wide + classes]
     grad_ada = jnp.dot(cond_all.T, own_columns(mod_all, 1), precision=highest)
-    grad_table = jnp.dot(onehot_all.T, own_columns(grad_cond_all, 1), precision=highest)
+    grad_cond = jnp.dot(mod_all, own_columns(ada_weight, 0).astype(f32).T, precision=highest)
+    grad_table = jnp.dot(onehot_all.T, grad_cond, precision=highest)
     grad_pair_weight = jnp.sum(own_columns(pair_all, 2), axis=0)
-
-    def summed_over_chains(values, collective_id, cuts_here):
-        count, _, wide = values.shape
-        if n_dp != 8:
-            split = values.reshape(count, n_dp, depth // n_dp, wide)
-            flat_values = jnp.swapaxes(split, 0, 1).reshape(-1, wide)
-            own_part = lax.psum_scatter(flat_values, "dp", scatter_dimension=0, tiled=True)
-            return own_part.astype(f32).reshape(count, depth // n_dp, wide)
-        own_count = depth // n_dp
-        n_y = 2
-        n_z = n_dp // n_y
-        return pl.pallas_call(
-            functools.partial(dp_sum_kernel, (n_z, n_y, cuts_here)),
-            out_shape=sds((count, own_count, wide), f32),
-            in_specs=[VMEM_SPEC],
-            out_specs=VMEM_SPEC,
-            scratch_shapes=[
-                pltpu.VMEM((n_z, count, own_count, wide), bf16),
-                pltpu.VMEM((n_z - 1, count, own_count, wide), bf16),
-                pltpu.VMEM((n_z - 1, count, own_count, wide), bf16),
-                pair_sems(cuts_here, n_z),
-                pair_sems(cuts_here, n_z - 1),
-            ],
-            compiler_params=params(collective_id),
-            name="dp_sum",
-        )(values.reshape(count, n_dp, own_count, wide))
-
-    ff_own = summed_over_chains(ff_weights, 3, 6)
-    attn_own = summed_over_chains(attn_weights, 4, 3)
     own_in = attn_own[0, :, : 4 * block].reshape(-1, 4, block)
     return (
         result,

time: 284 us -> 208 us (0.73)
  blocking collectives: 42.5 us -> 0 us
  local copies, waits for them, and re-layouts: 28.9 us -> 12.7 us
  Pallas kernels: 199 us -> 183 us
    all_gather x1 -> x0, blocking collectives: 31.4 us -> none  [local(): lax.all_gather(packed, 'dp', axis=0, tiled=True).reshape(n_dp, -1)]
    pallas_call x4, Pallas kernels: 157 us -> 141 us  [the longest x1 52.7 us: local(): pl.pallas_call(functools.partial(attn_bwd_kernel, (n_tp, heads, width, ff...]
    unnamed x26 -> x18, local copies, waits for them, and re-layouts: 16.2 us -> 2.19 us
    psum x1 -> x0, blocking collectives: 11.2 us -> none  [local(): lax.psum(pair_part[:all_heads].astype(bf16), 'tp').astype(f32)]
where the time goes in v3:
time: 208 us; the launch traced here: 207 us
  Pallas kernels  183 us (88%)
  local copies, waits for them, and re-layouts  12.7 us (6%)
  matrix products  6.83 us (3%)
  other arithmetic  4.32 us (2%)
    pallas_call x1, Pallas kernels, local(): pl.pallas_call(functools.partial(attn_bwd_kernel, (n_tp, heads, width, ff...  52.7 us
    pallas_call x1, Pallas kernels, local(): pl.pallas_call(functools.partial(ff_kernel, (n_tp, 256)), out_shape=(sds(...  41.5 us
    pallas_call x1, Pallas kernels, local(): pl.pallas_call(functools.partial(attn_fwd_kernel, (n_tp, n_dp, heads, wid...  37.7 us
    pallas_call x1, Pallas kernels, local(): pl.pallas_call(functools.partial(tail_kernel, (n_tp, n_dp, all_heads, att...  32.6 us
    pallas_call x1, Pallas kernels, local(): pl.pallas_call(functools.partial(pair_kernel, (n_tp, heads)), out_shape=(...  18 us

profile of v3, /device:TPU:0, one launch (start us, length us, event | category | flops | bytes accessed | tf_op | source)
XLA Modules:
  0.0 207.2 jit_solution(14848575967560434552)
XLA Ops:
  0.6 0.0 copy-start
  0.7 0.0 copy-start.1
  0.7 0.8 broadcast_multiply_fusion
  1.4 0.7 convert_convert_fusion
  2.2 0.1 multiply_sine_fusion
  2.3 1.3 compare_convert_fusion.valid
  3.6 0.8 subtract_convert_fusion
  4.4 1.3 pad.8.pair_w
  5.7 0.6 fusion.10.chain_facts
  6.3 2.7 %fusion.29 = f32[2,4608]{1,0:T(2,128)S(1)} fusion(f32[2,256]{1,0:T(2,128)S(1)} %get-tuple-element.80, bf16[256,4608]{1,0:T(8,128)(2,1)} %param.18), kind=kOutput, calls=%fused_computation.58 | convolution fusion | flops 28311552 | bytes 2398208 | tf_op jit(solution)/shard_map/dot_general | solution.py:749
  9.2 0.0 copy-start.2
  9.2 1.5 copy.26.w_in
  10.7 37.7 %attn_fwd.1 = (bf16[2,256,768]{2,1,0:T(8,128)(2,1)}, bf16[2,256,768]{2,1,0:T(8,128)(2,1)}, f32[2,256,192]{2,1,0:T(8,128)}, f32[2,3,256,256]{3,2,1,0:T(8,128)}, f...) custom-call(bf16[2,64,768]{2,1,0:T(8,128)(2,1)} %inputs.3, ...), custom_call_target="tpu_custom_call" | custom-call | tf_op jit(solution)/shard_map/attn_fwd/pallas_call | solution.py:771
  48.4 0.9 slice.59
  49.4 41.5 %ff.1 = (bf16[2,64,768]{2,1,0:T(8,128)(2,1)}, f32[2,64,768]{2,1,0:T(8,128)}, bf16[2,64,768]{2,1,0:T(8,128)(2,1)}, f32[4,2,1,768]{3,2,1,0:T(1,128)}, bf16[3,768,768]{2,1,0:T(8,128)(2,1)}) custom-call(f32[2,64,768]{2,1,0:T(8,128)} %get-tuple-element.33.middle, bf16[2,64,768]{2,1,0:T(8,128)(2,1)} %cotangent.1, f32[2,64,768]{2,1,0:T(8,128)} %get-tuple-element.34.attended, ...), custom_call_target="tpu_custom_call" | custom-call | tf_op jit(solution)/shard_map/ff/pallas_call | solution.py:803
  90.9 52.7 %attn_bwd.1 = (bf16[2,64,768]{2,1,0:T(8,128)(2,1)}, f32[2,2,1,768]{3,2,1,0:T(1,128)}, bf16[1,768,1024]{2,1,0:T(8,128)(2,1)}, bf16[4,2,3,64,256]{4,3,2,1,0:T(8,128)(2,1)}, f32[3,96,768]{2,1,0:T(8,128)}) custom-call(bf16[2,64,768]{2,1,0:T(8,128)(2,1)} %inputs.3, f32[6,2,1,768]{3,2,1,0:T(1,128)} %copy-done.2, bf16[2,64,768]{2,1,0:T(8,128)(2,1)} %get-tuple-element.36.grad_att, ...), custom_call_target="tpu_custom_call" | custom-call | tf_op jit(solution)/shard_map/attn_bwd/pallas_call | solution.py:838
  143.6 1.7 slice_bitcast_fusion
  145.3 1.9 slice.57
  147.2 18.0 %pair_grad.1 = (f32[16,256]{1,0:T(8,128)}, bf16[2,64,256,256]{3,2,1,0:T(8,128)(2,1)}) custom-call(bf16[4,2,3,64,256]{4,3,2,1,0:T(8,128)(2,1)} %get-tuple-element.46.score_full, bf16[16,256]{1,0:T(8,128)(2,1)} %pad.8.pair_w, bf16[2,64,256,256]{3,2,1,0:T(8,128)(2,1)} %pair_hbm.3), custom_call_target="tpu_custom_call" | custom-call | tf_op jit(solution)/shard_map/pair_grad/pallas_call | solution.py:878
  165.2 32.6 %tail.1 = (bf16[8,16,768]{2,1,0:T(8,128)(2,1)}, f32[1,96,1024]{2,1,0:T(8,128)}) custom-call(f32[2,2,1,768]{3,2,1,0:T(1,128)} %get-tuple-element.48.attn_sums, f32[4,2,1,768]{3,2,1,0:T(1,128)} %get-tuple-element.49.ff_sums, f32[16,256]{1,0:T(8,128)} %get-tuple-element.50.pair_part, f32[6,2,1,768]{3,2,1,0:T(1,128)} %copy-done.2, bf16[1,8,96,1024]{3,2,1,0:T(8,128)(2,1)} %bitcast.53), custom_call_target="tpu_custom_call" | custom-call | tf_op jit(solution)/shard_map/tail/pallas_call | solution.py:908
  197.8 0.9 slice_bitcast_fusion.1
  198.8 1.0 slice.55
  199.8 0.7 copy.31
  200.5 0.3 reshape_squeeze.3
  200.8 0.8 copy.34
  201.7 0.1 reshape.192
  201.7 0.7 dynamic-slice_reduce_fusion
  202.6 1.2 fusion
  203.7 0.8 fusion.24
  204.5 1.3 fusion.11
  205.9 0.7 copy.42
  206.6 0.7 copy.43
  (23 shorter events, 0.4 us)
Async XLA Ops:
  0.6 2.9 %copy-start = (bf16[41,256]{1,0:T(8,128)(2,1)S(1)}, bf16[41,256]{1,0:T(8,128)(2,1)}, u32[]{:S(2)}) copy-start(bf16[41,256]{1,0:T(8,128)(2,1)} %param.19) | copy-start | bytes 62980
  0.7 8.6 %copy-start.1 = (bf16[4,768,192]{1,2,0:T(8,128)(2,1)S(1)}, bf16[4,768,192]{1,2,0:T(8,128)(2,1)}, u32[]{:S(2)}) copy-start(bf16[4,768,192]{1,2,0:T(8,128)(2,1)} %param.21) | copy-start | bytes 3538948
  9.2 1.5 copy-start.2
  197.8 3.8 %copy-start.3 = (bf16[8,16,768]{2,1,0:T(8,128)(2,1)S(1)}, bf16[8,16,768]{2,1,0:T(8,128)(2,1)}, u32[]{:S(2)}) copy-start(bf16[8,16,768]{2,1,0:T(8,128)(2,1)} %get-tuple-element.55) | copy-start | bytes 589828
  198.7 7.1 %copy-start.4 = (bf16[2,64,768]{2,1,0:T(8,128)(2,1)S(1)}, bf16[2,64,768]{2,1,0:T(8,128)(2,1)}, u32[]{:S(2)}) copy-start(bf16[2,64,768]{2,1,0:T(8,128)(2,1)} %get-tuple-element.91) | copy-start | bytes 589828
  199.8 6.8 %copy-start.5 = (bf16[2,64,768]{2,1,0:T(8,128)(2,1)S(1)}, bf16[2,64,768]{2,1,0:T(8,128)(2,1)}, u32[]{:S(2)}) copy-start(bf16[2,64,768]{2,1,0:T(8,128)(2,1)} %get-tuple-element.92) | copy-start | bytes 589828

commit v4 on v3

--- a/solution.py
+++ b/solution.py
@@ -70,25 +70,82 @@
     return pl.ds(pl.multiple_of(me * rows, rows), rows)
 
 
-def gather_send(full, chain, me, rows, sems, peers):
-    place = full.at[chain, own_rows(me, rows)]
+class Gather:
+    def __init__(self, full, rows, sems):
+        self.full, self.rows, self.sems = full, rows, sems
+        self.me = lax.axis_index("tp")
+        self.cross, self.direct, self.handed = {}, {}, {}
+
+    def place(self, chain, index):
+        return self.full.at[chain, own_rows(index, self.rows)]
+
+    def send(self, chain):
+        here = self.place(chain, self.me)
+        self.cross[chain] = send(here, here, self.sems, (chain, 0), {"tp": self.me ^ 2})
+        self.direct[chain] = send(here, here, self.sems, (chain, 1), {"tp": self.me ^ 1})
+
+    def relay(self, chain):
+        self.cross[chain].wait_recv()
+        here = self.place(chain, self.me ^ 2)
+        self.handed[chain] = send(here, here, self.sems, (chain, 2), {"tp": self.me ^ 1})
+
+    def take(self, chain):
+        self.direct[chain].wait_recv()
+        self.handed[chain].wait_recv()
+
+    def done(self):
+        for group in (self.cross, self.direct, self.handed):
+            for copy in group.values():
+                copy.wait_send()
+
+
+class Scatter:
+    def __init__(self, terms, near, joint, far, rows, sems):
+        self.terms, self.near, self.joint, self.far = terms, near, joint, far
+        self.rows, self.sems = rows, sems
+        self.me = lax.axis_index("tp")
+        self.cross, self.direct, self.handed = {}, {}, {}
+
+    def place(self, chain, index):
+        return self.terms.at[chain, own_rows(index, self.rows)]
+
+    def send(self, chain):
+        other = {"tp": self.me ^ 1}
+        self.handed[chain] = send(
+            self.place(chain, self.me ^ 3), self.near.at[1, chain], self.sems, (chain, 0), other
+        )
+        self.direct[chain] = send(
+            self.place(chain, self.me ^ 1), self.near.at[0, chain], self.sems, (chain, 1), other
+        )
+
+    def relay(self, chain):
+        self.handed[chain].wait_recv()
+        mine = self.terms[chain, own_rows(self.me ^ 2, self.rows)].astype(f32)
+        self.joint[chain] = (mine + self.near[1, chain].astype(f32)).astype(bf16)
+        self.cross[chain] = send(
+            self.joint.at[chain], self.far.at[chain], self.sems, (chain, 2), {"tp": self.me ^ 2}
+        )
+
+    def take(self, chain):
+        self.direct[chain].wait_recv()
+        self.cross[chain].wait_recv()
+        total = self.terms[chain, own_rows(self.me, self.rows)].astype(f32)
+        return total + self.near[0, chain].astype(f32) + self.far[chain].astype(f32)
+
+    def done(self):
+        for group in (self.cross, self.direct, self.handed):
+            for copy in group.values():
+                copy.wait_send()
+
+
+def scatter_scratch(chains, rows, length, depth):
     return [
-        send(place, place, sems, (chain, step), peer) for step, (_, peer) in enumerate(peers)
+        pltpu.VMEM((chains, length, depth), bf16),
+        pltpu.VMEM((2, chains, rows, depth), bf16),
+        pltpu.VMEM((chains, rows, depth), bf16),
+        pltpu.VMEM((chains, rows, depth), bf16),
+        pair_sems(chains, 3),
     ]
-
-
-def scatter_send(terms, landing, chain, rows, sems, peers):
-    return [
-        send(terms.at[chain, own_rows(index, rows)], landing.at[step, chain], sems, (chain, step), peer)
-        for step, (index, peer) in enumerate(peers)
-    ]
-
-
-def scatter_take(terms, landing, chain, me, rows):
-    total = terms[chain, own_rows(me, rows)].astype(f32)
-    for step in range(landing.shape[0]):
-        total = total + landing[step, chain].astype(f32)
-    return total
 
 
 class DpSum:
@@ -194,7 +251,7 @@
     pair_w,
     w_in,
     w_out,
-    chain_facts,
+    cotangent,
     pair_hbm,
     rows_full,
     heads_out,
@@ -204,20 +261,22 @@
     gated_out,
     attended_out,
     middle_out,
-    facts_all,
+    grad_full,
     pair_buf,
     stack,
     bias_send,
     bias_full,
+    rows_sems,
+    grad_sems,
+    bias_sems,
+    pair_sems,
     terms,
-    landing,
-    rows_sems,
-    bias_sems,
+    near,
+    joint,
+    far,
     terms_sems,
-    facts_sems,
-    pair_sems,
 ):
-    n_tp, n_dp, heads, width = sizes
+    n_tp, heads, width = sizes
     chains, rows, _ = inputs.shape
     length = rows_full.shape[1]
     block = heads * width
@@ -234,16 +293,17 @@
 
     fetch(0, 0).start()
     fetch(1, 1).start()
-    place_dp, others = dp_others(n_dp)
-    enter([peer for _, peer in peers] + others)
-    rows_sent = []
+    enter([peer for _, peer in peers])
+    gather = Gather(rows_full, rows, rows_sems)
+    grad_gather = Gather(grad_full, rows, grad_sems)
+    scatter = Scatter(terms, near, joint, far, rows, terms_sems)
     for chain in range(chains):
         normed, _ = normalize(inputs[chain].astype(f32))
         rows_full[chain, own_rows(me, rows)] = (normed * mods[0, chain] + mods[1, chain]).astype(bf16)
-        rows_sent.append(gather_send(rows_full, chain, me, rows, rows_sems, peers))
-
-    facts_all[place_dp] = chain_facts[...]
-    facts_sent = share_over_dp(facts_all, place_dp, others, facts_sems)
+        gather.send(chain)
+
+    for chain in range(chains):
+        grad_full[chain, own_rows(me, rows)] = (mods[5, chain] * cotangent[chain].astype(f32)).astype(bf16)
 
     all_heads = heads * n_tp
     padded = pair_w.shape[0]
@@ -286,16 +346,17 @@
             ]
         )
 
-    for chain in range(chains):
+        gather.relay(chain)
         bias_full[chain, :, own_rows(me, rows), :] = bias_send[me, chain]
 
-    terms_sent = []
-    for chain in range(chains):
-        for copy in rows_sent[chain]:
-            copy.wait_recv()
+    for chain in range(chains):
+        grad_gather.send(chain)
+    for chain in range(chains):
+        gather.take(chain)
         projected = dot(rows_full[chain], w_in[...])
         heads_out[chain] = projected.astype(bf16)
         gate_out[chain] = jax.nn.sigmoid(projected[:, 3 * block :])
+    for chain in range(chains):
         for copy in bias_sent[chain]:
             copy.wait_recv()
         mixes = []
@@ -316,17 +377,21 @@
         gated = (mix * gate_out[chain]).astype(bf16)
         gated_out[chain] = gated
         terms[chain] = dot(gated, w_out[...]).astype(bf16)
-        terms_sent.append(scatter_send(terms, landing, chain, rows, terms_sems, peers))
-
-    for chain in range(chains):
-        for copy in terms_sent[chain]:
-            copy.wait_recv()
-        attended = scatter_take(terms, landing, chain, me, rows)
+        scatter.send(chain)
+        grad_gather.relay(chain)
+        if chain > 0:
+            scatter.relay(chain - 1)
+    scatter.relay(chains - 1)
+
+    for chain in range(chains):
+        attended = scatter.take(chain)
         attended_out[chain] = attended
         middle_out[chain] = inputs[chain].astype(f32) + mods[2, chain] * attended
-    for copy in facts_sent:
-        copy.wait_recv()
-    for group in rows_sent + bias_sent + terms_sent + [facts_sent]:
+    for chain in range(chains):
+        grad_gather.take(chain)
+    for part in (gather, grad_gather, scatter):
+        part.done()
+    for group in bias_sent:
         for copy in group:
             copy.wait_send()
 
@@ -337,6 +402,7 @@
     cotangent,
     attended,
     mods,
+    grad_full,
     w_in,
     w_out,
     result_out,
@@ -345,19 +411,12 @@
     sums_out,
     weight_out,
     rows_full,
-    grad_full,
     gate_keep,
     up_keep,
     hidden_keep,
     grad_gu,
-    terms,
-    back_terms,
-    landing,
-    back_landing,
     rows_sems,
-    grad_sems,
-    terms_sems,
-    back_sems,
+    *scatter_parts,
 ):
     n_tp, tile = sizes
     chains, rows, depth = middle.shape
@@ -365,18 +424,19 @@
     hidden_width = w_out.shape[0]
     tiles = hidden_width // tile
     me, peers = tp_peers(n_tp)
+    half = len(scatter_parts) // 2
     enter([peer for _, peer in peers])
-    rows_sent, grad_sent, terms_sent, back_sent = [], [], [], []
+    gather = Gather(rows_full, rows, rows_sems)
+    forward = Scatter(*scatter_parts[: half - 1], rows, scatter_parts[half - 1])
+    backward = Scatter(*scatter_parts[half:-1], rows, scatter_parts[-1])
+    terms, back_terms = forward.terms, backward.terms
     for chain in range(chains):
         normed, _ = normalize(middle[chain])
         rows_full[chain, own_rows(me, rows)] = (normed * mods[3, chain] + mods[4, chain]).astype(bf16)
-        rows_sent.append(gather_send(rows_full, chain, me, rows, rows_sems, peers))
-    for chain in range(chains):
-        grad_full[chain, own_rows(me, rows)] = (mods[5, chain] * cotangent[chain].astype(f32)).astype(bf16)
-        grad_sent.append(gather_send(grad_full, chain, me, rows, grad_sems, peers))
-    for chain in range(chains):
-        for copy in rows_sent[chain]:
-            copy.wait_recv()
+        gather.send(chain)
+    gather.relay(0)
+    for chain in range(chains):
+        gather.take(chain)
         for part in range(tiles):
             here = slice(part * tile, (part + 1) * tile)
             gate = dot(rows_full[chain], w_in[0, :, here])
@@ -384,13 +444,10 @@
             gate_keep[chain, :, here] = gate
             up_keep[chain, :, here] = up
             hidden_keep[chain, :, here] = (gate * jax.nn.sigmoid(gate) * up).astype(bf16)
-        for part in range(depth // tile):
-            here = slice(part * tile, (part + 1) * tile)
-            terms[chain, :, here] = dot(hidden_keep[chain], w_out[:, here]).astype(bf16)
-        terms_sent.append(scatter_send(terms, landing, chain, rows, terms_sems, peers))
-    for chain in range(chains):
-        for copy in grad_sent[chain]:
-            copy.wait_recv()
+        if chain + 1 < chains:
+            gather.relay(chain + 1)
+        if chain > 0:
+            backward.relay(chain - 1)
         for part in range(tiles):
             here = slice(part * tile, (part + 1) * tile)
             grad_hidden = dot(grad_full[chain], w_out[here, :], NT)
@@ -404,7 +461,14 @@
             back_terms[chain, :, here] = (
                 dot(grad_gu[0, chain], w_in[0, here, :], NT) + dot(grad_gu[1, chain], w_in[1, here, :], NT)
             ).astype(bf16)
-        back_sent.append(scatter_send(back_terms, back_landing, chain, rows, back_sems, peers))
+        backward.send(chain)
+    for chain in range(chains):
+        for part in range(depth // tile):
+            here = slice(part * tile, (part + 1) * tile)
+            terms[chain, :, here] = dot(hidden_keep[chain], w_out[:, here]).astype(bf16)
+        forward.send(chain)
+        if chain == 0:
+            backward.relay(chains - 1)
 
     def flat(ref_value):
         return ref_value.reshape(chains * length, ref_value.shape[-1])
@@ -418,18 +482,13 @@
         weight_out[2, :, here] = dot(
             flat(grad_full[...]), flat(hidden_keep[:, :, here]), TN
         ).astype(bf16)
-
-    for chain in range(chains):
-        for copy in terms_sent[chain]:
-            copy.wait_recv()
-        transition = scatter_take(terms, landing, chain, me, rows)
-        upstream = cotangent[chain].astype(f32)
-        result_out[chain] = (middle[chain] + mods[5, chain] * transition).astype(bf16)
-        sums_out[3, chain] = jnp.sum(upstream * transition, axis=0, keepdims=True)
-    for chain in range(chains):
-        for copy in back_sent[chain]:
-            copy.wait_recv()
-        grad_rows = scatter_take(back_terms, back_landing, chain, me, rows)
+        if part < chains:
+            forward.relay(part)
+    for chain in range(tiles, chains):
+        forward.relay(chain)
+
+    for chain in range(chains):
+        grad_rows = backward.take(chain)
         normed, inverse = normalize(middle[chain])
         sums_out[1, chain] = jnp.sum(grad_rows * normed, axis=0, keepdims=True)
         sums_out[2, chain] = jnp.sum(grad_rows, axis=0, keepdims=True)
@@ -437,9 +496,13 @@
         grad_middle_out[chain] = grad_middle
         grad_att_out[chain] = (mods[2, chain] * grad_middle).astype(bf16)
         sums_out[0, chain] = jnp.sum(grad_middle * attended[chain], axis=0, keepdims=True)
-    for group in rows_sent + grad_sent + terms_sent + back_sent:
-        for copy in group:
-            copy.wait_send()
+    for chain in range(chains):
+        transition = forward.take(chain)
+        upstream = cotangent[chain].astype(f32)
+        result_out[chain] = (middle[chain] + mods[5, chain] * transition).astype(bf16)
+        sums_out[3, chain] = jnp.sum(upstream * transition, axis=0, keepdims=True)
+    for part in (gather, forward, backward):
+        part.done()
 
 
 def attn_bwd_kernel(
@@ -465,10 +528,12 @@
     grad_full,
     grad_heads,
     score_send,
-    terms,
-    landing,
     grad_sems,
     score_sems,
+    terms,
+    near,
+    joint,
+    far,
     terms_sems,
     *dp_scratch,
 ):
@@ -485,15 +550,17 @@
         if ff_sum:
             ff_sum.work(count)
 
-    grad_sent, score_sent, terms_sent = [], [], []
+    score_sent = []
+    gather = Gather(grad_full, rows, grad_sems)
+    scatter = Scatter(terms, near, joint, far, rows, terms_sems)
     for chain in range(chains):
         grad_full[chain, own_rows(me, rows)] = grad_att[chain]
-        grad_sent.append(gather_send(grad_full, chain, me, rows, grad_sems, peers))
+        gather.send(chain)
     if ff_sum:
         ff_sum.start()
-    for chain in range(chains):
-        for copy in grad_sent[chain]:
-            copy.wait_recv()
+    gather.relay(0)
+    for chain in range(chains):
+        gather.take(chain)
         work(2)
         grad_gated = dot(grad_full[chain], w_out[...], NT)
         sig = gate_sig[chain]
@@ -515,6 +582,10 @@
             queries.append((dot(grad_scores, key_rows) * scale).astype(bf16))
             keys.append((dot(grad_scores, query, TN) * scale).astype(bf16))
             values.append(dot(weights.astype(bf16), grad_mix_head, TN).astype(bf16))
+            if head == 0 and chain > 0:
+                scatter.relay(chain - 1)
+        if chain + 1 < chains:
+            gather.relay(chain + 1)
         score_sent.append(
             [
                 send(
@@ -531,12 +602,13 @@
         work(2)
         grad_heads[chain] = jnp.concatenate(queries + keys + values + [grad_gate], axis=1)
         terms[chain] = dot(grad_heads[chain], w_in[...], NT).astype(bf16)
-        terms_sent.append(scatter_send(terms, landing, chain, rows, terms_sems, peers))
+        scatter.send(chain)
         work(2)
 
     def flat(ref_value):
         return ref_value.reshape(chains * length, ref_value.shape[-1])
 
+    scatter.relay(chains - 1)
     weight_out[0, :, : 4 * block] = dot(flat(rows_full[...]), flat(grad_heads[...]), TN).astype(bf16)
     work(2)
     weight_out[0, :, 4 * block : 5 * block] = dot(
@@ -546,10 +618,8 @@
     work(1)
 
     for chain in range(chains):
-        for copy in terms_sent[chain]:
-            copy.wait_recv()
+        grad_rows = scatter.take(chain)
         work(2)
-        grad_rows = scatter_take(terms, landing, chain, me, rows)
         normed, inverse = normalize(inputs[chain].astype(f32))
         sums_out[0, chain] = jnp.sum(grad_rows * normed, axis=0, keepdims=True)
         sums_out[1, chain] = jnp.sum(grad_rows, axis=0, keepdims=True)
@@ -564,7 +634,9 @@
         ff_sum.finish()
     else:
         ff_out[...] = jnp.zeros_like(ff_out)
-    for group in grad_sent + score_sent + terms_sent:
+    gather.done()
+    scatter.done()
+    for group in score_sent:
         for copy in group:
             copy.wait_send()
 
@@ -652,20 +724,23 @@
     ff_sums,
     pair_part,
     mods,
+    chain_facts,
     *rest,
 ):
     n_tp, n_dp, all_heads, dp_sizes = sizes
     if dp_sizes:
-        values, totals, own_out, own, arrived, tp_sems, dp_sems, *dp_scratch = rest
+        values, totals, facts_all, own_out, own, arrived, tp_sems, dp_sems, facts_sems, *dp_scratch = rest
         attn_sum = DpSum(dp_sizes, values, own_out, *dp_scratch)
     else:
-        totals, own, arrived, tp_sems, dp_sems = rest
+        totals, facts_all, own, arrived, tp_sems, dp_sems, facts_sems = rest
         attn_sum = None
     chains, depth = mods.shape[1], mods.shape[3]
     channels = pair_part.shape[1]
     _, peers = tp_peers(n_tp)
     place, others = dp_others(n_dp)
     enter([peer for _, peer in peers] + others)
+    facts_all[place] = chain_facts[...]
+    facts_sent = share_over_dp(facts_all, place, others, facts_sems)
     if attn_sum:
         attn_sum.start()
     for chain in range(chains):
@@ -695,9 +770,9 @@
     dp_sent = share_over_dp(totals, place, others, dp_sems)
     if attn_sum:
         attn_sum.finish()
-    for copy in dp_sent:
+    for copy in dp_sent + facts_sent:
         copy.wait_recv()
-    for copy in tp_sent + dp_sent:
+    for copy in tp_sent + dp_sent + facts_sent:
         copy.wait_send()
 
 
@@ -757,19 +832,17 @@
     pair_w = jnp.pad(pair_weight, ((0, padded - all_heads), (0, 0)))
     w_in = jnp.swapaxes(attn_in, 0, 1).reshape(depth, 4 * block)
 
-    high = condition.astype(bf16)
-    low = (condition - high.astype(f32)).astype(bf16)
     classes = onehot.shape[1]
-    facts = jnp.concatenate([high, low, onehot.astype(bf16)], axis=1)
-    facts = jnp.pad(facts, ((0, -chains % 16), (0, -facts.shape[1] % LANES)))
+    facts = jnp.concatenate([condition, onehot], axis=1)
+    facts = jnp.pad(facts, ((0, 0), (0, -facts.shape[1] % LANES)))
     direct = n_dp == 8
     dp_grid = (n_dp // 2, 2)
     own_count = depth // n_dp
     step_rows = 16
     full = (chains, length, depth)
     own = (chains, rows, depth)
-    rows_full, heads_kept, gate_sig, soft, mix, gated, attended, middle, facts_all = pl.pallas_call(
-        functools.partial(attn_fwd_kernel, (n_tp, n_dp, heads, width)),
+    rows_full, heads_kept, gate_sig, soft, mix, gated, attended, middle, grad_trans_full = pl.pallas_call(
+        functools.partial(attn_fwd_kernel, (n_tp, heads, width)),
         out_shape=(
             sds(full, bf16),
             sds((chains, length, 4 * block), bf16),
@@ -779,7 +852,7 @@
             sds((chains, length, block), bf16),
             sds(own, f32),
             sds(own, f32),
-            sds((n_dp,) + facts.shape, bf16),
+            sds(full, bf16),
         ),
         in_specs=[VMEM_SPEC] * 7 + [ANY_SPEC],
         out_specs=[VMEM_SPEC] * 9,
@@ -788,17 +861,15 @@
             pltpu.VMEM((length // LANES, step_rows * padded, LANES), f32),
             pltpu.VMEM((n_tp, chains, heads, rows, length), bf16),
             pltpu.VMEM((chains, heads, length, length), bf16),
-            pltpu.VMEM(full, bf16),
-            pltpu.VMEM((n_tp - 1,) + own, bf16),
+            pair_sems(chains, 3),
+            pair_sems(chains, 3),
             pair_sems(chains, n_tp - 1),
-            pair_sems(chains, n_tp - 1),
-            pair_sems(chains, n_tp - 1),
-            pair_sems(n_dp - 1),
             pltpu.SemaphoreType.DMA((2,)),
-        ],
+        ]
+        + scatter_scratch(chains, rows, length, depth),
         compiler_params=params(0),
         name="attn_fwd",
-    )(activations, mods, valid, pair_w, w_in, attn_out, facts, pair_rep)
+    )(activations, mods, valid, pair_w, w_in, attn_out, cotangent, pair_rep)
 
     result, grad_middle, grad_att, ff_sums, ff_weights = pl.pallas_call(
         functools.partial(ff_kernel, (n_tp, 256)),
@@ -809,27 +880,20 @@
             sds((4, chains, 1, depth), f32),
             sds((3, depth, hidden_width), bf16),
         ),
-        in_specs=[VMEM_SPEC] * 6,
+        in_specs=[VMEM_SPEC] * 7,
         out_specs=[VMEM_SPEC] * 5,
         scratch_shapes=[
-            pltpu.VMEM(full, bf16),
             pltpu.VMEM(full, bf16),
             pltpu.VMEM((chains, length, hidden_width), f32),
             pltpu.VMEM((chains, length, hidden_width), f32),
             pltpu.VMEM((chains, length, hidden_width), bf16),
             pltpu.VMEM((2, chains, length, hidden_width), bf16),
-            pltpu.VMEM(full, bf16),
-            pltpu.VMEM(full, bf16),
-            pltpu.VMEM((n_tp - 1,) + own, bf16),
-            pltpu.VMEM((n_tp - 1,) + own, bf16),
-            pair_sems(chains, n_tp - 1),
-            pair_sems(chains, n_tp - 1),
-            pair_sems(chains, n_tp - 1),
-            pair_sems(chains, n_tp - 1),
-        ],
+            pair_sems(chains, 3),
+        ]
+        + scatter_scratch(chains, rows, length, depth) * 2,
         compiler_params=params(1),
         name="ff",
-    )(middle, cotangent, attended, mods, ff_in, ff_out)
+    )(middle, cotangent, attended, mods, grad_trans_full, ff_in, ff_out)
 
     wide = -(-5 * block // LANES) * LANES
     ff_sizes = dp_grid + (6,) if direct else None
@@ -850,12 +914,10 @@
             pltpu.VMEM(full, bf16),
             pltpu.VMEM((chains, length, 4 * block), bf16),
             pltpu.VMEM(score_shape, bf16),
-            pltpu.VMEM(full, bf16),
-            pltpu.VMEM((n_tp - 1,) + own, bf16),
-            pair_sems(chains, n_tp - 1),
-            pair_sems(chains, n_tp - 1),
+            pair_sems(chains, 3),
             pair_sems(chains, n_tp - 1),
         ]
+        + scatter_scratch(chains, rows, length, depth)
         + (dp_sum_scratch(ff_sizes, 3, own_count, hidden_width) if direct else []),
         compiler_params=params(2),
         name="attn_bwd",
@@ -893,19 +955,20 @@
 
     attn_sizes = dp_grid + (6,) if direct else None
     total_rows = 6 * chains + all_heads * channels // depth
-    tail_in = [attn_sums, ff_sums, pair_part, mods]
-    tail_out = [sds((n_dp, total_rows, depth), bf16)]
+    tail_in = [attn_sums, ff_sums, pair_part, mods, facts]
+    tail_out = [sds((n_dp, total_rows, depth), bf16), sds((n_dp,) + facts.shape, f32)]
     tail_scratch = [
         pltpu.VMEM((total_rows, depth), bf16),
         pltpu.VMEM((n_tp - 1, total_rows, depth), bf16),
         pair_sems(n_tp - 1),
+        pair_sems(n_dp - 1),
         pair_sems(n_dp - 1),
     ]
     if direct:
         tail_in.append(attn_weights.reshape(1, n_dp, own_count, wide))
         tail_out.append(sds((1, own_count, wide), f32))
         tail_scratch += dp_sum_scratch(attn_sizes, 1, own_count, wide)
-    totals, *rest = pl.pallas_call(
+    totals, facts_all, *rest = pl.pallas_call(
         functools.partial(tail_kernel, (n_tp, n_dp, all_heads, attn_sizes)),
         out_shape=tuple(tail_out),
         in_specs=[VMEM_SPEC] * len(tail_in),
@@ -937,10 +1000,10 @@
     mod_all = totals[:, : 6 * chains].reshape(n_dp, 6, chains, depth)
     mod_all = jnp.swapaxes(mod_all, 1, 2).reshape(n_dp * chains, 6 * depth)
     pair_all = totals[:, 6 * chains :].reshape(n_dp, all_heads, channels)
-    facts_rows = facts_all[:, :chains].astype(f32).reshape(n_dp * chains, -1)
+    facts_rows = facts_all.reshape(n_dp * chains, -1)
     cond_wide = condition.shape[1]
-    cond_all = facts_rows[:, :cond_wide] + facts_rows[:, cond_wide : 2 * cond_wide]
-    onehot_all = facts_rows[:, 2 * cond_wide : 2 * cond_wide + classes]
+    cond_all = facts_rows[:, :cond_wide]
+    onehot_all = facts_rows[:, cond_wide : cond_wide + classes]
     grad_ada = jnp.dot(cond_all.T, own_columns(mod_all, 1), precision=highest)
     grad_cond = jnp.dot(mod_all, own_columns(ada_weight, 0).astype(f32).T, precision=highest)
     grad_table = jnp.dot(onehot_all.T, grad_cond, precision=highest)

time: 208 us -> 185 us (0.89)
  Pallas kernels: 183 us -> 164 us
  local copies, waits for them, and re-layouts: 12.7 us -> 8.92 us
    pallas_call x1, Pallas kernels: 41.5 us -> 25.9 us  [local(): pl.pallas_call(functools.partial(ff_kernel, (n_tp, 256)), out_shape=(sds(...]
    pallas_call x1, Pallas kernels: 37.7 us -> 32.5 us  [local(): pl.pallas_call(functools.partial(attn_fwd_kernel, (n_tp, heads, width)),...]
    pallas_call x1, Pallas kernels: 52.7 us -> 54.9 us  [local(): pl.pallas_call(functools.partial(attn_bwd_kernel, (n_tp, heads, width, ff...]
where the time goes in v4:
time: 185 us; the launch traced here: 184 us
  Pallas kernels  164 us (89%)
  local copies, waits for them, and re-layouts  8.92 us (5%)
  matrix products  6.89 us (4%)
  other arithmetic  3.87 us (2%)
    pallas_call x1, Pallas kernels, local(): pl.pallas_call(functools.partial(attn_bwd_kernel, (n_tp, heads, width, ff...  54.9 us
    pallas_call x1, Pallas kernels, local(): pl.pallas_call(functools.partial(tail_kernel, (n_tp, n_dp, all_heads, att...  32.6 us
    pallas_call x1, Pallas kernels, local(): pl.pallas_call(functools.partial(attn_fwd_kernel, (n_tp, heads, width)),...  32.5 us
    pallas_call x1, Pallas kernels, local(): pl.pallas_call(functools.partial(ff_kernel, (n_tp, 256)), out_shape=(sds(...  25.9 us
    pallas_call x1, Pallas kernels, local(): pl.pallas_call(functools.partial(pair_kernel, (n_tp, heads)), out_shape=(...  18 us

profile of v4, /device:TPU:0, one launch (start us, length us, event | category | flops | bytes accessed | tf_op | source)
XLA Modules:
  0.0 184.4 jit_solution(1290032907115388663)
XLA Ops:
  0.6 0.0 copy-start
  0.7 0.8 broadcast_multiply_fusion
  1.4 0.1 multiply_sine_fusion
  1.6 0.8 convolution_add_fusion
  2.4 2.7 %fusion.21 = f32[2,4608]{1,0:T(2,128)S(1)} fusion(f32[2,256]{1,0:T(2,128)S(1)} %convolution_add_fusion, bf16[256,4608]{1,0:T(8,128)(2,1)} %param.18), kind=kOutput, calls=%fused_computation.46 | convolution fusion | flops 28311552 | bytes 2398208 | tf_op jit(solution)/shard_map/dot_general | solution.py:824
  5.3 0.0 copy-start.3
  5.3 1.5 copy.26.w_in
  6.8 0.6 pad.8.pair_w
  7.4 0.6 compare_convert_fusion.valid
  8.0 32.5 %attn_fwd.1 = (bf16[2,256,768]{2,1,0:T(8,128)(2,1)}, bf16[2,256,768]{2,1,0:T(8,128)(2,1)}, f32[2,256,192]{2,1,0:T(8,128)}, f32[2,3,256,256]{3,2,1,0:T(8,128)}, f...) custom-call(bf16[2,64,768]{2,1,0:T(8,128)(2,1)} %inputs.3, ...), custom_call_target="tpu_custom_call" | custom-call | tf_op jit(solution)/shard_map/attn_fwd/pallas_call | solution.py:844
  40.6 25.9 %ff.1 = (bf16[2,64,768]{2,1,0:T(8,128)(2,1)}, f32[2,64,768]{2,1,0:T(8,128)}, bf16[2,64,768]{2,1,0:T(8,128)(2,1)}, f32[4,2,1,768]{3,2,1,0:T(1,128)}, bf16[3,768,768]{2,1,0:T(8,128)(2,1)}) custom-call(f32[2,64,768]{2,1,0:T(8,128)} %get-tuple-element.34.middle, bf16[2,64,768]{2,1,0:T(8,128)(2,1)} %cotangent.3, f32[2,64,768]{2,1,0:T(8,128)} %get-tuple-element.35.attended, ...), custom_call_target="tpu_custom_call" | custom-call | tf_op jit(solution)/shard_map/ff/pallas_call | solution.py:874
  66.4 54.9 %attn_bwd.1 = (bf16[2,64,768]{2,1,0:T(8,128)(2,1)}, f32[2,2,1,768]{3,2,1,0:T(1,128)}, bf16[1,768,1024]{2,1,0:T(8,128)(2,1)}, bf16[4,2,3,64,256]{4,3,2,1,0:T(8,128)(2,1)}, f32[3,96,768]{2,1,0:T(8,128)}) custom-call(bf16[2,64,768]{2,1,0:T(8,128)(2,1)} %inputs.3, f32[6,2,1,768]{3,2,1,0:T(1,128)} %copy-done.3, bf16[2,64,768]{2,1,0:T(8,128)(2,1)} %get-tuple-element.38.grad_att, ...), custom_call_target="tpu_custom_call" | custom-call | tf_op jit(solution)/shard_map/attn_bwd/pallas_call | solution.py:902
  121.4 0.0 copy-start.9
  121.4 18.0 %pair_grad.1 = (f32[16,256]{1,0:T(8,128)}, bf16[2,64,256,256]{3,2,1,0:T(8,128)(2,1)}) custom-call(bf16[4,2,3,64,256]{4,3,2,1,0:T(8,128)(2,1)} %get-tuple-element.48.score_full, bf16[16,256]{1,0:T(8,128)(2,1)} %pad.8.pair_w, bf16[2,64,256,256]{3,2,1,0:T(8,128)(2,1)} %pair_hbm.3), custom_call_target="tpu_custom_call" | custom-call | tf_op jit(solution)/shard_map/pair_grad/pallas_call | solution.py:940
  139.4 0.1 fusion.17
  139.5 0.6 select_maximum_fusion.chain_facts
  140.1 32.6 %tail.1 = (bf16[8,16,768]{2,1,0:T(8,128)(2,1)}, f32[8,2,384]{2,1,0:T(2,128)}, f32[1,96,1024]{2,1,0:T(8,128)}) custom-call(f32[2,2,1,768]{3,2,1,0:T(1,128)} %get-tuple-element.50.attn_sums, f32[4,2,1,768]{3,2,1,0:T(1,128)} %get-tuple-element.51.ff_sums, f32[16,256]{1,0:T(8,128)} %get-tuple-element.52.pair_part, f32[6,2,1,768]{3,2,1,0:T(1,128)} %copy-done.3, ...), custom_call_target="tpu_custom_call" | custom-call | tf_op jit(solution)/shard_map/tail/pallas_call | solution.py:971
  172.6 1.0 copy.29
  173.8 1.2 fusion
  175.0 0.8 reshape.182
  175.7 0.8 fusion.5
  176.6 1.3 fusion.2
  177.9 0.3 reshape_squeeze.3
  178.2 0.8 copy.34
  179.0 0.9 slice_convert_fusion
  179.9 0.1 reshape.188
  180.0 0.7 dynamic-slice_reduce_fusion
  180.7 0.7 copy.31
  181.5 0.9 slice.51
  182.3 0.7 slice_bitcast_fusion
  183.0 0.7 copy.42
  183.7 0.7 copy.43
  (29 shorter events, 0.3 us)
Async XLA Ops:
  0.6 0.9 copy-start
  0.7 4.7 %copy-start.1 = (bf16[4,768,192]{1,2,0:T(8,128)(2,1)S(1)}, bf16[4,768,192]{1,2,0:T(8,128)(2,1)}, u32[]{:S(2)}) copy-start(bf16[4,768,192]{1,2,0:T(8,128)(2,1)} %param.21) | copy-start | bytes 3538948
  2.4 4.4 %copy-start.7 = (bf16[12,256]{1,0:T(8,128)(2,1)S(1)}, bf16[12,256]{1,0:T(8,128)(2,1)}, u32[]{:S(2)}) copy-start(bf16[12,256]{1,0:T(8,128)(2,1)} %param.20) | copy-start | bytes 18436
  2.4 5.0 %copy-start.8 = (s32[2]{0:T(128)S(1)}, s32[2]{0:T(128)}, u32[]{:S(2)}) copy-start(s32[2]{0:T(128)} %param.17) | copy-start | bytes 28
  5.3 2.7 %copy-start.3 = (f32[6,2,1,768]{3,2,1,0:T(1,128)}, f32[6,2,1,768]{3,2,1,0:T(1,128)S(1)}, u32[]{:S(2)}) copy-start(f32[6,2,1,768]{3,2,1,0:T(1,128)S(1)} %constant_dynamic-update-slice_fusion.mods) | copy-start | bytes 110596
  121.4 18.0 %copy-start.9 = (s32[2]{0:T(128)S(1)}, s32[2]{0:T(128)}, u32[]{:S(2)}) copy-start(s32[2]{0:T(128)} %param.16) | copy-start | bytes 28
  172.6 5.3 %copy-start.4 = (f32[1,96,1024]{2,1,0:T(8,128)S(1)}, f32[1,96,1024]{2,1,0:T(8,128)}, u32[]{:S(2)}) copy-start(f32[1,96,1024]{2,1,0:T(8,128)} %get-tuple-element.54) | copy-start | bytes 1179652
  173.7 7.8 %copy-start.2 = (f32[3,96,768]{2,1,0:T(8,128)S(1)}, f32[3,96,768]{2,1,0:T(8,128)}, u32[]{:S(2)}) copy-start(f32[3,96,768]{2,1,0:T(8,128)} %get-tuple-element.55) | copy-start | bytes 2654212
  177.9 5.2 %copy-start.5 = (bf16[2,64,768]{2,1,0:T(8,128)(2,1)S(1)}, bf16[2,64,768]{2,1,0:T(8,128)(2,1)}, u32[]{:S(2)}) copy-start(bf16[2,64,768]{2,1,0:T(8,128)(2,1)} %get-tuple-element.90) | copy-start | bytes 589828
  177.9 5.8 %copy-start.6 = (bf16[2,64,768]{2,1,0:T(8,128)(2,1)S(1)}, bf16[2,64,768]{2,1,0:T(8,128)(2,1)}, u32[]{:S(2)}) copy-start(bf16[2,64,768]{2,1,0:T(8,128)(2,1)} %get-tuple-element.91) | copy-start | bytes 589828

commit v5 on v4

--- a/solution.py
+++ b/solution.py
@@ -520,11 +520,15 @@
     w_in,
     w_out,
     ff_values,
+    pair_w,
+    pair_hbm,
     grad_inputs_out,
     sums_out,
     weight_out,
     score_full,
     ff_out,
+    pair_w_out,
+    stacked_out,
     grad_full,
     grad_heads,
     score_send,
@@ -535,6 +539,9 @@
     joint,
     far,
     terms_sems,
+    stack,
+    pair_buf,
+    in_sems,
     *dp_scratch,
 ):
     n_tp, heads, width, dp_sizes = sizes
@@ -543,6 +550,19 @@
     block = heads * width
     scale = width ** (-0.5)
     me, peers = tp_peers(n_tp)
+    step_rows = pair_buf.shape[1]
+    steps = rows // step_rows
+    turns = chains * steps
+
+    def fetch(turn):
+        return pltpu.make_async_copy(
+            pair_hbm.at[turn // steps, pl.ds(turn % steps * step_rows, step_rows)],
+            pair_buf.at[turn % 2],
+            in_sems.at[turn % 2],
+        )
+
+    fetch(0).start()
+    fetch(1).start()
     ff_sum = DpSum(dp_sizes, ff_values, ff_out, *dp_scratch) if dp_sizes else None
     enter([peer for _, peer in peers] + (ff_sum.peers() if ff_sum else []))
 
@@ -561,7 +581,8 @@
     gather.relay(0)
     for chain in range(chains):
         gather.take(chain)
-        work(2)
+        if chain == 0:
+            work(2)
         grad_gated = dot(grad_full[chain], w_out[...], NT)
         sig = gate_sig[chain]
         grad_mix = (grad_gated * sig).astype(bf16)
@@ -603,14 +624,14 @@
         grad_heads[chain] = jnp.concatenate(queries + keys + values + [grad_gate], axis=1)
         terms[chain] = dot(grad_heads[chain], w_in[...], NT).astype(bf16)
         scatter.send(chain)
-        work(2)
+        work(1)
 
     def flat(ref_value):
         return ref_value.reshape(chains * length, ref_value.shape[-1])
 
     scatter.relay(chains - 1)
     weight_out[0, :, : 4 * block] = dot(flat(rows_full[...]), flat(grad_heads[...]), TN).astype(bf16)
-    work(2)
+    work(1)
     weight_out[0, :, 4 * block : 5 * block] = dot(
         flat(grad_full[...]), flat(gated[...]), TN
     ).astype(bf16)
@@ -619,7 +640,7 @@
 
     for chain in range(chains):
         grad_rows = scatter.take(chain)
-        work(2)
+        work(1)
         normed, inverse = normalize(inputs[chain].astype(f32))
         sums_out[0, chain] = jnp.sum(grad_rows * normed, axis=0, keepdims=True)
         sums_out[1, chain] = jnp.sum(grad_rows, axis=0, keepdims=True)
@@ -630,6 +651,33 @@
     for chain in range(chains):
         for copy in score_sent[chain]:
             copy.wait_recv()
+
+    padded = pair_w.shape[0]
+    pair_w_out[...] = jnp.zeros_like(pair_w_out)
+    stack[...] = jnp.zeros_like(stack)
+    for turn in range(turns):
+        chain, first_row = turn // steps, turn % steps * step_rows
+        fetch(turn).wait()
+        for head in range(heads * n_tp):
+            for part in range(length // LANES):
+                stack[part, pl.ds(head, step_rows, stride=padded), :] = score_full[
+                    head // heads, chain, head % heads, first_row : first_row + step_rows, lanes(part)
+                ].astype(f32)
+
+        def pair_row(row, total):
+            at = pl.ds(pl.multiple_of(row * padded, padded), padded)
+            scores = jnp.concatenate(
+                [stack[part, at, :] for part in range(length // LANES)], axis=1
+            ).astype(bf16)
+            stacked_out[chain, first_row + row] = scores
+            return total + dot(scores, pair_buf[turn % 2, row])
+
+        pair_w_out[...] += lax.fori_loop(
+            0, step_rows, pair_row, jnp.zeros(pair_w_out.shape, f32), unroll=True
+        )
+        if turn + 2 < turns:
+            fetch(turn + 2).start()
+        work(1)
     if ff_sum:
         ff_sum.finish()
     else:
@@ -641,81 +689,9 @@
             copy.wait_send()
 
 
-def pair_kernel(
-    sizes,
-    score_full,
-    pair_w,
-    pair_hbm,
-    pair_w_out,
-    grad_pair_hbm,
-    stack,
-    pair_buf,
-    out_buf,
-    in_sems,
-    out_sems,
-):
-    n_tp, heads = sizes
-    chains, rows, length = score_full.shape[1], score_full.shape[3], score_full.shape[4]
-    step_rows = pair_buf.shape[1]
-    steps = rows // step_rows
-    turns = chains * steps
-
-    def fetch(turn, slot):
-        return pltpu.make_async_copy(
-            pair_hbm.at[turn // steps, pl.ds(lax.rem(turn, steps) * step_rows, step_rows)],
-            pair_buf.at[slot],
-            in_sems.at[slot],
-        )
-
-    def put(turn, slot):
-        return pltpu.make_async_copy(
-            out_buf.at[slot],
-            grad_pair_hbm.at[turn // steps, pl.ds(lax.rem(turn, steps) * step_rows, step_rows)],
-            out_sems.at[slot],
-        )
-
-    fetch(0, 0).start()
-    fetch(1, 1).start()
-    padded = pair_w.shape[0]
-    pair_w_here = pair_w[...]
-    pair_w_out[...] = jnp.zeros_like(pair_w_out)
-    stack[...] = jnp.zeros_like(stack)
-
-    def pair_step(turn, carry):
-        slot = lax.rem(turn, 2)
-        chain = turn // steps
-        fetch(turn, slot).wait()
-        place = pl.ds(pl.multiple_of(lax.rem(turn, steps) * step_rows, step_rows), step_rows)
-        for head in range(heads * n_tp):
-            for part in range(length // LANES):
-                stack[part, pl.ds(head, step_rows, stride=padded), :] = score_full[
-                    head // heads, chain, head % heads, place, lanes(part)
-                ].astype(f32)
-
-        @pl.when(turn >= 2)
-        def _():
-            put(turn - 2, slot).wait()
-
-        total = jnp.zeros(pair_w_out.shape, f32)
-        for row in range(step_rows):
-            scores = jnp.concatenate(
-                [stack[part, row * padded : (row + 1) * padded, :] for part in range(length // LANES)],
-                axis=1,
-            ).astype(bf16)
-            out_buf[slot, row] = dot(scores, pair_w_here, TN).astype(bf16)
-            total = total + dot(scores, pair_buf[slot, row])
-        pair_w_out[...] += total
-
-        @pl.when(turn + 2 < turns)
-        def _():
-            fetch(turn + 2, slot).start()
-
-        put(turn, slot).start()
-        return carry
-
-    lax.fori_loop(0, turns, pair_step, 0)
-    put(turns - 2, lax.rem(turns - 2, 2)).wait()
-    put(turns - 1, lax.rem(turns - 1, 2)).wait()
+def pair_kernel(stacked, pair_w, grad_pair):
+    for row in range(stacked.shape[1]):
+        grad_pair[0, row] = dot(stacked[0, row], pair_w[...], TN).astype(bf16)
 
 
 def tail_kernel(
@@ -899,7 +875,7 @@
     ff_sizes = dp_grid + (6,) if direct else None
     ff_values = ff_weights.reshape(3, n_dp, own_count, hidden_width)
     score_shape = (n_tp, chains, heads, rows, length)
-    grad_inputs, attn_sums, attn_weights, score_full, ff_own = pl.pallas_call(
+    grad_inputs, attn_sums, attn_weights, _, ff_own, pair_part, stacked = pl.pallas_call(
         functools.partial(attn_bwd_kernel, (n_tp, heads, width, ff_sizes)),
         out_shape=(
             sds(own, bf16),
@@ -907,9 +883,11 @@
             sds((1, depth, wide), bf16),
             sds(score_shape, bf16),
             sds((3, own_count, hidden_width), f32),
+            sds((padded, channels), f32),
+            sds((chains, rows, padded, length), bf16),
         ),
-        in_specs=[VMEM_SPEC] * 13,
-        out_specs=[VMEM_SPEC] * 5,
+        in_specs=[VMEM_SPEC] * 14 + [ANY_SPEC],
+        out_specs=[VMEM_SPEC] * 7,
         scratch_shapes=[
             pltpu.VMEM(full, bf16),
             pltpu.VMEM((chains, length, 4 * block), bf16),
@@ -918,6 +896,11 @@
             pair_sems(chains, n_tp - 1),
         ]
         + scatter_scratch(chains, rows, length, depth)
+        + [
+            pltpu.VMEM((length // LANES, step_rows * padded, LANES), f32),
+            pltpu.VMEM((2, step_rows, length, channels), bf16),
+            pltpu.SemaphoreType.DMA((2,)),
+        ]
         + (dp_sum_scratch(ff_sizes, 3, own_count, hidden_width) if direct else []),
         compiler_params=params(2),
         name="attn_bwd",
@@ -935,23 +918,23 @@
         w_in,
         attn_out,
         ff_values,
+        pair_w,
+        pair_rep,
     )
 
-    pair_part, grad_pair = pl.pallas_call(
-        functools.partial(pair_kernel, (n_tp, heads)),
-        out_shape=(sds((padded, channels), f32), sds(pair_rep.shape, bf16)),
-        in_specs=[VMEM_SPEC] * 2 + [ANY_SPEC],
-        out_specs=[VMEM_SPEC, ANY_SPEC],
-        scratch_shapes=[
-            pltpu.VMEM((length // LANES, step_rows * padded, LANES), f32),
-            pltpu.VMEM((2, step_rows, length, channels), bf16),
-            pltpu.VMEM((2, step_rows, length, channels), bf16),
-            pltpu.SemaphoreType.DMA((2,)),
-            pltpu.SemaphoreType.DMA((2,)),
+    grad_pair = pl.pallas_call(
+        pair_kernel,
+        out_shape=sds(pair_rep.shape, bf16),
+        grid=(chains, rows // step_rows),
+        in_specs=[
+            pl.BlockSpec((1, step_rows, padded, length), lambda chain, step: (chain, step, 0, 0)),
+            pl.BlockSpec((padded, channels), lambda chain, step: (0, 0)),
         ],
-        compiler_params=pltpu.CompilerParams(vmem_limit_bytes=62 * 1024 * 1024),
+        out_specs=pl.BlockSpec(
+            (1, step_rows, length, channels), lambda chain, step: (chain, step, 0, 0)
+        ),
         name="pair_grad",
-    )(score_full, pair_w, pair_rep)
+    )(stacked, pair_w)
 
     attn_sizes = dp_grid + (6,) if direct else None
     total_rows = 6 * chains + all_heads * channels // depth

time: 185 us -> 182 us (0.984)
  Pallas kernels: 164 us -> 156 us
  local copies, waits for them, and re-layouts: 8.92 us -> 12.5 us
    pallas_call x1, Pallas kernels: 18 us -> 10.3 us  [local(): pl.pallas_call(pair_kernel, out_shape=sds(pair_rep.shape, bf16), grid=(ch...]
where the time goes in v5:
time: 182 us; the launch traced here: 181 us
  Pallas kernels  156 us (86%)
  local copies, waits for them, and re-layouts  12.5 us (7%)
  matrix products  6.84 us (4%)
  other arithmetic  4.29 us (2%)
    pallas_call x1, Pallas kernels, local(): pl.pallas_call(functools.partial(attn_bwd_kernel, (n_tp, heads, width, ff...  55.3 us
    pallas_call x1, Pallas kernels, local(): pl.pallas_call(functools.partial(tail_kernel, (n_tp, n_dp, all_heads, att...  32.5 us
    pallas_call x1, Pallas kernels, local(): pl.pallas_call(functools.partial(attn_fwd_kernel, (n_tp, heads, width)),...  32.4 us
    pallas_call x1, Pallas kernels, local(): pl.pallas_call(functools.partial(ff_kernel, (n_tp, 256)), out_shape=(sds(...  25.9 us
    pallas_call x1, Pallas kernels, local(): pl.pallas_call(pair_kernel, out_shape=sds(pair_rep.shape, bf16), grid=(ch...  10.3 us

profile of v5, /device:TPU:0, one launch (start us, length us, event | category | flops | bytes accessed | tf_op | source)
XLA Modules:
  0.0 180.9 jit_solution(3587693507756836954)
XLA Ops:
  0.6 0.0 copy-start
  0.7 0.8 broadcast_multiply_fusion
  1.4 0.7 fusion.17
  2.2 0.1 multiply_sine_fusion
  2.3 0.8 convolution_add_fusion
  3.1 0.6 select_maximum_fusion.chain_facts
  3.7 1.3 compare_convert_fusion.valid
  5.0 1.3 pad.8.pair_w
  6.3 2.7 %fusion.21 = f32[2,4608]{1,0:T(2,128)S(1)} fusion(f32[2,256]{1,0:T(2,128)S(1)} %convolution_add_fusion, bf16[256,4608]{1,0:T(8,128)(2,1)} %param.18), kind=kOutput, calls=%fused_computation.46 | convolution fusion | flops 28311552 | bytes 2398208 | tf_op jit(solution)/shard_map/dot_general | solution.py:800
  9.2 0.0 copy-start.2
  9.2 1.5 copy.26.w_in
  10.7 32.4 %attn_fwd.1 = (bf16[2,256,768]{2,1,0:T(8,128)(2,1)}, bf16[2,256,768]{2,1,0:T(8,128)(2,1)}, f32[2,256,192]{2,1,0:T(8,128)}, f32[2,3,256,256]{3,2,1,0:T(8,128)}, f...) custom-call(bf16[2,64,768]{2,1,0:T(8,128)(2,1)} %inputs.3, ...), custom_call_target="tpu_custom_call" | custom-call | tf_op jit(solution)/shard_map/attn_fwd/pallas_call | solution.py:820
  43.1 25.9 %ff.1 = (bf16[2,64,768]{2,1,0:T(8,128)(2,1)}, f32[2,64,768]{2,1,0:T(8,128)}, bf16[2,64,768]{2,1,0:T(8,128)(2,1)}, f32[4,2,1,768]{3,2,1,0:T(1,128)}, bf16[3,768,768]{2,1,0:T(8,128)(2,1)}) custom-call(f32[2,64,768]{2,1,0:T(8,128)} %get-tuple-element.33.middle, bf16[2,64,768]{2,1,0:T(8,128)(2,1)} %cotangent.3, f32[2,64,768]{2,1,0:T(8,128)} %get-tuple-element.34.attended, ...), custom_call_target="tpu_custom_call" | custom-call | tf_op jit(solution)/shard_map/ff/pallas_call | solution.py:850
  69.0 55.3 %attn_bwd.1 = (bf16[2,64,768]{2,1,0:T(8,128)(2,1)}, f32[2,2,1,768]{3,2,1,0:T(1,128)}, bf16[1,768,1024]{2,1,0:T(8,128)(2,1)}, bf16[4,2,3,64,256]{4,3,2,1,0:T(8,12...) custom-call(bf16[2,64,768]{2,1,0:T(8,128)(2,1)} %inputs.3, ...), custom_call_target="tpu_custom_call" | custom-call | tf_op jit(solution)/shard_map/attn_bwd/pallas_call | solution.py:878
  124.3 1.7 slice_bitcast_fusion
  126.0 1.9 %slice.51 = f32[2,96,768]{2,1,0:T(8,128)} slice(f32[3,96,768]{2,1,0:T(8,128)} %get-tuple-element.53), slice={[0:2], [0:96], [0:768]} | slice | bytes 1179648 | tf_op jit(solution)/shard_map/slice | solution.py:1001
  127.9 32.5 %tail.1 = (bf16[8,16,768]{2,1,0:T(8,128)(2,1)}, f32[8,2,384]{2,1,0:T(2,128)}, f32[1,96,1024]{2,1,0:T(8,128)}) custom-call(f32[2,2,1,768]{3,2,1,0:T(1,128)} %get-tuple-element.48.attn_sums, f32[4,2,1,768]{3,2,1,0:T(1,128)} %get-tuple-element.49.ff_sums, f32[16,256]{1,0:T(8,128)} %get-tuple-element.50.pair_part, f32[6,2,1,768]{3,2,1,0:T(1,128)} %copy-done.2, ...), custom_call_target="tpu_custom_call" | custom-call | tf_op jit(solution)/shard_map/tail/pallas_call | solution.py:954
  160.5 0.8 reshape.182
  161.3 0.9 slice_bitcast_fusion.1
  162.2 1.0 slice.49
  163.2 0.7 copy.31
  163.9 0.3 reshape_squeeze.3
  164.2 0.8 copy.34
  165.0 0.0 copy-done.3
  165.0 0.1 reshape.188
  165.1 0.7 dynamic-slice_reduce_fusion
  165.9 1.2 fusion
  167.1 0.8 fusion.5
  167.9 1.3 fusion.2
  169.2 10.3 %pair_grad.1 = bf16[2,64,256,256]{3,2,1,0:T(8,128)(2,1)} custom-call(bf16[2,64,16,256]{3,2,1,0:T(8,128)(2,1)} %get-tuple-element.47.stacked, bf16[16,256]{1,0:T(8,128)(2,1)} %pad.8.pair_w), custom_call_target="tpu_custom_call" | custom-call | tf_op jit(solution)/shard_map/pair_grad/pallas_call | solution.py:925
  179.5 0.7 copy.42
  180.2 0.7 copy.43
  (21 shorter events, 0.3 us)
Async XLA Ops:
  0.6 1.6 copy-start
  0.7 8.5 %copy-start.1 = (bf16[4,768,192]{1,2,0:T(8,128)(2,1)S(1)}, bf16[4,768,192]{1,2,0:T(8,128)(2,1)}, u32[]{:S(2)}) copy-start(bf16[4,768,192]{1,2,0:T(8,128)(2,1)} %param.21) | copy-start | bytes 3538948
  9.2 1.5 copy-start.2
  160.5 4.5 %copy-start.3 = (bf16[8,16,768]{2,1,0:T(8,128)(2,1)S(1)}, bf16[8,16,768]{2,1,0:T(8,128)(2,1)}, u32[]{:S(2)}) copy-start(bf16[8,16,768]{2,1,0:T(8,128)(2,1)} %get-tuple-element.55) | copy-start | bytes 589828
  169.2 10.3 %copy-start.4 = (bf16[2,64,768]{2,1,0:T(8,128)(2,1)S(1)}, bf16[2,64,768]{2,1,0:T(8,128)(2,1)}, u32[]{:S(2)}) copy-start(bf16[2,64,768]{2,1,0:T(8,128)(2,1)} %get-tuple-element.88) | copy-start | bytes 589828
  169.2 11.0 %copy-start.5 = (bf16[2,64,768]{2,1,0:T(8,128)(2,1)S(1)}, bf16[2,64,768]{2,1,0:T(8,128)(2,1)}, u32[]{:S(2)}) copy-start(bf16[2,64,768]{2,1,0:T(8,128)(2,1)} %get-tuple-element.89) | copy-start | bytes 589828

commit v6 on v5

--- a/solution.py
+++ b/solution.py
@@ -692,6 +692,18 @@
 def pair_kernel(stacked, pair_w, grad_pair):
     for row in range(stacked.shape[1]):
         grad_pair[0, row] = dot(stacked[0, row], pair_w[...], TN).astype(bf16)
+
+
+def unpack_kernel(attn_own, ff_own, result, grad_inputs, w_in, w_out, ff_in, ff_out, result_out, inputs_out):
+    parts, _, block = w_in.shape
+    for part in range(parts):
+        w_in[part] = attn_own[0, :, part * block : (part + 1) * block]
+    w_out[...] = attn_own[0, :, parts * block : (parts + 1) * block]
+    for part in range(ff_in.shape[0]):
+        ff_in[part] = ff_own[part]
+    ff_out[...] = ff_own[ff_in.shape[0]]
+    result_out[...] = result[...]
+    inputs_out[...] = grad_inputs[...]
 
 
 def tail_kernel(
@@ -991,15 +1003,28 @@
     grad_cond = jnp.dot(mod_all, own_columns(ada_weight, 0).astype(f32).T, precision=highest)
     grad_table = jnp.dot(onehot_all.T, grad_cond, precision=highest)
     grad_pair_weight = jnp.sum(own_columns(pair_all, 2), axis=0)
-    own_in = attn_own[0, :, : 4 * block].reshape(-1, 4, block)
+    sum_in, sum_out, sum_ff_in, sum_ff_out, result, grad_inputs = pl.pallas_call(
+        unpack_kernel,
+        out_shape=(
+            sds((4, own_count, block), f32),
+            sds((own_count, block), f32),
+            sds((2, own_count, hidden_width), f32),
+            sds((own_count, hidden_width), f32),
+            sds(own, bf16),
+            sds(own, bf16),
+        ),
+        in_specs=[VMEM_SPEC] * 4,
+        out_specs=(VMEM_SPEC,) * 6,
+        name="unpack",
+    )(attn_own, ff_own, result, grad_inputs)
     return (
         result,
         grad_inputs,
         grad_pair,
-        jnp.swapaxes(own_in, 0, 1),
-        attn_own[0, :, 4 * block : 5 * block].T,
-        ff_own[:2],
-        ff_own[2].T,
+        sum_in,
+        sum_out.T,
+        sum_ff_in,
+        sum_ff_out.T,
         grad_ada,
         grad_table,
         grad_pair_weight,

time: 182 us -> 173 us (0.951)
  local copies, waits for them, and re-layouts: 12.5 us -> 3.1 us
  Pallas kernels: 156 us -> 159 us
    slice x2 -> x0, local copies, waits for them, and re-layouts: 2.9 us -> none  [the longest x1 1.92 us: local(): ff_own[:2]]
    pallas_call x0 -> x1, Pallas kernels: none -> 2.6 us  [local(): pl.pallas_call(unpack_kernel, out_shape=(sds((4, own_count, block), f32),...]
    transpose x2 -> x0, local copies, waits for them, and re-layouts: 2.6 us -> none  [the longest x1 1.7 us: local(): ff_own[2]]
where the time goes in v6:
time: 173 us
  Pallas kernels  159 us (92%)
  matrix products  6.83 us (4%)
  local copies, waits for them, and re-layouts  3.1 us (2%)
  other arithmetic  2.98 us (2%)
    pallas_call x1, Pallas kernels, local(): pl.pallas_call(functools.partial(attn_bwd_kernel, (n_tp, heads, width, ff...  55.3 us
    pallas_call x1, Pallas kernels, local(): pl.pallas_call(functools.partial(tail_kernel, (n_tp, n_dp, all_heads, att...  32.5 us
    pallas_call x1, Pallas kernels, local(): pl.pallas_call(functools.partial(attn_fwd_kernel, (n_tp, heads, width)),...  32.4 us
    pallas_call x1, Pallas kernels, local(): pl.pallas_call(functools.partial(ff_kernel, (n_tp, 256)), out_shape=(sds(...  25.9 us
    pallas_call x1, Pallas kernels, local(): pl.pallas_call(pair_kernel, out_shape=sds(pair_rep.shape, bf16), grid=(ch...  10.3 us

profile of v6, /device:TPU:0, one launch (start us, length us, event | category | flops | bytes accessed | tf_op | source)
XLA Modules:
  0.0 172.8 jit_solution(5298907666763040302)
XLA Ops:
  0.6 0.0 copy-start
  0.7 0.0 copy-start.7
  0.7 0.0 copy-start.6
  0.7 0.0 copy-start.1
  0.7 0.8 broadcast_multiply_fusion
  1.5 0.1 multiply_sine_fusion
  1.6 0.0 copy-done
  1.6 0.8 convolution_add_fusion
  2.4 2.7 %fusion.21 = f32[2,4608]{1,0:T(2,128)S(1)} fusion(f32[2,256]{1,0:T(2,128)S(1)} %convolution_add_fusion, bf16[256,4608]{1,0:T(8,128)(2,1)} %param.18), kind=kOutput, calls=%fused_computation.43 | convolution fusion | flops 28311552 | bytes 2398208 | tf_op jit(solution)/shard_map/dot_general | solution.py:812
  5.3 0.0 copy-done.7
  5.3 0.0 copy-start.2
  5.3 0.7 compare_convert_fusion.valid
  6.0 0.0 copy-done.6
  6.0 0.6 pad.8.pair_w
  6.6 0.0 copy-done.1
  6.6 1.4 copy.25.w_in
  8.0 0.0 copy-done.2
  8.0 32.4 %attn_fwd.1 = (bf16[2,256,768]{2,1,0:T(8,128)(2,1)}, bf16[2,256,768]{2,1,0:T(8,128)(2,1)}, f32[2,256,192]{2,1,0:T(8,128)}, f32[2,3,256,256]{3,2,1,0:T(8,128)}, f...) custom-call(bf16[2,64,768]{2,1,0:T(8,128)(2,1)} %inputs.3, ...), custom_call_target="tpu_custom_call" | custom-call | tf_op jit(solution)/shard_map/attn_fwd/pallas_call | solution.py:832
  40.5 25.9 %ff.1 = (bf16[2,64,768]{2,1,0:T(8,128)(2,1)}, f32[2,64,768]{2,1,0:T(8,128)}, bf16[2,64,768]{2,1,0:T(8,128)(2,1)}, f32[4,2,1,768]{3,2,1,0:T(1,128)}, bf16[3,768,768]{2,1,0:T(8,128)(2,1)}) custom-call(f32[2,64,768]{2,1,0:T(8,128)} %get-tuple-element.39.middle, bf16[2,64,768]{2,1,0:T(8,128)(2,1)} %cotangent.3, f32[2,64,768]{2,1,0:T(8,128)} %get-tuple-element.40.attended, ...), custom_call_target="tpu_custom_call" | custom-call | tf_op jit(solution)/shard_map/ff/pallas_call | solution.py:862
  66.3 0.0 copy-start.8
  66.3 55.3 %attn_bwd.1 = (bf16[2,64,768]{2,1,0:T(8,128)(2,1)}, f32[2,2,1,768]{3,2,1,0:T(1,128)}, bf16[1,768,1024]{2,1,0:T(8,128)(2,1)}, bf16[4,2,3,64,256]{4,3,2,1,0:T(8,12...) custom-call(bf16[2,64,768]{2,1,0:T(8,128)(2,1)} %inputs.3, ...), custom_call_target="tpu_custom_call" | custom-call | tf_op jit(solution)/shard_map/attn_bwd/pallas_call | solution.py:890
  121.7 0.1 fusion.17
  121.7 0.6 select_maximum_fusion.chain_facts
  122.3 32.5 %tail.1 = (bf16[8,16,768]{2,1,0:T(8,128)(2,1)}, f32[8,2,384]{2,1,0:T(2,128)}, f32[1,96,1024]{2,1,0:T(8,128)}) custom-call(f32[2,2,1,768]{3,2,1,0:T(1,128)} %get-tuple-element.51.attn_sums, f32[4,2,1,768]{3,2,1,0:T(1,128)} %get-tuple-element.52.ff_sums, f32[16,256]{1,0:T(8,128)} %get-tuple-element.53.pair_part, f32[6,2,1,768]{3,2,1,0:T(1,128)} %copy-done.2, ...), custom_call_target="tpu_custom_call" | custom-call | tf_op jit(solution)/shard_map/tail/pallas_call | solution.py:966
  154.9 2.6 %unpack.1 = (f32[4,96,192]{2,1,0:T(8,128)}, f32[96,192]{1,0:T(8,128)}, f32[2,96,768]{2,1,0:T(8,128)}, f32[96,768]{1,0:T(8,128)}, bf16[2,64,768]{2,1,0:T(8,128)(2,1)}, /*index=5*/bf16[2,64,768]{2,1,0:T(8,128)(2,1)}) custom-call(f32[1,96,1024]{2,1,0:T(8,128)} %get-tuple-element.55.attn_own, f32[3,96,768]{2,1,0:T(8,128)} %get-tuple-element.56.ff_own, ...), custom_call_target="tpu_custom_call" | custom-call | tf_op jit(solution)/shard_map/unpack/pallas_call | solution.py:1006
  157.5 10.3 %pair_grad.1 = bf16[2,64,256,256]{3,2,1,0:T(8,128)(2,1)} custom-call(bf16[2,64,16,256]{3,2,1,0:T(8,128)(2,1)} %get-tuple-element.61.stacked, bf16[16,256]{1,0:T(8,128)(2,1)} %pad.8.pair_w), custom_call_target="tpu_custom_call" | custom-call | tf_op jit(solution)/shard_map/pair_grad/pallas_call | solution.py:937
  167.8 0.7 copy.29
  168.7 1.3 fusion.2
  170.1 1.1 fusion
  171.2 0.8 fusion.5
  172.1 0.1 reshape.188
  172.1 0.7 dynamic-slice_reduce_fusion
  (20 shorter events, 0.3 us)
Async XLA Ops:
  0.6 0.9 copy-start
  0.7 4.6 %copy-start.7 = (s32[2]{0:T(128)S(1)}, s32[2]{0:T(128)}, u32[]{:S(2)}) copy-start(s32[2]{0:T(128)} %param.17) | copy-start | bytes 28
  0.7 5.3 %copy-start.6 = (bf16[12,256]{1,0:T(8,128)(2,1)S(1)}, bf16[12,256]{1,0:T(8,128)(2,1)}, u32[]{:S(2)}) copy-start(bf16[12,256]{1,0:T(8,128)(2,1)} %param.20) | copy-start | bytes 18436
  0.7 5.9 %copy-start.1 = (bf16[4,768,192]{1,2,0:T(8,128)(2,1)S(1)}, bf16[4,768,192]{1,2,0:T(8,128)(2,1)}, u32[]{:S(2)}) copy-start(bf16[4,768,192]{1,2,0:T(8,128)(2,1)} %param.21) | copy-start | bytes 3538948
  5.3 2.7 %copy-start.2 = (f32[6,2,1,768]{3,2,1,0:T(1,128)}, f32[6,2,1,768]{3,2,1,0:T(1,128)S(1)}, u32[]{:S(2)}) copy-start(f32[6,2,1,768]{3,2,1,0:T(1,128)S(1)} %constant_dynamic-update-slice_fusion.mods) | copy-start | bytes 110596
  66.3 55.3 %copy-start.8 = (s32[2]{0:T(128)S(1)}, s32[2]{0:T(128)}, u32[]{:S(2)}) copy-start(s32[2]{0:T(128)} %param.16) | copy-start | bytes 28
  157.5 10.4 %copy-start.4 = (f32[96,192]{1,0:T(8,128)S(1)}, f32[96,192]{1,0:T(8,128)}, u32[]{:S(2)}) copy-start(f32[96,192]{1,0:T(8,128)} %get-tuple-element.63) | copy-start | bytes 221188
  157.5 11.1 %copy-start.3 = (bf16[8,16,768]{2,1,0:T(8,128)(2,1)S(1)}, bf16[8,16,768]{2,1,0:T(8,128)(2,1)}, u32[]{:S(2)}) copy-start(bf16[8,16,768]{2,1,0:T(8,128)(2,1)} %get-tuple-element.67) | copy-start | bytes 589828
  157.5 11.2 %copy-start.5 = (f32[8,2,384]{2,1,0:T(2,128)S(1)}, f32[8,2,384]{2,1,0:T(2,128)}, u32[]{:S(2)}) copy-start(f32[8,2,384]{2,1,0:T(2,128)} %get-tuple-element.66) | copy-start | bytes 73732
